TPU v7x, 32 devices: a whole 2x2x4 slice. The times are simulated.
32 devices in a mesh: gx: 4 (over y, x), gy: 4 (over z), dev: 2 (over core).
Axes of the slice: x: 2, y: 2, z: 4, core: 2. Of those that a mesh axis runs over, the one named last changes fastest.
Arguments:
- fine_now: float32 [3, 8, 64, 1024], P(None, 'dev', 'gx', 'gy'), may hold values from -6 to 6
- fine_before: float32 [3, 8, 64, 1024], P(None, 'dev', 'gx', 'gy'), may hold values from -6 to 6
- fine_material: float32 [4, 8, 64, 1024], P(None, 'dev', 'gx', 'gy'), may hold values from 0.5 to 2
- coarse_now: float32 [3, 16, 32, 512], P(None, 'dev', 'gx', 'gy'), may hold values from -6 to 6
- coarse_before: float32 [3, 16, 32, 512], P(None, 'dev', 'gx', 'gy'), may hold values from -6 to 6
- coarse_material: float32 [3, 16, 32, 512], P(None, 'dev', 'gx', 'gy'), may hold values from 0.5 to 2
Outputs:
- fine_after: float32 [3, 8, 64, 1024], P(None, 'dev', 'gx', 'gy')
- coarse_after: float32 [3, 16, 32, 512], P(None, 'dev', 'gx', 'gy')
All inputs are finite; a program needn't handle non-finite values.
Results may differ from a plain program's by a relative error of at most 0.0001.
Values sent between devices are 32-bit elements; how exact they have to be, the bound alone decides.
No kernel may reach another device: no remote copies, remote signals or barrier semaphores. Data moves between devices by JAX's collectives and lax.ppermute only.
A program may use at most 64 MiB of HBM per device.

v0:
```python
import jax
import jax.numpy as jnp
from jax import lax
from jax.sharding import PartitionSpec as P

STEPS = 2


time_step = 0.15


def with_halo(cells, sides, width):
    for axis, dim in sides:
        count = lax.axis_size(axis)
        ends = count - 1
        head = lax.slice_in_dim(cells, 0, width, axis=dim)
        tail = lax.slice_in_dim(cells, cells.shape[dim] - width, cells.shape[dim], axis=dim)
        cells = jnp.concatenate(
            [
                lax.ppermute(tail, axis, [(i, (i + 1) % count) for i in range(ends)]),
                cells,
                lax.ppermute(head, axis, [((i + 1) % count, i) for i in range(ends)]),
            ],
            axis=dim,
        )
    return cells


def swapped(value, axis, stride):
    return lax.ppermute(value, axis, [(i, i ^ 1 << stride) for i in range(lax.axis_size(axis))])


def from_behind(value, axis, steps):
    count = lax.axis_size(axis)
    initial, last = (max(0, -steps), min(count, count - steps))
    return lax.ppermute(value, axis, [(source, source + steps) for source in range(initial, last)])


def restrict(plane):
    return plane.reshape(plane.shape[0], plane.shape[1] // 2, 2, plane.shape[2] // 2, 2).mean(
        axis=(2, 4)
    )


def prolong(plane):
    return jnp.repeat(jnp.repeat(plane, 2, axis=1), 2, axis=2)


def backward(field, direction):
    inner = field[1:, 1:, 1:]
    if direction == 0:
        return inner - field[:-1, 1:, 1:]
    if direction == 1:
        return inner - field[1:, :-1, 1:]
    return inner - field[1:, 1:, :-1]


def forces(padded, medium, spacing, stretched):
    centre = padded[:, :-1, :-1, :-1]
    medium_cells = medium[:, :, :-1, :-1]
    if stretched:
        vertical = medium_cells[3] / spacing
        outward = medium[3, 1:, 1:-1, 1:-1] / spacing
    else:
        vertical = 1.0 / spacing
        outward = 1.0 / spacing
    along_z = (padded[:, 1:, :-1, :-1] - centre) * vertical
    along_x = (padded[:, :-1, 1:, :-1] - centre) / spacing
    along_y = (padded[:, :-1, :-1, 1:] - centre) / spacing
    rigidity = medium_cells[1]
    lame_first = medium_cells[2]
    dilation = along_x[0] + along_y[1] + along_z[2]
    normal_x = lame_first * dilation + 2.0 * rigidity * along_x[0]
    normal_y = lame_first * dilation + 2.0 * rigidity * along_y[1]
    normal_z = lame_first * dilation + 2.0 * rigidity * along_z[2]
    shear_xy = rigidity * (along_y[0] + along_x[1])
    shear_xz = rigidity * (along_z[0] + along_x[2])
    shear_yz = rigidity * (along_z[1] + along_y[2])
    force_x = (backward(normal_x, 1) + backward(shear_xy, 2)) / spacing + backward(
        shear_xz, 0
    ) * outward
    force_y = (backward(shear_xy, 1) + backward(normal_y, 2)) / spacing + backward(
        shear_yz, 0
    ) * outward
    force_z = (backward(shear_xz, 1) + backward(shear_yz, 2)) / spacing + backward(
        normal_z, 0
    ) * outward
    return jnp.stack([force_x, force_y, force_z])


def advance(field, before, padded, medium, density, spacing, stretched):
    return (
        2.0 * field
        - before
        + time_step * time_step * forces(padded, medium, spacing, stretched) / density
    )


def layer_sides(field):
    return with_halo(field, (("gx", 2), ("gy", 3)), 1)


def depth_pads(fine_field, coarse_field, top_device):
    fine_edge = jnp.where(top_device, fine_field[:, -1], fine_field[:, 0])
    coarse_edge = jnp.where(top_device, coarse_field[:, -1], coarse_field[:, 0])
    interface = jnp.where(top_device, coarse_field[:, 0], restrict(fine_field[:, -1]))
    fine_count = fine_edge.size
    coarse_count = coarse_edge.size
    packed = jnp.concatenate(
        [fine_edge.reshape(-1), coarse_edge.reshape(-1), interface.reshape(-1)]
    )
    arrived = swapped(packed, "dev", 0)
    fine_got = arrived[:fine_count].reshape(fine_edge.shape)
    coarse_got = arrived[fine_count : fine_count + coarse_count].reshape(coarse_edge.shape)
    interface_got = arrived[fine_count + coarse_count :].reshape(coarse_edge.shape)
    fine_upper = jnp.where(top_device, jnp.zeros_like(fine_got), fine_got)
    fine_lower = jnp.where(top_device, fine_got, prolong(interface_got))
    coarse_upper = jnp.where(top_device, interface_got, coarse_got)
    coarse_lower = jnp.where(top_device, coarse_got, jnp.zeros_like(coarse_got))
    fine_padded = jnp.concatenate([fine_upper[:, None], fine_field, fine_lower[:, None]], axis=1)
    coarse_padded = jnp.concatenate(
        [coarse_upper[:, None], coarse_field, coarse_lower[:, None]], axis=1
    )
    return (fine_padded, coarse_padded)


def per_device(fine_now, fine_before, fine_material, coarse_now, coarse_before, coarse_material):
    top_device = lax.axis_index("dev") == 0
    fine_count = fine_material[:, -1].size
    packed = jnp.concatenate([fine_material[:, -1].reshape(-1), coarse_material[:, -1].reshape(-1)])
    arrived = from_behind(packed, "dev", 1)
    fine_top = arrived[:fine_count].reshape(fine_material[:, :1].shape)
    coarse_top = jnp.where(
        top_device,
        coarse_material[:, :1],
        arrived[fine_count:].reshape(coarse_material[:, :1].shape),
    )
    fine_medium = layer_sides(jnp.concatenate([fine_top, fine_material], axis=1))
    coarse_medium = layer_sides(jnp.concatenate([coarse_top, coarse_material], axis=1))
    fine_field, fine_prior = (fine_now, fine_before)
    coarse_field, coarse_prior = (coarse_now, coarse_before)
    for instant in range(STEPS):
        fine_deep, coarse_deep = depth_pads(fine_field, coarse_field, top_device)
        fine_padded = layer_sides(fine_deep)
        coarse_padded = layer_sides(coarse_deep)
        fine_next = advance(
            fine_field, fine_prior, fine_padded, fine_medium, fine_material[0], 1.0, True
        )
        coarse_next = advance(
            coarse_field, coarse_prior, coarse_padded, coarse_medium, coarse_material[0], 2.0, False
        )
        fine_prior, fine_field = (fine_field, fine_next)
        coarse_prior, coarse_field = (coarse_field, coarse_next)
    return (fine_field, coarse_field)


def solution(mesh):
    return jax.shard_map(
        per_device,
        mesh=mesh,
        in_specs=(
            P(None, "dev", "gx", "gy"),
            P(None, "dev", "gx", "gy"),
            P(None, "dev", "gx", "gy"),
            P(None, "dev", "gx", "gy"),
            P(None, "dev", "gx", "gy"),
            P(None, "dev", "gx", "gy"),
        ),
        out_specs=(P(None, "dev", "gx", "gy"), P(None, "dev", "gx", "gy")),
        check_vma=False,
    )
```

profile of v0, /device:TPU:0, one launch (start us, length us, event | category | flops | bytes accessed | tf_op | source)
XLA Modules:
  0.0 125.2 jit_solution(4592496217749878757)
XLA Ops:
  0.6 0.9 slice_bitcast_fusion.15
  1.5 3.2 %reshape_squeeze.14 = f32[3,8,2,128,2]{4,3,2,1,0:T(8,128)S(1)} reshape(f32[3,1,16,256]{3,2,0,1:T(8,128)S(1)} %slice_bitcast_fusion.15) | data formatting | bytes 98304 | tf_op jit(solution)/shard_map/reshape;squeeze | solution.py:40
  4.7 1.1 reduce_sum.18
  5.8 0.8 bitcast_select_fusion.3
  6.6 0.6 collective-permute-start.4
  7.2 0.7 slice_bitcast_fusion.24
  7.9 1.9 %collective-permute-start = (f32[19456]{0:T(1024)S(1)}, f32[19456]{0:T(1024)S(1)}, u32[]{:S(2)}, u32[]{:S(2)}) collective-permute-start(f32[19456]{0:T(1024)S(1)} %pad_maximum_fusion.39), channel_id=1, source_target_pairs={{0,1},{2,3},{4,5},{6,7},{8,9},{10,11},{12,13},{14,15},{16,17},{18,... | collective-permute-start | bytes 233480 | tf_op jit(solution)/shard_map/ppermute | solution.py:36
  9.9 0.8 slice_bitcast_fusion.14
  10.7 0.8 slice_bitcast_fusion.16
  12.0 4.9 %collective-permute-start.5 = (f32[3,6,1,256]{3,2,1,0:T(1,128)S(1)}, f32[3,6,1,256]{3,2,1,0:T(1,128)S(1)}, u32[]{:S(2)}, u32[]{:S(2)}) collective-permute-start(f32[3,6,1,256]{3,2,1,0:T(1,128)S(1)} %get-tuple-element.55), channel_id=1, source_target_pairs={{0,8},{8,16},{16,24},{1,9},{9,17},{17,25},{2,10},{10,18},{18,26},{... | collective-permute-start | bytes 55304 | tf_op jit(solution)/shard_map/ppermute | solution.py:20
  16.9 1.3 %collective-permute-start.6 = (f32[3,6,1,256]{3,2,1,0:T(1,128)S(1)}, f32[3,6,1,256]{3,2,1,0:T(1,128)S(1)}, u32[]{:S(2)}, u32[]{:S(2)}) collective-permute-start(f32[3,6,1,256]{3,2,1,0:T(1,128)S(1)} %get-tuple-element.56), channel_id=1, source_target_pairs={{8,0},{16,8},{24,16},{9,1},{17,9},{25,17},{10,2},{18,10},{26,18},{... | collective-permute-start | bytes 55304 | tf_op jit(solution)/shard_map/ppermute | solution.py:22
  18.2 4.5 %collective-permute-start.12 = (f32[3,10,1,128]{3,2,1,0:T(1,128)S(1)}, f32[3,10,1,128]{3,2,1,0:T(1,128)S(1)}, u32[]{:S(2)}, u32[]{:S(2)}) collective-permute-start(f32[3,10,1,128]{3,2,1,0:T(1,128)S(1)} %get-tuple-element.71), channel_id=1, source_target_pairs={{0,8},{8,16},{16,24},{1,9},{9,17},{17,25},{2,10},{10,18},{18,26},{... | collective-permute-start | bytes 46088 | tf_op jit(solution)/shard_map/ppermute | solution.py:20
  22.8 1.3 %collective-permute-start.13 = (f32[3,10,1,128]{3,2,1,0:T(1,128)S(1)}, f32[3,10,1,128]{3,2,1,0:T(1,128)S(1)}, u32[]{:S(2)}, u32[]{:S(2)}) collective-permute-start(f32[3,10,1,128]{3,2,1,0:T(1,128)S(1)} %get-tuple-element.72), channel_id=1, source_target_pairs={{8,0},{16,8},{24,16},{9,1},{17,9},{25,17},{10,2},{18,10},{26,18},{... | collective-permute-start | bytes 46088 | tf_op jit(solution)/shard_map/ppermute | solution.py:22
  24.2 4.9 %collective-permute-start.1 = (f32[4,5,1,256]{3,2,1,0:T(1,128)S(1)}, f32[4,5,1,256]{3,2,1,0:T(1,128)S(1)}, u32[]{:S(2)}, u32[]{:S(2)}) collective-permute-start(f32[4,5,1,256]{3,2,1,0:T(1,128)S(1)} %get-tuple-element.47), channel_id=1, source_target_pairs={{0,8},{8,16},{16,24},{1,9},{9,17},{17,25},{2,10},{10,18},{18,26},{... | collective-permute-start | bytes 61448 | tf_op jit(solution)/shard_map/ppermute | solution.py:20
  29.3 3.5 %collective-permute-start.14 = (f32[3,10,10,1]{3,2,1,0:T(8,128)S(1)}, f32[3,10,10,1]{3,2,1,0:T(8,128)S(1)}, u32[]{:S(2)}, u32[]{:S(2)}) collective-permute-start(f32[3,10,10,1]{3,2,1,0:T(8,128)S(1)} %get-tuple-element.60), channel_id=1, source_target_pairs={{0,2},{2,4},{4,6},{1,3},{3,5},{5,7},{8,10},{10,12},{12,14},{9,11},... | collective-permute-start | bytes 3608 | tf_op jit(solution)/shard_map/ppermute | solution.py:20
  32.9 1.3 %collective-permute-start.10 = (f32[3,9,1,128]{3,2,1,0:T(1,128)S(1)}, f32[3,9,1,128]{3,2,1,0:T(1,128)S(1)}, u32[]{:S(2)}, u32[]{:S(2)}) collective-permute-start(f32[3,9,1,128]{3,2,1,0:T(1,128)S(1)} %get-tuple-element.74), channel_id=1, source_target_pairs={{8,0},{16,8},{24,16},{9,1},{17,9},{25,17},{10,2},{18,10},{26,18},{... | collective-permute-start | bytes 41480 | tf_op jit(solution)/shard_map/ppermute | solution.py:22
  34.2 2.4 %collective-permute-done.14 = f32[3,10,10,1]{3,2,1,0:T(8,128)S(1)} collective-permute-done((f32[3,10,10,1]{3,2,1,0:T(8,128)S(1)}, f32[3,10,10,1]{3,2,1,0:T(8,128)S(1)}, u32[]{:S(2)}, u32[]{:S(2)}) %collective-permute-start.14) | collective-permute-done | bytes 1232 | tf_op jit(solution)/shard_map/ppermute | solution.py:20
  36.5 1.3 %collective-permute-start.15 = (f32[3,10,10,1]{3,2,1,0:T(8,128)S(1)}, f32[3,10,10,1]{3,2,1,0:T(8,128)S(1)}, u32[]{:S(2)}, u32[]{:S(2)}) collective-permute-start(f32[3,10,10,1]{3,2,1,0:T(8,128)S(1)} %get-tuple-element.59), channel_id=1, source_target_pairs={{2,0},{4,2},{6,4},{3,1},{5,3},{7,5},{10,8},{12,10},{14,12},{11,9},... | collective-permute-start | bytes 3608 | tf_op jit(solution)/shard_map/ppermute | solution.py:22
  37.8 0.3 maximum_maximum_fusion.1
  38.1 6.9 %collective-permute-done.15 = f32[3,10,10,1]{3,2,1,0:T(8,128)S(1)} collective-permute-done((f32[3,10,10,1]{3,2,1,0:T(8,128)S(1)}, f32[3,10,10,1]{3,2,1,0:T(8,128)S(1)}, u32[]{:S(2)}, u32[]{:S(2)}) %collective-permute-start.15) | collective-permute-done | bytes 1232 | tf_op jit(solution)/shard_map/ppermute | solution.py:22
  45.1 4.8 %collective-permute-start.9 = (f32[3,9,1,128]{3,2,1,0:T(1,128)S(1)}, f32[3,9,1,128]{3,2,1,0:T(1,128)S(1)}, u32[]{:S(2)}, u32[]{:S(2)}) collective-permute-start(f32[3,9,1,128]{3,2,1,0:T(1,128)S(1)} %get-tuple-element.73), channel_id=1, source_target_pairs={{0,8},{8,16},{16,24},{1,9},{9,17},{17,25},{2,10},{10,18},{18,26},{... | collective-permute-start | bytes 41480 | tf_op jit(solution)/shard_map/ppermute | solution.py:20
  49.9 0.2 fusion.14
  50.1 1.4 %collective-permute-start.2 = (f32[4,5,1,256]{3,2,1,0:T(1,128)S(1)}, f32[4,5,1,256]{3,2,1,0:T(1,128)S(1)}, u32[]{:S(2)}, u32[]{:S(2)}) collective-permute-start(f32[4,5,1,256]{3,2,1,0:T(1,128)S(1)} %get-tuple-element.48), channel_id=1, source_target_pairs={{8,0},{16,8},{24,16},{9,1},{17,9},{25,17},{10,2},{18,10},{26,18},{... | collective-permute-start | bytes 61448 | tf_op jit(solution)/shard_map/ppermute | solution.py:22
  51.6 0.2 pad_maximum_fusion.28
  51.8 3.9 %collective-permute-start.11 = (f32[3,9,10,1]{3,2,1,0:T(8,128)S(1)}, f32[3,9,10,1]{3,2,1,0:T(8,128)S(1)}, u32[]{:S(2)}, u32[]{:S(2)}) collective-permute-start(f32[3,9,10,1]{3,2,1,0:T(8,128)S(1)} %pad_maximum_fusion.28), channel_id=1, source_target_pairs={{0,2},{2,4},{4,6},{1,3},{3,5},{5,7},{8,10},{10,12},{12,14},{9,11},... | collective-permute-start | bytes 3248 | tf_op jit(solution)/shard_map/ppermute | solution.py:20
  55.9 3.5 %collective-permute-start.7 = (f32[3,6,18,1]{3,2,1,0:T(8,128)S(1)}, f32[3,6,18,1]{3,2,1,0:T(8,128)S(1)}, u32[]{:S(2)}, u32[]{:S(2)}) collective-permute-start(f32[3,6,18,1]{3,2,1,0:T(8,128)S(1)} %get-tuple-element.42), channel_id=1, source_target_pairs={{0,2},{2,4},{4,6},{1,3},{3,5},{5,7},{8,10},{10,12},{12,14},{9,11},... | collective-permute-start | bytes 3896 | tf_op jit(solution)/shard_map/ppermute | solution.py:20
  59.4 1.3 %collective-permute-start.8 = (f32[3,6,18,1]{3,2,1,0:T(8,128)S(1)}, f32[3,6,18,1]{3,2,1,0:T(8,128)S(1)}, u32[]{:S(2)}, u32[]{:S(2)}) collective-permute-start(f32[3,6,18,1]{3,2,1,0:T(8,128)S(1)} %get-tuple-element.41), channel_id=1, source_target_pairs={{2,0},{4,2},{6,4},{3,1},{5,3},{7,5},{10,8},{12,10},{14,12},{11,9},... | collective-permute-start | bytes 3896 | tf_op jit(solution)/shard_map/ppermute | solution.py:22
  60.8 0.2 fusion.50
  61.1 0.5 copy-done.5
  61.7 0.2 fusion.106
  61.9 0.7 fusion.57
  62.8 4.6 %collective-permute-start.3 = (f32[4,5,18,1]{3,2,1,0:T(8,128)S(1)}, f32[4,5,18,1]{3,2,1,0:T(8,128)S(1)}, u32[]{:S(2)}, u32[]{:S(2)}) collective-permute-start(f32[4,5,18,1]{3,2,1,0:T(8,128)S(1)} %pad_maximum_fusion.23), channel_id=1, source_target_pairs={{0,2},{2,4},{4,6},{1,3},{3,5},{5,7},{8,10},{10,12},{12,14},{9,11},... | collective-permute-start | bytes 4328 | tf_op jit(solution)/shard_map/ppermute | solution.py:20
  67.4 0.4 maximum_maximum_fusion
  67.8 3.3 %collective-permute-done.3 = f32[4,5,18,1]{3,2,1,0:T(8,128)S(1)} collective-permute-done((f32[4,5,18,1]{3,2,1,0:T(8,128)S(1)}, f32[4,5,18,1]{3,2,1,0:T(8,128)S(1)}, u32[]{:S(2)}, u32[]{:S(2)}) %collective-permute-start.3) | collective-permute-done | bytes 1472 | tf_op jit(solution)/shard_map/ppermute | solution.py:20
  71.4 0.9 fusion.32
  72.7 0.2 fusion.82
  73.0 0.6 slice_select_fusion
  73.6 3.9 %reshape_squeeze.15 = f32[3,8,2,128,2]{4,3,2,1,0:T(8,128)S(1)} reshape(f32[3,1,16,256]{3,2,0,1:T(8,128)} %get-tuple-element.62) | data formatting | bytes 98304 | tf_op jit(solution)/shard_map/reshape;squeeze | solution.py:40
  77.5 0.5 reduce_sum.19
  78.0 0.9 copy.69
  78.9 0.7 fusion.108
  79.7 1.3 %collective-permute-done.16 = f32[18432]{0:T(1024)S(1)} collective-permute-done((f32[18432]{0:T(1024)S(1)}, f32[18432]{0:T(1024)S(1)}, u32[]{:S(2)}, u32[]{:S(2)}) %collective-permute-start.16) | collective-permute-done | bytes 73760 | tf_op jit(solution)/shard_map/ppermute | solution.py:30
  81.0 1.0 pad_maximum_fusion.52
  82.0 4.5 %collective-permute-start.21 = (f32[3,10,1,128]{3,2,1,0:T(1,128)S(1)}, f32[3,10,1,128]{3,2,1,0:T(1,128)S(1)}, u32[]{:S(2)}, u32[]{:S(2)}) collective-permute-start(f32[3,10,1,128]{3,2,1,0:T(1,128)S(1)} %get-tuple-element.69), channel_id=1, source_target_pairs={{0,8},{8,16},{16,24},{1,9},{9,17},{17,25},{2,10},{10,18},{18,26},{... | collective-permute-start | bytes 46088 | tf_op jit(solution)/shard_map/ppermute | solution.py:20
  86.5 1.3 %collective-permute-start.22 = (f32[3,10,1,128]{3,2,1,0:T(1,128)S(1)}, f32[3,10,1,128]{3,2,1,0:T(1,128)S(1)}, u32[]{:S(2)}, u32[]{:S(2)}) collective-permute-start(f32[3,10,1,128]{3,2,1,0:T(1,128)S(1)} %get-tuple-element.70), channel_id=1, source_target_pairs={{8,0},{16,8},{24,16},{9,1},{17,9},{25,17},{10,2},{18,10},{26,18},{... | collective-permute-start | bytes 46088 | tf_op jit(solution)/shard_map/ppermute | solution.py:22
  88.3 3.8 %collective-permute-done.22 = f32[3,10,1,128]{3,2,1,0:T(1,128)S(1)} collective-permute-done((f32[3,10,1,128]{3,2,1,0:T(1,128)S(1)}, f32[3,10,1,128]{3,2,1,0:T(1,128)S(1)}, u32[]{:S(2)}, u32[]{:S(2)}) %collective-permute-start.22) | collective-permute-done | bytes 15392 | tf_op jit(solution)/shard_map/ppermute | solution.py:22
  92.1 0.9 pad_maximum_fusion.27
  93.3 4.5 %collective-permute-start.23 = (f32[3,10,10,1]{3,2,1,0:T(8,128)S(1)}, f32[3,10,10,1]{3,2,1,0:T(8,128)S(1)}, u32[]{:S(2)}, u32[]{:S(2)}) collective-permute-start(f32[3,10,10,1]{3,2,1,0:T(8,128)S(1)} %get-tuple-element.58), channel_id=1, source_target_pairs={{0,2},{2,4},{4,6},{1,3},{3,5},{5,7},{8,10},{10,12},{12,14},{9,11},... | collective-permute-start | bytes 3608 | tf_op jit(solution)/shard_map/ppermute | solution.py:20
  97.8 4.0 %collective-permute-start.17 = (f32[3,6,1,256]{3,2,0,1:T(1,128)S(1)}, f32[3,6,1,256]{3,2,0,1:T(1,128)S(1)}, u32[]{:S(2)}, u32[]{:S(2)}) collective-permute-start(f32[3,6,1,256]{3,2,0,1:T(1,128)S(1)} %get-tuple-element.51), channel_id=1, source_target_pairs={{0,8},{8,16},{16,24},{1,9},{9,17},{17,25},{2,10},{10,18},{18,26},{... | collective-permute-start | bytes 55304 | tf_op jit(solution)/shard_map/ppermute | solution.py:20
  101.8 1.3 %collective-permute-start.18 = (f32[3,6,1,256]{3,2,0,1:T(1,128)S(1)}, f32[3,6,1,256]{3,2,0,1:T(1,128)S(1)}, u32[]{:S(2)}, u32[]{:S(2)}) collective-permute-start(f32[3,6,1,256]{3,2,0,1:T(1,128)S(1)} %get-tuple-element.52), channel_id=1, source_target_pairs={{8,0},{16,8},{24,16},{9,1},{17,9},{25,17},{10,2},{18,10},{26,18},{... | collective-permute-start | bytes 55304 | tf_op jit(solution)/shard_map/ppermute | solution.py:22
  103.1 1.3 %collective-permute-start.24 = (f32[3,10,10,1]{3,2,1,0:T(8,128)S(1)}, f32[3,10,10,1]{3,2,1,0:T(8,128)S(1)}, u32[]{:S(2)}, u32[]{:S(2)}) collective-permute-start(f32[3,10,10,1]{3,2,1,0:T(8,128)S(1)} %get-tuple-element.57), channel_id=1, source_target_pairs={{2,0},{4,2},{6,4},{3,1},{5,3},{7,5},{10,8},{12,10},{14,12},{11,9},... | collective-permute-start | bytes 3608 | tf_op jit(solution)/shard_map/ppermute | solution.py:22
  104.5 0.3 maximum_maximum_fusion.2
  104.8 6.4 %collective-permute-done.24 = f32[3,10,10,1]{3,2,1,0:T(8,128)S(1)} collective-permute-done((f32[3,10,10,1]{3,2,1,0:T(8,128)S(1)}, f32[3,10,10,1]{3,2,1,0:T(8,128)S(1)}, u32[]{:S(2)}, u32[]{:S(2)}) %collective-permute-start.24) | collective-permute-done | bytes 1232 | tf_op jit(solution)/shard_map/ppermute | solution.py:22
  111.2 0.2 fusion.10
  112.3 2.0 %collective-permute-start.19 = (f32[3,6,18,1]{3,2,1,0:T(8,128)S(1)}, f32[3,6,18,1]{3,2,1,0:T(8,128)S(1)}, u32[]{:S(2)}, u32[]{:S(2)}) collective-permute-start(f32[3,6,18,1]{3,2,1,0:T(8,128)S(1)} %copy.82), channel_id=1, source_target_pairs={{0,2},{2,4},{4,6},{1,3},{3,5},{5,7},{8,10},{10,12},{12,14},{9,11},... | collective-permute-start | bytes 3896 | tf_op jit(solution)/shard_map/ppermute | solution.py:20
  114.3 0.7 fusion.59
  115.0 1.4 %collective-permute-start.20 = (f32[3,6,18,1]{3,2,0,1:T(8,128)S(1)}, f32[3,6,18,1]{3,2,0,1:T(8,128)S(1)}, u32[]{:S(2)}, u32[]{:S(2)}) collective-permute-start(f32[3,6,18,1]{3,2,0,1:T(8,128)S(1)} %slice.839), channel_id=1, source_target_pairs={{2,0},{4,2},{6,4},{3,1},{5,3},{7,5},{10,8},{12,10},{14,12},{11,9},... | collective-permute-start | bytes 3896 | tf_op jit(solution)/shard_map/ppermute | solution.py:22
  116.5 1.3 %collective-permute-done.19 = f32[3,6,18,1]{3,2,1,0:T(8,128)S(1)} collective-permute-done((f32[3,6,18,1]{3,2,1,0:T(8,128)S(1)}, f32[3,6,18,1]{3,2,1,0:T(8,128)S(1)}, u32[]{:S(2)}, u32[]{:S(2)}) %collective-permute-start.19) | collective-permute-done | bytes 1328 | tf_op jit(solution)/shard_map/ppermute | solution.py:20
  117.7 0.4 fusion.4
  118.1 4.9 %collective-permute-done.20 = f32[3,6,18,1]{3,2,0,1:T(8,128)S(1)} collective-permute-done((f32[3,6,18,1]{3,2,0,1:T(8,128)S(1)}, f32[3,6,18,1]{3,2,0,1:T(8,128)S(1)}, u32[]{:S(2)}, u32[]{:S(2)}) %collective-permute-start.20) | collective-permute-done | bytes 1328 | tf_op jit(solution)/shard_map/ppermute | solution.py:22
  123.2 0.3 fusion.2
  123.7 0.4 copy-done.4
  124.2 0.2 fusion.70
  124.5 0.7 fusion.18
  (136 shorter events, 4.1 us)
Async XLA Ops:
  0.6 4.1 %copy-start = (f32[3,4,16,256]{3,2,1,0:T(8,128)S(1)}, f32[3,4,16,256]{3,2,1,0:T(8,128)}, u32[]{:S(2)}) copy-start(f32[3,4,16,256]{3,2,1,0:T(8,128)} %param.6) | copy-start | bytes 589828
  1.5 4.3 %copy-start.7 = (f32[3,8,8,128]{3,2,1,0:T(8,128)S(1)}, f32[3,8,8,128]{3,2,1,0:T(8,128)}, u32[]{:S(2)}) copy-start(f32[3,8,8,128]{3,2,1,0:T(8,128)} %param.9) | copy-start | bytes 294916
  1.5 5.7 %slice-start = ((f32[4,4,16,256]{3,2,1,0:T(8,128)}), f32[4,1,16,256]{3,2,1,0:T(8,128)S(1)}, s32[]{:S(2)}) async-start(f32[4,4,16,256]{3,2,1,0:T(8,128)} %param.8), calls=%async_computation | async-start | bytes 131072 | tf_op jit(solution)/shard_map/slice | solution.py:130
  5.8 18.3 %copy-start.3 = (f32[4,4,16,256]{3,2,1,0:T(8,128)S(1)}, f32[4,4,16,256]{3,2,1,0:T(8,128)}, u32[]{:S(2)}) copy-start(f32[4,4,16,256]{3,2,1,0:T(8,128)} %param.8) | copy-start | bytes 786436
  5.8 23.3 %copy-start.10 = (f32[3,8,8,128]{3,2,1,0:T(8,128)S(1)}, f32[3,8,8,128]{3,2,1,0:T(8,128)}, u32[]{:S(2)}) copy-start(f32[3,8,8,128]{3,2,1,0:T(8,128)} %param.11) | copy-start | bytes 294916
  6.6 4.9 %collective-permute-start.4 = (f32[18432]{0:T(1024)S(1)}, f32[18432]{0:T(1024)S(1)}, u32[]{:S(2)}, u32[]{:S(2)}) collective-permute-start(f32[18432]{0:T(1024)S(1)} %pad_maximum_fusion.40), channel_id=1, source_target_pairs={{0,1},{1,0},{2,3},{3,2},{4,5},{5,4},{6,7},{7,6},{8,9},{9,8},{10,11... | collective-permute-start | bytes 221192 | tf_op jit(solution)/shard_map/ppermute | solution.py:30
  7.9 16.1 %collective-permute-start = (f32[19456]{0:T(1024)S(1)}, f32[19456]{0:T(1024)S(1)}, u32[]{:S(2)}, u32[]{:S(2)}) collective-permute-start(f32[19456]{0:T(1024)S(1)} %pad_maximum_fusion.39), channel_id=1, source_target_pairs={{0,1},{2,3},{4,5},{6,7},{8,9},{10,11},{12,13},{14,15},{16,17},{18,... | collective-permute-start | bytes 233480 | tf_op jit(solution)/shard_map/ppermute | solution.py:36
  10.7 62.2 %copy-start.17 = (f32[4,16,256]{2,1,0:T(8,128)}, f32[4,16,256]{2,1,0:T(8,128)S(1)}, u32[]{:S(2)}) copy-start(f32[4,16,256]{2,1,0:T(8,128)S(1)} %slice_bitcast_fusion.14) | copy-start | bytes 196612
  11.5 50.4 %copy-start.19 = (f32[8,8,128]{2,1,0:T(8,128)}, f32[8,8,128]{2,1,0:T(8,128)S(1)}, u32[]{:S(2)}) copy-start(f32[8,8,128]{2,1,0:T(8,128)S(1)} %slice_bitcast_fusion.16) | copy-start | bytes 98308
  12.0 43.7 %collective-permute-start.5 = (f32[3,6,1,256]{3,2,1,0:T(1,128)S(1)}, f32[3,6,1,256]{3,2,1,0:T(1,128)S(1)}, u32[]{:S(2)}, u32[]{:S(2)}) collective-permute-start(f32[3,6,1,256]{3,2,1,0:T(1,128)S(1)} %get-tuple-element.55), channel_id=1, source_target_pairs={{0,8},{8,16},{16,24},{1,9},{9,17},{17,25},{2,10},{10,18},{18,26},{... | collective-permute-start | bytes 55304 | tf_op jit(solution)/shard_map/ppermute | solution.py:20
  16.9 38.9 %collective-permute-start.6 = (f32[3,6,1,256]{3,2,1,0:T(1,128)S(1)}, f32[3,6,1,256]{3,2,1,0:T(1,128)S(1)}, u32[]{:S(2)}, u32[]{:S(2)}) collective-permute-start(f32[3,6,1,256]{3,2,1,0:T(1,128)S(1)} %get-tuple-element.56), channel_id=1, source_target_pairs={{8,0},{16,8},{24,16},{9,1},{17,9},{25,17},{10,2},{18,10},{26,18},{... | collective-permute-start | bytes 55304 | tf_op jit(solution)/shard_map/ppermute | solution.py:22
  18.2 10.9 %collective-permute-start.12 = (f32[3,10,1,128]{3,2,1,0:T(1,128)S(1)}, f32[3,10,1,128]{3,2,1,0:T(1,128)S(1)}, u32[]{:S(2)}, u32[]{:S(2)}) collective-permute-start(f32[3,10,1,128]{3,2,1,0:T(1,128)S(1)} %get-tuple-element.71), channel_id=1, source_target_pairs={{0,8},{8,16},{16,24},{1,9},{9,17},{17,25},{2,10},{10,18},{18,26},{... | collective-permute-start | bytes 46088 | tf_op jit(solution)/shard_map/ppermute | solution.py:20
  22.8 6.4 %collective-permute-start.13 = (f32[3,10,1,128]{3,2,1,0:T(1,128)S(1)}, f32[3,10,1,128]{3,2,1,0:T(1,128)S(1)}, u32[]{:S(2)}, u32[]{:S(2)}) collective-permute-start(f32[3,10,1,128]{3,2,1,0:T(1,128)S(1)} %get-tuple-element.72), channel_id=1, source_target_pairs={{8,0},{16,8},{24,16},{9,1},{17,9},{25,17},{10,2},{18,10},{26,18},{... | collective-permute-start | bytes 46088 | tf_op jit(solution)/shard_map/ppermute | solution.py:22
  24.2 38.4 %collective-permute-start.1 = (f32[4,5,1,256]{3,2,1,0:T(1,128)S(1)}, f32[4,5,1,256]{3,2,1,0:T(1,128)S(1)}, u32[]{:S(2)}, u32[]{:S(2)}) collective-permute-start(f32[4,5,1,256]{3,2,1,0:T(1,128)S(1)} %get-tuple-element.47), channel_id=1, source_target_pairs={{0,8},{8,16},{16,24},{1,9},{9,17},{17,25},{2,10},{10,18},{18,26},{... | collective-permute-start | bytes 61448 | tf_op jit(solution)/shard_map/ppermute | solution.py:20
  29.3 7.2 %collective-permute-start.14 = (f32[3,10,10,1]{3,2,1,0:T(8,128)S(1)}, f32[3,10,10,1]{3,2,1,0:T(8,128)S(1)}, u32[]{:S(2)}, u32[]{:S(2)}) collective-permute-start(f32[3,10,10,1]{3,2,1,0:T(8,128)S(1)} %get-tuple-element.60), channel_id=1, source_target_pairs={{0,2},{2,4},{4,6},{1,3},{3,5},{5,7},{8,10},{10,12},{12,14},{9,11},... | collective-permute-start | bytes 3608 | tf_op jit(solution)/shard_map/ppermute | solution.py:20
  32.9 17.2 %collective-permute-start.10 = (f32[3,9,1,128]{3,2,1,0:T(1,128)S(1)}, f32[3,9,1,128]{3,2,1,0:T(1,128)S(1)}, u32[]{:S(2)}, u32[]{:S(2)}) collective-permute-start(f32[3,9,1,128]{3,2,1,0:T(1,128)S(1)} %get-tuple-element.74), channel_id=1, source_target_pairs={{8,0},{16,8},{24,16},{9,1},{17,9},{25,17},{10,2},{18,10},{26,18},{... | collective-permute-start | bytes 41480 | tf_op jit(solution)/shard_map/ppermute | solution.py:22
  36.5 8.5 %collective-permute-start.15 = (f32[3,10,10,1]{3,2,1,0:T(8,128)S(1)}, f32[3,10,10,1]{3,2,1,0:T(8,128)S(1)}, u32[]{:S(2)}, u32[]{:S(2)}) collective-permute-start(f32[3,10,10,1]{3,2,1,0:T(8,128)S(1)} %get-tuple-element.59), channel_id=1, source_target_pairs={{2,0},{4,2},{6,4},{3,1},{5,3},{7,5},{10,8},{12,10},{14,12},{11,9},... | collective-permute-start | bytes 3608 | tf_op jit(solution)/shard_map/ppermute | solution.py:22
  45.1 6.5 %collective-permute-start.9 = (f32[3,9,1,128]{3,2,1,0:T(1,128)S(1)}, f32[3,9,1,128]{3,2,1,0:T(1,128)S(1)}, u32[]{:S(2)}, u32[]{:S(2)}) collective-permute-start(f32[3,9,1,128]{3,2,1,0:T(1,128)S(1)} %get-tuple-element.73), channel_id=1, source_target_pairs={{0,8},{8,16},{16,24},{1,9},{9,17},{17,25},{2,10},{10,18},{18,26},{... | collective-permute-start | bytes 41480 | tf_op jit(solution)/shard_map/ppermute | solution.py:20
  50.1 11.8 %copy-start.28 = (f32[3,8,8,128]{3,2,1,0:T(8,128)S(1)}, f32[3,8,8,128]{3,2,1,0:T(8,128)}, u32[]{:S(2)}) copy-start(f32[3,8,8,128]{3,2,1,0:T(8,128)} %param.10) | copy-start | bytes 294916
  50.1 12.5 %copy-start.24 = (f32[3,9,1,128]{3,2,1,0:T(1,128)}, f32[3,9,1,128]{3,2,1,0:T(1,128)S(1)}, u32[]{:S(2)}) copy-start(f32[3,9,1,128]{3,2,1,0:T(1,128)S(1)} %collective-permute-done.10) | copy-start | bytes 41476
  50.1 12.5 %collective-permute-start.2 = (f32[4,5,1,256]{3,2,1,0:T(1,128)S(1)}, f32[4,5,1,256]{3,2,1,0:T(1,128)S(1)}, u32[]{:S(2)}, u32[]{:S(2)}) collective-permute-start(f32[4,5,1,256]{3,2,1,0:T(1,128)S(1)} %get-tuple-element.48), channel_id=1, source_target_pairs={{8,0},{16,8},{24,16},{9,1},{17,9},{25,17},{10,2},{18,10},{26,18},{... | collective-permute-start | bytes 61448 | tf_op jit(solution)/shard_map/ppermute | solution.py:22
  51.6 11.0 %copy-start.26 = (f32[3,9,1,128]{3,2,1,0:T(1,128)}, f32[3,9,1,128]{3,2,1,0:T(1,128)S(1)}, u32[]{:S(2)}) copy-start(f32[3,9,1,128]{3,2,1,0:T(1,128)S(1)} %collective-permute-done.9) | copy-start | bytes 41476
  51.8 9.0 %collective-permute-start.11 = (f32[3,9,10,1]{3,2,1,0:T(8,128)S(1)}, f32[3,9,10,1]{3,2,1,0:T(8,128)S(1)}, u32[]{:S(2)}, u32[]{:S(2)}) collective-permute-start(f32[3,9,10,1]{3,2,1,0:T(8,128)S(1)} %pad_maximum_fusion.28), channel_id=1, source_target_pairs={{0,2},{2,4},{4,6},{1,3},{3,5},{5,7},{8,10},{10,12},{12,14},{9,11},... | collective-permute-start | bytes 3248 | tf_op jit(solution)/shard_map/ppermute | solution.py:20
  55.7 5.0 %copy-start.22 = (f32[3,6,1,256]{3,2,1,0:T(1,128)}, f32[3,6,1,256]{3,2,1,0:T(1,128)S(1)}, u32[]{:S(2)}) copy-start(f32[3,6,1,256]{3,2,1,0:T(1,128)S(1)} %collective-permute-done.6) | copy-start | bytes 55300
  55.9 11.4 %collective-permute-start.7 = (f32[3,6,18,1]{3,2,1,0:T(8,128)S(1)}, f32[3,6,18,1]{3,2,1,0:T(8,128)S(1)}, u32[]{:S(2)}, u32[]{:S(2)}) collective-permute-start(f32[3,6,18,1]{3,2,1,0:T(8,128)S(1)} %get-tuple-element.42), channel_id=1, source_target_pairs={{0,2},{2,4},{4,6},{1,3},{3,5},{5,7},{8,10},{10,12},{12,14},{9,11},... | collective-permute-start | bytes 3896 | tf_op jit(solution)/shard_map/ppermute | solution.py:20
  59.4 11.8 %collective-permute-start.8 = (f32[3,6,18,1]{3,2,1,0:T(8,128)S(1)}, f32[3,6,18,1]{3,2,1,0:T(8,128)S(1)}, u32[]{:S(2)}, u32[]{:S(2)}) collective-permute-start(f32[3,6,18,1]{3,2,1,0:T(8,128)S(1)} %get-tuple-element.41), channel_id=1, source_target_pairs={{2,0},{4,2},{6,4},{3,1},{5,3},{7,5},{10,8},{12,10},{14,12},{11,9},... | collective-permute-start | bytes 3896 | tf_op jit(solution)/shard_map/ppermute | solution.py:22
  60.7 7.0 %copy-start.14 = (f32[3,9,10,1]{3,2,1,0:T(8,128)}, f32[3,9,10,1]{3,2,1,0:T(8,128)S(1)}, u32[]{:S(2)}) copy-start(f32[3,9,10,1]{3,2,1,0:T(8,128)S(1)} %collective-permute-done.11) | copy-start | bytes 3244
  60.8 6.6 %copy-start.23 = (f32[3,6,1,256]{3,2,1,0:T(1,128)S(1)}, f32[3,6,1,256]{3,2,1,0:T(1,128)}, u32[]{:S(2)}) copy-start(f32[3,6,1,256]{3,2,1,0:T(1,128)} %copy-done.22) | copy-start | bytes 55300
  61.0 0.7 copy-start.5
  62.8 8.3 %collective-permute-start.3 = (f32[4,5,18,1]{3,2,1,0:T(8,128)S(1)}, f32[4,5,18,1]{3,2,1,0:T(8,128)S(1)}, u32[]{:S(2)}, u32[]{:S(2)}) collective-permute-start(f32[4,5,18,1]{3,2,1,0:T(8,128)S(1)} %pad_maximum_fusion.23), channel_id=1, source_target_pairs={{0,2},{2,4},{4,6},{1,3},{3,5},{5,7},{8,10},{10,12},{12,14},{9,11},... | collective-permute-start | bytes 4328 | tf_op jit(solution)/shard_map/ppermute | solution.py:20
  71.2 1.2 copy-start.12
  71.4 1.5 %copy-start.1 = (f32[3,4,16,256]{3,2,1,0:T(8,128)S(1)}, f32[3,4,16,256]{3,2,1,0:T(8,128)}, u32[]{:S(2)}) copy-start(f32[3,4,16,256]{3,2,1,0:T(8,128)} %param.6) | copy-start | bytes 589828
  71.4 1.5 %copy-start.21 = (f32[3,4,16,256]{3,2,1,0:T(8,128)S(1)}, f32[3,4,16,256]{3,2,1,0:T(8,128)}, u32[]{:S(2)}) copy-start(f32[3,4,16,256]{3,2,1,0:T(8,128)} %param.7) | copy-start | bytes 589828
  78.0 26.4 %copy-start.9 = (f32[3,8,8,128]{3,2,1,0:T(8,128)S(1)}, f32[3,8,8,128]{3,2,1,0:T(8,128)}, u32[]{:S(2)}) copy-start(f32[3,8,8,128]{3,2,1,0:T(8,128)} %fusion.57) | copy-start | bytes 294916
  79.6 1.3 %collective-permute-start.16 = (f32[18432]{0:T(1024)S(1)}, f32[18432]{0:T(1024)S(1)}, u32[]{:S(2)}, u32[]{:S(2)}) collective-permute-start(f32[18432]{0:T(1024)S(1)} %pad_maximum_fusion.41), channel_id=1, source_target_pairs={{0,1},{1,0},{2,3},{3,2},{4,5},{5,4},{6,7},{7,6},{8,9},{9,8},{10,11... | collective-permute-start | bytes 221192 | tf_op jit(solution)/shard_map/ppermute | solution.py:30
  82.0 6.4 %collective-permute-start.21 = (f32[3,10,1,128]{3,2,1,0:T(1,128)S(1)}, f32[3,10,1,128]{3,2,1,0:T(1,128)S(1)}, u32[]{:S(2)}, u32[]{:S(2)}) collective-permute-start(f32[3,10,1,128]{3,2,1,0:T(1,128)S(1)} %get-tuple-element.69), channel_id=1, source_target_pairs={{0,8},{8,16},{16,24},{1,9},{9,17},{17,25},{2,10},{10,18},{18,26},{... | collective-permute-start | bytes 46088 | tf_op jit(solution)/shard_map/ppermute | solution.py:20
  86.5 5.6 %collective-permute-start.22 = (f32[3,10,1,128]{3,2,1,0:T(1,128)S(1)}, f32[3,10,1,128]{3,2,1,0:T(1,128)S(1)}, u32[]{:S(2)}, u32[]{:S(2)}) collective-permute-start(f32[3,10,1,128]{3,2,1,0:T(1,128)S(1)} %get-tuple-element.70), channel_id=1, source_target_pairs={{8,0},{16,8},{24,16},{9,1},{17,9},{25,17},{10,2},{18,10},{26,18},{... | collective-permute-start | bytes 46088 | tf_op jit(solution)/shard_map/ppermute | solution.py:22
  88.1 23.3 %copy-start.6 = (f32[1,9,9,129]{3,2,1,0:T(8,128)S(1)}, f32[1,9,9,129]{3,2,1,0:T(8,128)}, u32[]{:S(2)}) copy-start(f32[1,9,9,129]{3,2,1,0:T(8,128)} %copy-done.5) | copy-start | bytes 125392
  93.1 18.5 %copy-start.11 = (f32[3,8,8,128]{3,2,1,0:T(8,128)S(1)}, f32[3,8,8,128]{3,2,1,0:T(8,128)}, u32[]{:S(2)}) copy-start(f32[3,8,8,128]{3,2,1,0:T(8,128)} %param.11) | copy-start | bytes 294916
  93.1 18.5 %copy-start.15 = (f32[3,9,10,1]{3,2,1,0:T(8,128)S(1)}, f32[3,9,10,1]{3,2,1,0:T(8,128)}, u32[]{:S(2)}) copy-start(f32[3,9,10,1]{3,2,1,0:T(8,128)} %copy-done.14) | copy-start | bytes 3244
  93.1 18.5 %copy-start.25 = (f32[3,9,1,128]{3,2,1,0:T(1,128)S(1)}, f32[3,9,1,128]{3,2,1,0:T(1,128)}, u32[]{:S(2)}) copy-start(f32[3,9,1,128]{3,2,1,0:T(1,128)} %copy-done.24) | copy-start | bytes 41476
  93.1 18.5 %copy-start.27 = (f32[3,9,1,128]{3,2,1,0:T(1,128)S(1)}, f32[3,9,1,128]{3,2,1,0:T(1,128)}, u32[]{:S(2)}) copy-start(f32[3,9,1,128]{3,2,1,0:T(1,128)} %copy-done.26) | copy-start | bytes 41476
  93.3 11.2 %collective-permute-start.23 = (f32[3,10,10,1]{3,2,1,0:T(8,128)S(1)}, f32[3,10,10,1]{3,2,1,0:T(8,128)S(1)}, u32[]{:S(2)}, u32[]{:S(2)}) collective-permute-start(f32[3,10,10,1]{3,2,1,0:T(8,128)S(1)} %get-tuple-element.58), channel_id=1, source_target_pairs={{0,2},{2,4},{4,6},{1,3},{3,5},{5,7},{8,10},{10,12},{12,14},{9,11},... | collective-permute-start | bytes 3608 | tf_op jit(solution)/shard_map/ppermute | solution.py:20
  97.8 14.2 %collective-permute-start.17 = (f32[3,6,1,256]{3,2,0,1:T(1,128)S(1)}, f32[3,6,1,256]{3,2,0,1:T(1,128)S(1)}, u32[]{:S(2)}, u32[]{:S(2)}) collective-permute-start(f32[3,6,1,256]{3,2,0,1:T(1,128)S(1)} %get-tuple-element.51), channel_id=1, source_target_pairs={{0,8},{8,16},{16,24},{1,9},{9,17},{17,25},{2,10},{10,18},{18,26},{... | collective-permute-start | bytes 55304 | tf_op jit(solution)/shard_map/ppermute | solution.py:20
  101.8 10.2 %collective-permute-start.18 = (f32[3,6,1,256]{3,2,0,1:T(1,128)S(1)}, f32[3,6,1,256]{3,2,0,1:T(1,128)S(1)}, u32[]{:S(2)}, u32[]{:S(2)}) collective-permute-start(f32[3,6,1,256]{3,2,0,1:T(1,128)S(1)} %get-tuple-element.52), channel_id=1, source_target_pairs={{8,0},{16,8},{24,16},{9,1},{17,9},{25,17},{10,2},{18,10},{26,18},{... | collective-permute-start | bytes 55304 | tf_op jit(solution)/shard_map/ppermute | solution.py:22
  103.1 8.1 %collective-permute-start.24 = (f32[3,10,10,1]{3,2,1,0:T(8,128)S(1)}, f32[3,10,10,1]{3,2,1,0:T(8,128)S(1)}, u32[]{:S(2)}, u32[]{:S(2)}) collective-permute-start(f32[3,10,10,1]{3,2,1,0:T(8,128)S(1)} %get-tuple-element.57), channel_id=1, source_target_pairs={{2,0},{4,2},{6,4},{3,1},{5,3},{7,5},{10,8},{12,10},{14,12},{11,9},... | collective-permute-start | bytes 3608 | tf_op jit(solution)/shard_map/ppermute | solution.py:22
  111.4 2.9 %copy-start.8 = (f32[3,8,8,128]{3,2,1,0:T(8,128)S(1)}, f32[3,8,8,128]{3,2,1,0:T(8,128)}, u32[]{:S(2)}) copy-start(f32[3,8,8,128]{3,2,1,0:T(8,128)} %param.9) | copy-start | bytes 294916
  111.5 2.9 %copy-start.20 = (f32[8,8,128]{2,1,0:T(8,128)S(1)}, f32[8,8,128]{2,1,0:T(8,128)}, u32[]{:S(2)}) copy-start(f32[8,8,128]{2,1,0:T(8,128)} %copy-done.19) | copy-start | bytes 98308
  111.5 6.3 %copy-start.13 = (f32[5,17,257]{2,1,0:T(8,128)S(1)}, f32[5,17,257]{2,1,0:T(8,128)}, u32[]{:S(2)}) copy-start(f32[5,17,257]{2,1,0:T(8,128)} %copy-done.12) | copy-start | bytes 262144
  112.3 5.5 %collective-permute-start.19 = (f32[3,6,18,1]{3,2,1,0:T(8,128)S(1)}, f32[3,6,18,1]{3,2,1,0:T(8,128)S(1)}, u32[]{:S(2)}, u32[]{:S(2)}) collective-permute-start(f32[3,6,18,1]{3,2,1,0:T(8,128)S(1)} %copy.82), channel_id=1, source_target_pairs={{0,2},{2,4},{4,6},{1,3},{3,5},{5,7},{8,10},{10,12},{12,14},{9,11},... | collective-permute-start | bytes 3896 | tf_op jit(solution)/shard_map/ppermute | solution.py:20
  115.0 8.5 %copy-start.16 = (f32[5,17,257]{2,1,0:T(8,128)S(1)}, f32[5,17,257]{2,1,0:T(8,128)}, u32[]{:S(2)}) copy-start(f32[5,17,257]{2,1,0:T(8,128)} %get-tuple-element.16) | copy-start | bytes 262144
  115.0 8.0 %collective-permute-start.20 = (f32[3,6,18,1]{3,2,0,1:T(8,128)S(1)}, f32[3,6,18,1]{3,2,0,1:T(8,128)S(1)}, u32[]{:S(2)}, u32[]{:S(2)}) collective-permute-start(f32[3,6,18,1]{3,2,0,1:T(8,128)S(1)} %slice.839), channel_id=1, source_target_pairs={{2,0},{4,2},{6,4},{3,1},{5,3},{7,5},{10,8},{12,10},{14,12},{11,9},... | collective-permute-start | bytes 3896 | tf_op jit(solution)/shard_map/ppermute | solution.py:22
  123.1 1.0 copy-start.4
  123.1 1.3 %copy-start.2 = (f32[3,4,16,256]{3,2,1,0:T(8,128)S(1)}, f32[3,4,16,256]{3,2,1,0:T(8,128)}, u32[]{:S(2)}) copy-start(f32[3,4,16,256]{3,2,1,0:T(8,128)} %param.6) | copy-start | bytes 589828
  123.2 1.3 %copy-start.18 = (f32[4,16,256]{2,1,0:T(8,128)S(1)}, f32[4,16,256]{2,1,0:T(8,128)}, u32[]{:S(2)}) copy-start(f32[4,16,256]{2,1,0:T(8,128)} %copy-done.17) | copy-start | bytes 196612
where the time goes:
time: 126 us; the launch traced here: 125 us
  starting transfers between devices  65.5 us (52%)
  waiting for transfers between devices  30.3 us (24%)
  other arithmetic  14.1 us (11%)
  local copies, waits for them, and re-layouts  13.6 us (11%)
  between operations  1.73 us (1%)
    ppermute x12, starting transfers between devices, with_halo(): lax.ppermute(tail, axis, [(i, (i + 1) % count) for i in range(ends)])  49.7 us
    ppermute x10, waiting for transfers between devices, with_halo(): lax.ppermute(head, axis, [((i + 1) % count, i) for i in range(ends)])  22.1 us
    ppermute x10, starting transfers between devices, with_halo(): lax.ppermute(head, axis, [((i + 1) % count, i) for i in range(ends)])  13.2 us
    another operation x2, local copies, waits for them, and re-layouts, restrict(): plane.reshape(plane.shape[0], plane.shape[1] // 2, 2, plane.shape[2] // 2...  7.05 us
    ppermute x12, waiting for transfers between devices, with_halo(): lax.ppermute(tail, axis, [(i, (i + 1) % count) for i in range(ends)])  6.92 us
    unnamed x63, local copies, waits for them, and re-layouts  2.89 us
  transfers between devices with their start and end apart: 25, of which 8 were waited for; matrix products, arithmetic and copies ran while one was open for 7% of the time, Pallas kernels for 0%

commit v1 on v0

v1 whole, which is shorter than its diff:
```python
import functools

import jax
import jax.numpy as jnp
from jax import lax
from jax.experimental import pallas as pl
from jax.experimental.pallas import tpu as pltpu
from jax.sharding import PartitionSpec as P

time_step = 0.15
LANES = 128
MARGIN = 8
U, Q, RHO, MU, LAM, W = 0, 3, 6, 7, 8, 9
FINE_FIELDS, COARSE_FIELDS = 10, 9


def fine_widths(field, layer, layers):
    bottom, above = layer == layers - 1, layer == layers - 2
    if field < Q:
        return (4 if bottom else 3 if above else 2), 2
    if field <= RHO:
        return (2 if bottom else 1), 1
    return (2 if bottom or above else 1), 2


def coarse_widths(field):
    if field < Q:
        return 2, 2
    if field <= RHO:
        return 1, 1
    return 1, 2


def plane_table(fields, layers, widths):
    table, offset = [], 0
    for layer in range(layers):
        for field in range(fields):
            high, low = widths(field, layer)
            table.append((field, layer, high, low, offset))
            offset += max(high, low)
    return table, offset


def round_up(value, multiple):
    return -(-value // multiple) * multiple


def tables(fine_layers, coarse_layers):
    fine, fine_rows = plane_table(
        FINE_FIELDS, fine_layers, lambda f, l: fine_widths(f, l, fine_layers)
    )
    coarse, coarse_rows = plane_table(COARSE_FIELDS, coarse_layers, lambda f, l: coarse_widths(f))
    assert fine_rows <= LANES and coarse_rows <= LANES
    return fine, round_up(fine_rows, 8), coarse, round_up(coarse_rows, 8)


def plane_of(now, before, material, field):
    if field < Q:
        return now, field
    if field < RHO:
        return before, field - Q
    return material, field - RHO


def pack_x_kernel(fu, fp, fm, cu, cp, cm, to_even, to_odd):
    fine, fine_rows, coarse, _ = tables(fu.shape[1], cu.shape[1])
    tiles = fu.shape[3] // LANES
    coarse_tiles = cu.shape[3] // LANES

    def fill(out, first):
        for group, refs, base, rows, parts in (
            (fine, (fu, fp, fm), 0, fine_rows, tiles),
            (coarse, (cu, cp, cm), tiles * fine_rows, tables(fu.shape[1], cu.shape[1])[3], coarse_tiles),
        ):
            for field, layer, high, low, offset in group:
                ref, comp = plane_of(*refs, field)
                size = high if first else low
                start = 0 if first else ref.shape[2] - low
                for t in range(parts):
                    at = base + t * rows + offset
                    out[at : at + size, :] = ref[
                        comp, layer, start : start + size, t * LANES : (t + 1) * LANES
                    ]

    even = lax.rem(lax.axis_index("gx"), 2) == 0

    @pl.when(even)
    def _():
        fill(to_even, False)
        fill(to_odd, True)

    @pl.when(jnp.logical_not(even))
    def _():
        fill(to_even, True)
        fill(to_odd, False)


def pack_y_kernel(fu, fp, fm, cu, cp, cm, got_even, got_odd, fine_out, coarse_out, to_even, to_odd):
    fine, fine_rows, coarse, coarse_rows = tables(fu.shape[1], cu.shape[1])
    tiles = fu.shape[3] // LANES
    coarse_tiles = cu.shape[3] // LANES
    groups = (
        (fine, (fu, fp, fm), fine_out, 0, fine_rows, tiles),
        (coarse, (cu, cp, cm), coarse_out, tiles * fine_rows, coarse_rows, coarse_tiles),
    )

    def halo(high_ref, low_ref):
        for group, refs, out, base, rows, parts in groups:
            for field, layer, high, low, offset in group:
                cells = out.shape[2] - MARGIN
                for t in range(parts):
                    at = base + t * rows + offset
                    lanes = slice(t * LANES, (t + 1) * LANES)
                    out[field, layer, cells : cells + high, lanes] = high_ref[at : at + high, :]
                    out[field, layer, cells + MARGIN - low : cells + MARGIN, lanes] = low_ref[
                        at : at + low, :
                    ]

    for group, refs, out, base, rows, parts in groups:
        for field, layer, high, low, offset in group:
            cells = out.shape[2] - MARGIN
            ref, comp = plane_of(*refs, field)
            out[field, layer, :cells, :] = ref[comp, layer]
            out[field, layer, cells:, :] = jnp.zeros((MARGIN, out.shape[3]), jnp.float32)

    even = lax.rem(lax.axis_index("gx"), 2) == 0

    @pl.when(even)
    def _():
        halo(got_even, got_odd)

    @pl.when(jnp.logical_not(even))
    def _():
        halo(got_odd, got_even)

    packed = []
    for group, refs, out, base, rows, parts in groups:
        shape = (out.shape[2], LANES)
        lane = lax.broadcasted_iota(jnp.int32, shape, 1)
        firsts = jnp.zeros(shape, jnp.float32)
        lasts = jnp.zeros(shape, jnp.float32)
        for field, layer, high, low, offset in group:
            first = out[field, layer, :, :LANES]
            last = out[field, layer, :, out.shape[3] - LANES :]
            first = pltpu.roll(first, offset, 1) if offset else first
            last = pltpu.roll(last, (offset + low) % LANES, 1)
            firsts = jnp.where((lane >= offset) & (lane < offset + high), first, firsts)
            lasts = jnp.where((lane >= offset) & (lane < offset + low), last, lasts)
        packed.append((firsts, lasts))
    fine_height = fine_out.shape[2]
    even_y = lax.rem(lax.axis_index("gy"), 2) == 0

    @pl.when(even_y)
    def _():
        for k, (firsts, lasts) in enumerate(packed):
            at = slice(0, fine_height) if k == 0 else slice(fine_height, None)
            to_even[at, :] = lasts
            to_odd[at, :] = firsts

    @pl.when(jnp.logical_not(even_y))
    def _():
        for k, (firsts, lasts) in enumerate(packed):
            at = slice(0, fine_height) if k == 0 else slice(fine_height, None)
            to_even[at, :] = firsts
            to_odd[at, :] = lasts


def ahead(value, axis):
    return pltpu.roll(value, value.shape[axis] - 1, axis)


def behind(value, axis):
    return value - pltpu.roll(value, 1, axis)


def stress_of(here, below, medium, stretched):
    rigidity, lame = medium[0], medium[1]
    dx = [ahead(f, 0) - f for f in here]
    dy = [ahead(f, 1) - f for f in here]
    dz = [b - f for b, f in zip(below, here)]
    if stretched:
        dz = [f * medium[2] for f in dz]
    trace = lame * (dx[0] + dy[1] + dz[2])
    double = rigidity + rigidity
    return (
        trace + double * dx[0],
        trace + double * dy[1],
        trace + double * dz[2],
        rigidity * (dy[0] + dx[1]),
        rigidity * (dz[0] + dx[2]),
        rigidity * (dz[1] + dy[2]),
    )


def force_of(stress, above, outward):
    nx, ny, nz, xy, xz, yz = stress
    up = [xz - above[0], yz - above[1], nz - above[2]]
    if outward is not None:
        up = [f * outward for f in up]
    return (
        behind(nx, 0) + behind(xy, 1) + up[0],
        behind(xy, 0) + behind(ny, 1) + up[1],
        behind(xz, 0) + behind(yz, 1) + up[2],
    )


def vertical(stress):
    return (stress[4], stress[5], stress[2])


def steps_kernel(
    own_f, own_c, far_f, far_c, own_ye, own_yo, far_ye, far_yo, fine_ref, coarse_ref, fs, fn, cs, cn
):
    layers, height, width = own_f.shape[1:]
    clayers, cheight, cwidth = own_c.shape[1:]
    n, nc = height - MARGIN, cheight - MARGIN
    full, cfull = width + LANES, cwidth + LANES
    depth, cdepth = 2 * layers, 2 * clayers
    fine, _, coarse, _ = tables(layers, clayers)
    gx, gy, dev = lax.axis_index("gx"), lax.axis_index("gy"), lax.axis_index("dev")
    nx, ny = lax.axis_size("gx"), lax.axis_size("gy")

    def assemble(high_ref, low_ref, from_f, from_c, half):
        for group, src, dst, top, count in (
            (fine, from_f, fs, 0, layers),
            (coarse, from_c, cs, height, clayers),
        ):
            rows = src.shape[2]
            lane = lax.broadcasted_iota(jnp.int32, (rows, LANES), 1)
            highs, lows = high_ref[top : top + rows, :], low_ref[top : top + rows, :]
            for field, layer, high, low, offset in group:
                side = jnp.where(
                    lane < high, pltpu.roll(highs, (LANES - offset) % LANES, 1), 0.0
                )
                side = jnp.where(
                    lane >= LANES - low, pltpu.roll(lows, LANES - low - offset, 1), side
                )
                at = half * count + layer
                dst[field, at, :, : src.shape[3]] = src[field, layer]
                dst[field, at, :, src.shape[3] :] = side

    even_y = lax.rem(gy, 2) == 0

    @pl.when(even_y)
    def _():
        assemble(own_ye, own_yo, own_f, own_c, dev)
        assemble(far_ye, far_yo, far_f, far_c, 1 - dev)

    @pl.when(jnp.logical_not(even_y))
    def _():
        assemble(own_yo, own_ye, own_f, own_c, dev)
        assemble(far_yo, far_ye, far_f, far_c, 1 - dev)

    def position(size, extent, axis, shape, turn):
        index = lax.broadcasted_iota(jnp.int32, shape, axis)
        return jnp.where(index < turn, index, index - size)

    fx = position(height, n, 0, (height, full), n + 4)
    fy = position(full, width, 1, (height, full), width + 64)
    cx = position(cheight, nc, 0, (cheight, cfull), nc + 4)
    cy = position(cfull, cwidth, 1, (cheight, cfull), cwidth + 64)
    in_domain_f = (
        (fx + gx * n >= 0) & (fx + gx * n < nx * n)
        & (fy + gy * width >= 0) & (fy + gy * width < ny * width)
    )
    in_domain_c = (
        (cx + gx * nc >= 0) & (cx + gx * nc < nx * nc)
        & (cy + gy * cwidth >= 0) & (cy + gy * cwidth < ny * cwidth)
        & (cx >= -1) & (cx <= nc) & (cy >= -1) & (cy <= cwidth)
    )

    def wrap(index, turn, size):
        return jnp.where(index < turn, index, index - size)

    def pairing(fine_size, fine_turn, coarse_size, transpose):
        shape = (coarse_size, fine_size) if transpose else (fine_size, coarse_size)
        f = wrap(lax.broadcasted_iota(jnp.int32, shape, 1 if transpose else 0), fine_turn, fine_size)
        c = lax.broadcasted_iota(jnp.int32, shape, 0 if transpose else 1)
        half = jnp.right_shift(f, 1)
        half = jnp.where(half < 0, half + coarse_size, half)
        return (half == c).astype(jnp.float32)

    dot = functools.partial(
        jnp.dot, precision=lax.Precision.HIGHEST, preferred_element_type=jnp.float32
    )

    def prolong(plane):
        rows = pairing(height, n + 4, cheight, False)
        lanes = pairing(full, width + 64, cfull, True)
        return dot(rows, dot(plane, lanes))

    def restrict(plane):
        rows = pairing(height, n + 4, cheight, True)
        lanes = pairing(full, width + 64, cfull, False)
        return dot(rows, dot(plane, lanes)) * 0.25

    def ghosts(fine_state, coarse_state):
        for k in range(3):
            fine_state[k, depth] = prolong(coarse_state[k, 1])
            coarse_state[k, 0] = restrict(fine_state[k, depth - 1])

    for k in range(3):
        fn[k, depth] = jnp.zeros((height, full), jnp.float32)
        zero = jnp.zeros((cheight, cfull), jnp.float32)
        cn[k, cdepth + 1] = zero

    @pl.loop(0, cdepth)
    def _(g):
        for k in range(3):
            cn[k, g + 1] = cs[k, g]

    for k in range(3):
        fs[k, depth] = prolong(cn[k, 1])
        cn[k, 0] = restrict(fs[k, depth - 1])

    scale = jnp.float32(time_step * time_step)

    def fine_stress(state, g):
        return stress_of(
            [state[k, g] for k in range(3)],
            [state[k, g + 1] for k in range(3)],
            [fs[k, g] for k in (MU, LAM, W)],
            True,
        )

    def coarse_stress(state, g):
        row = jnp.maximum(g, 0)
        return stress_of(
            [state[k, g + 1] for k in range(3)],
            [state[k, g + 2] for k in range(3)],
            [cs[k, row] for k in (MU, LAM)],
            False,
        )

    def first_fine(g, above):
        stress = fine_stress(fs, g)
        force = force_of(stress, above, fs[W, g])
        rate = scale / fs[RHO, g]
        last = (g == depth - 1).astype(jnp.int32)
        keep = in_domain_f & (fx >= -1) & (fx <= n + last) & (fy >= -1) & (fy <= width + last)
        for k in range(3):
            u = fs[k, g]
            fn[k, g] = jnp.where(keep, u + u - fs[Q + k, g] + force[k] * rate, 0.0)
        return vertical(stress)

    nothing = jnp.zeros((height, full), jnp.float32)
    lax.fori_loop(0, depth, first_fine, (nothing, nothing, nothing))

    def first_coarse(g, above):
        stress = coarse_stress(cn, g)
        force = force_of(stress, above, None)
        rate = (0.25 * scale) / cs[RHO, g]
        for k in range(3):
            v = cs[k, g]
            cs[Q + k, g] = jnp.where(
                in_domain_c, v + v - cs[Q + k, g] + force[k] * rate, 0.0
            )
        return vertical(stress)

    lax.fori_loop(0, cdepth, first_coarse, vertical(coarse_stress(cn, -1)))

    @pl.loop(0, cdepth)
    def _(g):
        for k in range(3):
            cn[k, g + 1] = cs[Q + k, g]

    for k in range(3):
        fn[k, depth] = prolong(cn[k, 1])
        cn[k, 0] = restrict(fn[k, depth - 1])

    def second_fine(l, above):
        g = dev * layers + l
        stress = fine_stress(fn, g)
        force = force_of(stress, above, fs[W, g])
        rate = scale / fs[RHO, g]
        for k in range(3):
            u = fn[k, g]
            out = u + u - fs[k, g] + force[k] * rate
            fine_ref[k, l] = out[:n, :width]
        return vertical(stress)

    start = jnp.maximum(dev * layers - 1, 0)
    entry = [jnp.where(dev == 0, 0.0, f) for f in vertical(fine_stress(fn, start))]
    lax.fori_loop(0, layers, second_fine, tuple(entry))

    def second_coarse(l, above):
        g = dev * clayers + l
        stress = coarse_stress(cn, g)
        force = force_of(stress, above, None)
        rate = (0.25 * scale) / cs[RHO, g]
        for k in range(3):
            v = cn[k, g + 1]
            out = v + v - cs[k, g] + force[k] * rate
            coarse_ref[k, l] = out[:nc, :cwidth]
        return vertical(stress)

    lax.fori_loop(0, clayers, second_coarse, vertical(coarse_stress(cn, dev * clayers - 1)))


def partners(count, parity):
    pairs = [(i, ((i + parity) ^ 1) - parity) for i in range(count)]
    return [(i, j) for i, j in pairs if 0 <= j < count]


def swap(value, axis, parity):
    return lax.ppermute(value, axis, partners(lax.axis_size(axis), parity))


def call(kernel, out_shape, operands, scratch=(), flops=0):
    vmem = pl.BlockSpec(memory_space=pltpu.VMEM)
    size = sum(o.size for o in jax.tree.leaves(out_shape)) * 4
    return pl.pallas_call(
        kernel,
        out_shape=out_shape,
        in_specs=[vmem] * len(operands),
        out_specs=[vmem] * len(out_shape),
        scratch_shapes=list(scratch),
        cost_estimate=pl.CostEstimate(flops=flops, bytes_accessed=size, transcendentals=0),
        compiler_params=pltpu.CompilerParams(vmem_limit_bytes=32 * 1024 * 1024),
    )(*operands)


def shape(*dims):
    return jax.ShapeDtypeStruct(dims, jnp.float32)


def per_device(fine_now, fine_before, fine_material, coarse_now, coarse_before, coarse_material):
    inputs = (fine_now, fine_before, fine_material, coarse_now, coarse_before, coarse_material)
    _, layers, n, width = fine_now.shape
    _, clayers, nc, cwidth = coarse_now.shape
    _, fine_rows, _, coarse_rows = tables(layers, clayers)
    rows = (width // LANES) * fine_rows + (cwidth // LANES) * coarse_rows
    height, cheight = n + MARGIN, nc + MARGIN

    edge = shape(rows, LANES)
    to_even, to_odd = call(pack_x_kernel, (edge, edge), inputs)
    got_odd = swap(to_odd, "gx", 1)
    got_even = swap(to_even, "gx", 0)

    side = shape(height + cheight, LANES)
    tiles = (shape(FINE_FIELDS, layers, height, width), shape(COARSE_FIELDS, clayers, cheight, cwidth))
    own_f, own_c, to_even, to_odd = call(
        pack_y_kernel, tiles + (side, side), inputs + (got_even, got_odd)
    )
    own_yo = swap(to_odd, "gy", 1)
    own_ye = swap(to_even, "gy", 0)
    far_f, far_c = swap(own_f, "dev", 0), swap(own_c, "dev", 0)
    far_yo, far_ye = swap(own_yo, "dev", 0), swap(own_ye, "dev", 0)

    full, cfull = width + LANES, cwidth + LANES
    return call(
        steps_kernel,
        (shape(*fine_now.shape), shape(*coarse_now.shape)),
        (own_f, own_c, far_f, far_c, own_ye, own_yo, far_ye, far_yo),
        scratch=(
            pltpu.VMEM((FINE_FIELDS, 2 * layers + 1, height, full), jnp.float32),
            pltpu.VMEM((3, 2 * layers + 1, height, full), jnp.float32),
            pltpu.VMEM((COARSE_FIELDS, 2 * clayers, cheight, cfull), jnp.float32),
            pltpu.VMEM((3, 2 * clayers + 2, cheight, cfull), jnp.float32),
        ),
    )


def solution(mesh):
    spec = P(None, "dev", "gx", "gy")
    return jax.shard_map(
        per_device,
        mesh=mesh,
        in_specs=(spec,) * 6,
        out_specs=(spec, spec),
        check_vma=False,
    )
```

time: 126 us -> 40.2 us (0.32)
  the two profiles are of different devices: /device:TPU:0 before, /device:TPU:21 now
where the time goes in v1:
time: 40.2 us; the launch traced here: 39.9 us
  Pallas kernels  15 us (37%)
  starting transfers between devices  11.4 us (28%)
  waiting for transfers between devices  7.4 us (18%)
  local copies, waits for them, and re-layouts  5.47 us (14%)
  between operations  0.69 us (2%)
    pallas_call x3, Pallas kernels, call(): pl.pallas_call(kernel, out_shape=out_shape, in_specs=[vmem] * len(operand...  15 us
    ppermute x8, starting transfers between devices, swap(): return lax.ppermute(value, axis, partners(lax.axis_size(axis), parity))  11.4 us
    ppermute x8, waiting for transfers between devices, swap(): return lax.ppermute(value, axis, partners(lax.axis_size(axis), parity))  7.4 us
    unnamed x12, local copies, waits for them, and re-layouts  5.47 us
  transfers between devices with their start and end apart: 8, of which 4 were waited for; matrix products, arithmetic and copies ran while one was open for 0% of the time, Pallas kernels for 0%

profile of v1, /device:TPU:21, one launch (start us, length us, event | category | flops | bytes accessed | tf_op | source)
XLA Modules:
  0.0 39.9 jit_solution(17984369391377936452)
XLA Ops:
  0.6 0.0 copy-start
  0.6 0.9 %copy-done = f32[4,4,16,256]{3,2,1,0:T(8,128)S(1)} copy-done((f32[4,4,16,256]{3,2,1,0:T(8,128)S(1)}, f32[4,4,16,256]{3,2,1,0:T(8,128)}, u32[]{:S(2)}) %copy-start) | copy-done | bytes 262168
  1.6 0.0 copy-start.1
  1.6 0.9 %copy-done.1 = f32[3,4,16,256]{3,2,1,0:T(8,128)S(1)} copy-done((f32[3,4,16,256]{3,2,1,0:T(8,128)S(1)}, f32[3,4,16,256]{3,2,1,0:T(8,128)}, u32[]{:S(2)}) %copy-start.1) | copy-done | bytes 196632
  2.5 0.0 copy-start.2
  2.5 0.9 %copy-done.2 = f32[3,4,16,256]{3,2,1,0:T(8,128)S(1)} copy-done((f32[3,4,16,256]{3,2,1,0:T(8,128)S(1)}, f32[3,4,16,256]{3,2,1,0:T(8,128)}, u32[]{:S(2)}) %copy-start.2) | copy-done | bytes 196632
  3.4 0.0 copy-start.3
  3.4 0.9 %copy-done.3 = f32[3,8,8,128]{3,2,1,0:T(8,128)S(1)} copy-done((f32[3,8,8,128]{3,2,1,0:T(8,128)S(1)}, f32[3,8,8,128]{3,2,1,0:T(8,128)}, u32[]{:S(2)}) %copy-start.3) | copy-done | bytes 98328
  4.3 0.0 copy-start.4
  4.3 0.9 %copy-done.4 = f32[3,8,8,128]{3,2,1,0:T(8,128)S(1)} copy-done((f32[3,8,8,128]{3,2,1,0:T(8,128)S(1)}, f32[3,8,8,128]{3,2,1,0:T(8,128)}, u32[]{:S(2)}) %copy-start.4) | copy-done | bytes 98328
  5.2 0.0 copy-start.5
  5.2 0.9 %copy-done.5 = f32[3,8,8,128]{3,2,1,0:T(8,128)S(1)} copy-done((f32[3,8,8,128]{3,2,1,0:T(8,128)S(1)}, f32[3,8,8,128]{3,2,1,0:T(8,128)}, u32[]{:S(2)}) %copy-start.5) | copy-done | bytes 98328
  6.1 0.1 shard_map.77
  6.2 1.3 %collective-permute-start = (f32[272,128]{1,0:T(8,128)S(1)}, f32[272,128]{1,0:T(8,128)S(1)}, u32[]{:S(2)}, u32[]{:S(2)}) collective-permute-start(f32[272,128]{1,0:T(8,128)S(1)} %get-tuple-element.8), channel_id=1, source_target_pairs={{0,8},{8,0},{16,24},{24,16},{1,9},{9,1},{17,25},{25,17},{2,10},{10... | collective-permute-start | bytes 417800 | tf_op jit(solution)/shard_map/ppermute | solution.py:406
  7.5 2.1 %collective-permute-start.1 = (f32[272,128]{1,0:T(8,128)S(1)}, f32[272,128]{1,0:T(8,128)S(1)}, u32[]{:S(2)}, u32[]{:S(2)}) collective-permute-start(f32[272,128]{1,0:T(8,128)S(1)} %get-tuple-element.9), channel_id=1, source_target_pairs={{8,16},{16,8},{9,17},{17,9},{10,18},{18,10},{11,19},{19,11},{12,20... | collective-permute-start | bytes 417800 | tf_op jit(solution)/shard_map/ppermute | solution.py:406
  9.6 1.2 %collective-permute-done.got_even = f32[272,128]{1,0:T(8,128)S(1)} collective-permute-done((f32[272,128]{1,0:T(8,128)S(1)}, f32[272,128]{1,0:T(8,128)S(1)}, u32[]{:S(2)}, u32[]{:S(2)}) %collective-permute-start) | collective-permute-done | bytes 139296 | tf_op jit(solution)/shard_map/ppermute | solution.py:406
  10.9 3.7 %collective-permute-done.1.got_odd = f32[272,128]{1,0:T(8,128)S(1)} collective-permute-done((f32[272,128]{1,0:T(8,128)S(1)}, f32[272,128]{1,0:T(8,128)S(1)}, u32[]{:S(2)}, u32[]{:S(2)}) %collective-permute-start.1) | collective-permute-done | bytes 139296 | tf_op jit(solution)/shard_map/ppermute | solution.py:406
  14.6 0.9 %shard_map.78 = (f32[10,4,24,256]{3,2,1,0:T(8,128)S(1)}, f32[9,8,16,128]{3,2,1,0:T(8,128)S(1)}, f32[40,128]{1,0:T(8,128)S(1)}, f32[40,128]{1,0:T(8,128)S(1)}) custom-call(f32[3,4,16,256]{3,2,1,0:T(8,128)S(1)} %copy-done.1, f32[3,4,16,256]{3,2,1,0:T(8,128)S(1)} %copy-done.2, f32[4,4,16,256]{3,2,1,0:T(8,128)S(1)} %copy-done, f32[3,8,8,128]{3,2,1,0:T(8,128)S(1)} %copy-done.3, ...), custom_call_target="tpu_custom_call" | custom-call | bytes 1613824 | tf_op jit(solution)/shard_map/pallas_call | solution.py:412
  15.4 1.9 %collective-permute-start.2 = (f32[10,4,24,256]{3,2,1,0:T(8,128)S(1)}, f32[10,4,24,256]{3,2,1,0:T(8,128)S(1)}, u32[]{:S(2)}, u32[]{:S(2)}) collective-permute-start(f32[10,4,24,256]{3,2,1,0:T(8,128)S(1)} %get-tuple-element.10.own_f), channel_id=1, source_target_pairs={{0,1},{1,0},{2,3},{3,2},{4,5},{5,4},{6,7},{7,6},{8,9},{9,8},{10,11... | collective-permute-start | bytes 2949128 | tf_op jit(solution)/shard_map/ppermute | solution.py:406
  17.3 0.1 collective-permute-start.3
  17.4 1.3 %collective-permute-start.4 = (f32[40,128]{1,0:T(8,128)S(1)}, f32[40,128]{1,0:T(8,128)S(1)}, u32[]{:S(2)}, u32[]{:S(2)}) collective-permute-start(f32[40,128]{1,0:T(8,128)S(1)} %get-tuple-element.12), channel_id=1, source_target_pairs={{0,2},{2,0},{4,6},{6,4},{1,3},{3,1},{5,7},{7,5},{8,10},{10,8},{12,... | collective-permute-start | bytes 61448 | tf_op jit(solution)/shard_map/ppermute | solution.py:406
  18.7 1.9 %collective-permute-start.5 = (f32[40,128]{1,0:T(8,128)S(1)}, f32[40,128]{1,0:T(8,128)S(1)}, u32[]{:S(2)}, u32[]{:S(2)}) collective-permute-start(f32[40,128]{1,0:T(8,128)S(1)} %get-tuple-element.13), channel_id=1, source_target_pairs={{2,4},{4,2},{3,5},{5,3},{10,12},{12,10},{11,13},{13,11},{18,20},{2... | collective-permute-start | bytes 61448 | tf_op jit(solution)/shard_map/ppermute | solution.py:406
  20.6 0.0 collective-permute-done.4.own_ye
  20.6 1.0 %collective-permute-start.6 = (f32[40,128]{1,0:T(8,128)S(1)}, f32[40,128]{1,0:T(8,128)S(1)}, u32[]{:S(2)}, u32[]{:S(2)}) collective-permute-start(f32[40,128]{1,0:T(8,128)S(1)} %collective-permute-done.4.own_ye), channel_id=1, source_target_pairs={{0,1},{1,0},{2,3},{3,2},{4,5},{5,4},{6,7},{7,6},{8,9},{9,8},{10,11... | collective-permute-start | bytes 61448 | tf_op jit(solution)/shard_map/ppermute | solution.py:406
  21.6 1.6 %collective-permute-done.5.own_yo = f32[40,128]{1,0:T(8,128)S(1)} collective-permute-done((f32[40,128]{1,0:T(8,128)S(1)}, f32[40,128]{1,0:T(8,128)S(1)}, u32[]{:S(2)}, u32[]{:S(2)}) %collective-permute-start.5) | collective-permute-done | bytes 20512 | tf_op jit(solution)/shard_map/ppermute | solution.py:406
  23.2 1.9 %collective-permute-start.7 = (f32[40,128]{1,0:T(8,128)S(1)}, f32[40,128]{1,0:T(8,128)S(1)}, u32[]{:S(2)}, u32[]{:S(2)}) collective-permute-start(f32[40,128]{1,0:T(8,128)S(1)} %collective-permute-done.5.own_yo), channel_id=1, source_target_pairs={{0,1},{1,0},{2,3},{3,2},{4,5},{5,4},{6,7},{7,6},{8,9},{9,8},{10,11... | collective-permute-start | bytes 61448 | tf_op jit(solution)/shard_map/ppermute | solution.py:406
  25.1 0.0 collective-permute-done.6.far_ye
  25.1 0.8 %collective-permute-done.7.far_yo = f32[40,128]{1,0:T(8,128)S(1)} collective-permute-done((f32[40,128]{1,0:T(8,128)S(1)}, f32[40,128]{1,0:T(8,128)S(1)}, u32[]{:S(2)}, u32[]{:S(2)}) %collective-permute-start.7) | collective-permute-done | bytes 20512 | tf_op jit(solution)/shard_map/ppermute | solution.py:406
  25.9 0.0 collective-permute-done.3.far_c
  25.9 0.0 collective-permute-done.2.far_f
  25.9 14.0 %shard_map.79 = (f32[3,4,16,256]{3,2,1,0:T(8,128)}, f32[3,8,8,128]{3,2,1,0:T(8,128)}) custom-call(f32[10,4,24,256]{3,2,1,0:T(8,128)S(1)} %get-tuple-element.10.own_f, f32[9,8,16,128]{3,2,1,0:T(8,128)S(1)} %get-tuple-element.11.own_c, f32[10,4,24,256]{3,2,1,0:T(8,128)S(1)} %collective-permute-done.2.far_f, ...), custom_call_target="tpu_custom_call" | custom-call | bytes 294912 | tf_op jit(solution)/shard_map/pallas_call | solution.py:412
Async XLA Ops:
  0.6 1.0 %copy-start = (f32[4,4,16,256]{3,2,1,0:T(8,128)S(1)}, f32[4,4,16,256]{3,2,1,0:T(8,128)}, u32[]{:S(2)}) copy-start(f32[4,4,16,256]{3,2,1,0:T(8,128)} %fm.3) | copy-start | bytes 786436
  1.6 0.9 %copy-start.1 = (f32[3,4,16,256]{3,2,1,0:T(8,128)S(1)}, f32[3,4,16,256]{3,2,1,0:T(8,128)}, u32[]{:S(2)}) copy-start(f32[3,4,16,256]{3,2,1,0:T(8,128)} %fu.3) | copy-start | bytes 589828
  2.5 0.9 %copy-start.2 = (f32[3,4,16,256]{3,2,1,0:T(8,128)S(1)}, f32[3,4,16,256]{3,2,1,0:T(8,128)}, u32[]{:S(2)}) copy-start(f32[3,4,16,256]{3,2,1,0:T(8,128)} %fp.3) | copy-start | bytes 589828
  3.4 0.9 %copy-start.3 = (f32[3,8,8,128]{3,2,1,0:T(8,128)S(1)}, f32[3,8,8,128]{3,2,1,0:T(8,128)}, u32[]{:S(2)}) copy-start(f32[3,8,8,128]{3,2,1,0:T(8,128)} %cu.3) | copy-start | bytes 294916
  4.3 0.9 %copy-start.4 = (f32[3,8,8,128]{3,2,1,0:T(8,128)S(1)}, f32[3,8,8,128]{3,2,1,0:T(8,128)}, u32[]{:S(2)}) copy-start(f32[3,8,8,128]{3,2,1,0:T(8,128)} %cp.3) | copy-start | bytes 294916
  5.2 0.9 %copy-start.5 = (f32[3,8,8,128]{3,2,1,0:T(8,128)S(1)}, f32[3,8,8,128]{3,2,1,0:T(8,128)}, u32[]{:S(2)}) copy-start(f32[3,8,8,128]{3,2,1,0:T(8,128)} %cm.3) | copy-start | bytes 294916
  6.2 4.6 %collective-permute-start = (f32[272,128]{1,0:T(8,128)S(1)}, f32[272,128]{1,0:T(8,128)S(1)}, u32[]{:S(2)}, u32[]{:S(2)}) collective-permute-start(f32[272,128]{1,0:T(8,128)S(1)} %get-tuple-element.8), channel_id=1, source_target_pairs={{0,8},{8,0},{16,24},{24,16},{1,9},{9,1},{17,25},{25,17},{2,10},{10... | collective-permute-start | bytes 417800 | tf_op jit(solution)/shard_map/ppermute | solution.py:406
  7.5 7.1 %collective-permute-start.1 = (f32[272,128]{1,0:T(8,128)S(1)}, f32[272,128]{1,0:T(8,128)S(1)}, u32[]{:S(2)}, u32[]{:S(2)}) collective-permute-start(f32[272,128]{1,0:T(8,128)S(1)} %get-tuple-element.9), channel_id=1, source_target_pairs={{8,16},{16,8},{9,17},{17,9},{10,18},{18,10},{11,19},{19,11},{12,20... | collective-permute-start | bytes 417800 | tf_op jit(solution)/shard_map/ppermute | solution.py:406
  15.4 10.5 %collective-permute-start.2 = (f32[10,4,24,256]{3,2,1,0:T(8,128)S(1)}, f32[10,4,24,256]{3,2,1,0:T(8,128)S(1)}, u32[]{:S(2)}, u32[]{:S(2)}) collective-permute-start(f32[10,4,24,256]{3,2,1,0:T(8,128)S(1)} %get-tuple-element.10.own_f), channel_id=1, source_target_pairs={{0,1},{1,0},{2,3},{3,2},{4,5},{5,4},{6,7},{7,6},{8,9},{9,8},{10,11... | collective-permute-start | bytes 2949128 | tf_op jit(solution)/shard_map/ppermute | solution.py:406
  17.3 8.6 %collective-permute-start.3 = (f32[9,8,16,128]{3,2,1,0:T(8,128)S(1)}, f32[9,8,16,128]{3,2,1,0:T(8,128)S(1)}, u32[]{:S(2)}, u32[]{:S(2)}) collective-permute-start(f32[9,8,16,128]{3,2,1,0:T(8,128)S(1)} %get-tuple-element.11.own_c), channel_id=1, source_target_pairs={{0,1},{1,0},{2,3},{3,2},{4,5},{5,4},{6,7},{7,6},{8,9},{9,8},{10,11... | collective-permute-start | bytes 1769480 | tf_op jit(solution)/shard_map/ppermute | solution.py:406
  17.4 3.2 %collective-permute-start.4 = (f32[40,128]{1,0:T(8,128)S(1)}, f32[40,128]{1,0:T(8,128)S(1)}, u32[]{:S(2)}, u32[]{:S(2)}) collective-permute-start(f32[40,128]{1,0:T(8,128)S(1)} %get-tuple-element.12), channel_id=1, source_target_pairs={{0,2},{2,0},{4,6},{6,4},{1,3},{3,1},{5,7},{7,5},{8,10},{10,8},{12,... | collective-permute-start | bytes 61448 | tf_op jit(solution)/shard_map/ppermute | solution.py:406
  18.7 4.5 %collective-permute-start.5 = (f32[40,128]{1,0:T(8,128)S(1)}, f32[40,128]{1,0:T(8,128)S(1)}, u32[]{:S(2)}, u32[]{:S(2)}) collective-permute-start(f32[40,128]{1,0:T(8,128)S(1)} %get-tuple-element.13), channel_id=1, source_target_pairs={{2,4},{4,2},{3,5},{5,3},{10,12},{12,10},{11,13},{13,11},{18,20},{2... | collective-permute-start | bytes 61448 | tf_op jit(solution)/shard_map/ppermute | solution.py:406
  20.6 4.5 %collective-permute-start.6 = (f32[40,128]{1,0:T(8,128)S(1)}, f32[40,128]{1,0:T(8,128)S(1)}, u32[]{:S(2)}, u32[]{:S(2)}) collective-permute-start(f32[40,128]{1,0:T(8,128)S(1)} %collective-permute-done.4.own_ye), channel_id=1, source_target_pairs={{0,1},{1,0},{2,3},{3,2},{4,5},{5,4},{6,7},{7,6},{8,9},{9,8},{10,11... | collective-permute-start | bytes 61448 | tf_op jit(solution)/shard_map/ppermute | solution.py:406
  23.2 2.7 %collective-permute-start.7 = (f32[40,128]{1,0:T(8,128)S(1)}, f32[40,128]{1,0:T(8,128)S(1)}, u32[]{:S(2)}, u32[]{:S(2)}) collective-permute-start(f32[40,128]{1,0:T(8,128)S(1)} %collective-permute-done.5.own_yo), channel_id=1, source_target_pairs={{0,1},{1,0},{2,3},{3,2},{4,5},{5,4},{6,7},{7,6},{8,9},{9,8},{10,11... | collective-permute-start | bytes 61448 | tf_op jit(solution)/shard_map/ppermute | solution.py:406

commit v2 on v1

v2 whole, which is shorter than its diff:
```python
import jax
import jax.numpy as jnp
from jax import lax
from jax.experimental import pallas as pl
from jax.experimental.pallas import tpu as pltpu
from jax.sharding import PartitionSpec as P


time_step = 0.15
LANES = 128
MARGIN = 8
U, Q, RHO, MU, LAM, W = 0, 3, 6, 7, 8, 9
FINE_FIELDS, COARSE_FIELDS = 10, 9


def fine_widths(field, layer, layers):
    bottom, above = layer == layers - 1, layer == layers - 2
    if field < Q:
        return (4 if bottom else 3 if above else 2), 2
    if field <= RHO:
        return (2 if bottom else 1), 1
    return (2 if bottom or above else 1), 2


def coarse_widths(field):
    if field < Q:
        return 2, 2
    if field <= RHO:
        return 1, 1
    return 1, 2


def plane_table(fields, layers, widths):
    table, offset = [], 0
    for layer in range(layers):
        for field in range(fields):
            high, low = widths(field, layer)
            table.append((field, layer, high, low, offset))
            offset += max(high, low)
    return table, offset


def round_up(value, multiple):
    return -(-value // multiple) * multiple


def tables(fine_layers, coarse_layers):
    fine, fine_rows = plane_table(
        FINE_FIELDS, fine_layers, lambda f, l: fine_widths(f, l, fine_layers)
    )
    coarse, coarse_rows = plane_table(COARSE_FIELDS, coarse_layers, lambda f, l: coarse_widths(f))
    assert fine_rows <= LANES and coarse_rows <= LANES
    return fine, round_up(fine_rows, 8), coarse, round_up(coarse_rows, 8)


def groups_of(fine_layers, coarse_layers, fine_parts, coarse_parts):
    fine, fine_rows, coarse, coarse_rows = tables(fine_layers, coarse_layers)
    return (fine, 0, fine_rows, fine_parts), (
        coarse,
        fine_parts * fine_rows,
        coarse_rows,
        coarse_parts,
    )


def pack_x_kernel(fu, fp, fm, cu, cp, cm, fine, coarse, to_even, to_odd, sems):
    copies = []
    for out, sources in ((fine, (fu, fp, fm)), (coarse, (cu, cp, cm))):
        for first, source in zip((U, Q, RHO), sources):
            copies.append(
                pltpu.make_async_copy(
                    source, out.at[first : first + source.shape[0]], sems.at[len(copies)]
                )
            )
    for copy in copies:
        copy.start()
    for copy in copies:
        copy.wait()
    groups = groups_of(
        fine.shape[1], coarse.shape[1], fine.shape[3] // LANES, coarse.shape[3] // LANES
    )

    def fill(out, first):
        for (table, base, rows, parts), ref in zip(groups, (fine, coarse)):
            for field, layer, high, low, offset in table:
                size = high if first else low
                start = 0 if first else ref.shape[2] - low
                for t in range(parts):
                    at = base + t * rows + offset
                    out[at : at + size, :] = ref[
                        field, layer, start : start + size, t * LANES : (t + 1) * LANES
                    ]

    even = lax.rem(lax.axis_index("gx"), 2) == 0

    @pl.when(even)
    def _():
        fill(to_even, False)
        fill(to_odd, True)

    @pl.when(jnp.logical_not(even))
    def _():
        fill(to_even, True)
        fill(to_odd, False)


def pack_y_kernel(fine, coarse, got_even, got_odd, fine_halo, coarse_halo, to_even, to_odd):
    groups = groups_of(
        fine.shape[1], coarse.shape[1], fine.shape[3] // LANES, coarse.shape[3] // LANES
    )

    def halo(high_ref, low_ref):
        for (table, base, rows, parts), out in zip(groups, (fine_halo, coarse_halo)):
            for field, layer, high, low, offset in table:
                for t in range(parts):
                    at = base + t * rows + offset
                    lanes = slice(t * LANES, (t + 1) * LANES)
                    out[field, layer, :high, lanes] = high_ref[at : at + high, :]
                    out[field, layer, MARGIN - low :, lanes] = low_ref[at : at + low, :]

    for (table, *_), out in zip(groups, (fine_halo, coarse_halo)):
        for field, layer, high, low, offset in table:
            out[field, layer] = jnp.zeros((MARGIN, out.shape[3]), jnp.float32)

    even = lax.rem(lax.axis_index("gx"), 2) == 0

    @pl.when(even)
    def _():
        halo(got_even, got_odd)

    @pl.when(jnp.logical_not(even))
    def _():
        halo(got_odd, got_even)

    packed = []
    for (table, *_), ref, edge in zip(groups, (fine, coarse), (fine_halo, coarse_halo)):
        shape = (ref.shape[2] + MARGIN, LANES)
        lane = lax.broadcasted_iota(jnp.int32, shape, 1)
        firsts = jnp.zeros(shape, jnp.float32)
        lasts = jnp.zeros(shape, jnp.float32)
        for field, layer, high, low, offset in table:
            left, right = slice(0, LANES), slice(ref.shape[3] - LANES, ref.shape[3])
            first, last = (
                jnp.concatenate([ref[field, layer, :, s], edge[field, layer, :, s]], axis=0)
                for s in (left, right)
            )
            first = pltpu.roll(first, offset, 1) if offset else first
            last = pltpu.roll(last, (offset + low) % LANES, 1)
            firsts = jnp.where((lane >= offset) & (lane < offset + high), first, firsts)
            lasts = jnp.where((lane >= offset) & (lane < offset + low), last, lasts)
        packed.append((firsts, lasts))
    height = fine.shape[2] + MARGIN
    even_y = lax.rem(lax.axis_index("gy"), 2) == 0

    @pl.when(even_y)
    def _():
        for at, (firsts, lasts) in zip((slice(0, height), slice(height, None)), packed):
            to_even[at, :] = lasts
            to_odd[at, :] = firsts

    @pl.when(jnp.logical_not(even_y))
    def _():
        for at, (firsts, lasts) in zip((slice(0, height), slice(height, None)), packed):
            to_even[at, :] = firsts
            to_odd[at, :] = lasts


def ahead(value, axis):
    return pltpu.roll(value, value.shape[axis] - 1, axis)


def behind(value, axis):
    return value - pltpu.roll(value, 1, axis)


def stress_of(here, below, medium, stretched):
    rigidity, lame = medium[0], medium[1]
    dx = [ahead(f, 0) - f for f in here]
    dy = [ahead(f, 1) - f for f in here]
    dz = [b - f for b, f in zip(below, here)]
    if stretched:
        dz = [f * medium[2] for f in dz]
    trace = lame * (dx[0] + dy[1] + dz[2])
    double = rigidity + rigidity
    return (
        trace + double * dx[0],
        trace + double * dy[1],
        trace + double * dz[2],
        rigidity * (dy[0] + dx[1]),
        rigidity * (dz[0] + dx[2]),
        rigidity * (dz[1] + dy[2]),
    )


def force_of(stress, above, outward):
    nx, ny, nz, xy, xz, yz = stress
    up = [xz, yz, nz]
    if above is not None:
        up = [f - a for f, a in zip(up, (above[4], above[5], above[2]))]
    if outward is not None:
        up = [f * outward for f in up]
    return (
        behind(nx, 0) + behind(xy, 1) + up[0],
        behind(xy, 0) + behind(ny, 1) + up[1],
        behind(xz, 0) + behind(yz, 1) + up[2],
    )


def bf16_parts(value):
    parts = []
    for _ in range(3):
        part = value.astype(jnp.bfloat16)
        parts.append(part)
        value = value - part.astype(jnp.float32)
    return parts


def select_lanes(planes, matrix):
    rows = planes[0].shape[0]
    parts = bf16_parts(jnp.concatenate(planes, axis=0))
    product = jnp.dot(
        jnp.concatenate(parts, axis=0), matrix, preferred_element_type=jnp.float32
    )
    size = rows * len(planes)
    total = product[:size] + product[size : 2 * size] + product[2 * size :]
    return [total[k * rows : (k + 1) * rows] for k in range(len(planes))]


def select_rows(matrix, planes):
    lanes = planes[0].shape[1]
    parts = bf16_parts(jnp.concatenate(planes, axis=1))
    product = jnp.dot(
        jnp.concatenate([matrix] * 3, axis=1),
        jnp.concatenate(parts, axis=0),
        preferred_element_type=jnp.float32,
    )
    return [product[:, k * lanes : (k + 1) * lanes] for k in range(len(planes))]


def bf16_mask(condition):
    return jnp.where(condition, 1.0, 0.0).astype(jnp.bfloat16)


class Grids:
    def __init__(self, height, cheight, lanes, clanes, lane_of):
        def pairs(shape, fine_axis, size_of):
            f = lax.broadcasted_iota(jnp.int32, shape, fine_axis)
            c = lax.broadcasted_iota(jnp.int32, shape, 1 - fine_axis)
            return bf16_mask(size_of(f) == c)

        def row_of(f):
            turn = height - MARGIN // 2
            return jnp.right_shift(jnp.where(f < turn, f, f - height + 2 * cheight), 1)

        self.up_rows = pairs((height, cheight), 0, row_of)
        self.down_rows = pairs((cheight, height), 1, row_of)
        self.up_lanes = pairs((clanes, lanes), 1, lane_of)
        self.down_lanes = pairs((lanes, clanes), 0, lane_of)

    def prolong(self, planes):
        return select_rows(self.up_rows, select_lanes(planes, self.up_lanes))

    def restrict(self, planes):
        planes = select_lanes(select_rows(self.down_rows, planes), self.down_lanes)
        return [0.25 * plane for plane in planes]


def row_index(height, shape):
    index = lax.broadcasted_iota(jnp.int32, shape, 0)
    return jnp.where(index < height - MARGIN // 2, index, index - height)


def two_steps(dev, layers, clayers, fine, coarse, grids, keep_f, keep_c, state_f, state_c, out_f, out_c):
    depth, cdepth = 2 * layers, 2 * clayers
    scale = jnp.float32(time_step * time_step)
    three = range(3)
    ghost_f = grids.prolong([coarse(k, 0) for k in three])
    ghost_c = grids.restrict([fine(k, depth - 1) for k in three])

    def solver(plane, medium, ghost_above, ghost_below, last, stretched, first_layer):
        known = {}

        def here(g):
            if g < 0:
                return ghost_above
            if g == last + 1:
                return ghost_below
            return [plane(k, g) for k in three]

        def stress(g):
            if g < first_layer:
                return None
            if g not in known:
                top = max(g, 0)
                known[g] = stress_of(
                    here(g), here(g + 1), [medium(k, top) for k in (MU, LAM, W)[: 3 if stretched else 2]], stretched
                )
            return known[g]

        return stress

    zero_c = [jnp.zeros_like(ghost_c[0])] * 3
    stress_f = solver(fine, fine, None, ghost_f, depth - 1, True, 0)
    stress_c = solver(coarse, coarse, ghost_c, zero_c, cdepth - 1, False, -1)
    own = range(dev * layers, (dev + 1) * layers)
    cown = range(dev * clayers, (dev + 1) * clayers)
    near = sorted({max(own[0] - 1, 0), *own, min(own[-1] + 1, depth - 1)} | ({depth - 1} if dev == 0 else set()))
    cnear = sorted({0, max(cown[0] - 1, 0), *cown, min(cown[-1] + 1, cdepth - 1)})
    for g in near:
        force = force_of(stress_f(g), stress_f(g - 1), fine(W, g))
        rate = scale / fine(RHO, g)
        for k in three:
            u = fine(k, g)
            state_f[k, g] = jnp.where(keep_f(g), u + u - fine(Q + k, g) + force[k] * rate, 0.0)
    for g in cnear:
        force = force_of(stress_c(g), stress_c(g - 1), None)
        rate = (0.25 * scale) / coarse(RHO, g)
        for k in three:
            v = coarse(k, g)
            state_c[k, g] = jnp.where(keep_c, v + v - coarse(Q + k, g) + force[k] * rate, 0.0)

    ghost_f = ghost_c = None
    if dev == 1:
        ghost_f = grids.prolong([state_c[k, 0] for k in three])
    else:
        ghost_c = grids.restrict([state_f[k, depth - 1] for k in three])
    stress_f = solver(lambda k, g: state_f[k, g], fine, None, ghost_f, depth - 1, True, 0)
    stress_c = solver(lambda k, g: state_c[k, g], coarse, ghost_c, zero_c, cdepth - 1, False, -1)
    for l, g in enumerate(own):
        force = force_of(stress_f(g), stress_f(g - 1), fine(W, g))
        rate = scale / fine(RHO, g)
        for k in three:
            u = state_f[k, g]
            out_f(k, l, u + u - fine(k, g) + force[k] * rate)
    for l, g in enumerate(cown):
        force = force_of(stress_c(g), stress_c(g - 1), None)
        rate = (0.25 * scale) / coarse(RHO, g)
        for k in three:
            v = state_c[k, g]
            out_c(k, l, v + v - coarse(k, g) + force[k] * rate)


def for_each_core(body):
    dev = lax.axis_index("dev")

    @pl.when(dev == 0)
    def _():
        body(0)

    @pl.when(dev != 0)
    def _():
        body(1)


def inside(index, axis, size):
    at = index + lax.axis_index(axis) * size
    return (at >= 0) & (at < lax.axis_size(axis) * size)


def main_kernel(
    own_f, own_c, far_f, far_c, own_fh, own_ch, far_fh, far_ch, out_f, out_c, strip_f, strip_c, state_f, state_c
):
    layers, n, width = own_f.shape[1:]
    clayers, nc, cwidth = own_c.shape[1:]
    height, cheight = n + MARGIN, nc + MARGIN
    fx = row_index(height, (height, width))
    cx = row_index(cheight, (cheight, cwidth))
    rows_f = inside(fx, "gx", n) & (fx >= -1)
    keep_c = inside(cx, "gx", nc) & (cx >= -1) & (cx <= nc)
    grids = Grids(height, cheight, width, cwidth, lambda f: jnp.right_shift(f, 1))

    def body(dev):
        def reader(own, far, own_halo, far_halo, count):
            def read(field, g, lanes=slice(None)):
                mine = g // count == dev
                ref, edge = (own, own_halo) if mine else (far, far_halo)
                return jnp.concatenate(
                    [ref[field, g % count, :, lanes], edge[field, g % count, :, lanes]], axis=0
                )

            return read

        fine = reader(own_f, far_f, own_fh, far_fh, layers)
        coarse = reader(own_c, far_c, own_ch, far_ch, clayers)

        def store_f(k, l, value):
            out_f[k, l] = value[:n]

        def store_c(k, l, value):
            out_c[k, l] = value[:nc]

        two_steps(
            dev, layers, clayers, fine, coarse, grids,
            lambda g: rows_f & (fx <= n + (g == 2 * layers - 1)), keep_c,
            state_f, state_c, store_f, store_c,
        )
        for read, strip, fields, count, room in (
            (fine, strip_f, FINE_FIELDS, layers, 4),
            (coarse, strip_c, COARSE_FIELDS, clayers, 2),
        ):
            lane = lax.broadcasted_iota(jnp.int32, strip.shape[2:], 1)
            wide = own_f.shape[3] if room == 4 else own_c.shape[3]
            for field in range(fields):
                for g in strip_layers(dev, count, room == 4):
                    left = pltpu.roll(read(field, g, slice(0, LANES)), room, 1)
                    right = pltpu.roll(
                        read(field, g, slice(wide - LANES, wide)), LANES - room, 1
                    )
                    strip[field, g] = jnp.where(lane < LANES // 2, left, right)

    for_each_core(body)


def strip_layers(dev, count, fine):
    depth = 2 * count
    if fine:
        return range(depth) if dev == 0 else range(count - 2, depth)
    if dev == 0:
        return range(count + 2)
    return [0, 1, *range(count - 2, depth)]


def strip_kernel(
    strip_f, strip_c, main_f, main_c, own_ye, own_yo, far_ye, far_yo, out_f, out_c, fs, cs, state_f, state_c
):
    layers, n, width = main_f.shape[1:]
    clayers, nc, cwidth = main_c.shape[1:]
    height, cheight = n + MARGIN, nc + MARGIN
    fine_table, _, coarse_table, _ = tables(layers, clayers)
    middle = LANES // 2
    fx = row_index(height, (height, LANES))
    cx = row_index(cheight, (cheight, LANES))
    lane_f = lax.broadcasted_iota(jnp.int32, (height, LANES), 1)
    lane_c = lax.broadcasted_iota(jnp.int32, (cheight, LANES), 1)
    fy = jnp.where(lane_f < middle, lane_f - 4, lane_f - LANES + 4 + width)
    cy = jnp.where(lane_c < middle, lane_c - 2, lane_c - LANES + 2 + cwidth)
    base_f = inside(fx, "gx", n) & inside(fy, "gy", width) & (fx >= -1) & (fy >= -1)
    keep_c = (
        inside(cx, "gx", nc) & inside(cy, "gy", cwidth)
        & (cx >= -1) & (cx <= nc) & (cy >= -1) & (cy <= cwidth)
    )
    grids = Grids(
        height, cheight, LANES, LANES,
        lambda f: jnp.right_shift(f, 1) + jnp.where(f < middle, 0, middle),
    )
    even = lax.rem(lax.axis_index("gy"), 2) == 0

    def body(dev):
        for table, src, dst, top, count, room, lane in (
            (fine_table, strip_f, fs, 0, layers, 4, lane_f),
            (coarse_table, strip_c, cs, height, clayers, 2, lane_c),
        ):
            rows = src.shape[2]
            for near in (True, False):
                e, o = (own_ye, own_yo) if near else (far_ye, far_yo)
                e, o = e[top : top + rows, :], o[top : top + rows, :]
                highs, lows = jnp.where(even, e, o), jnp.where(even, o, e)
                for field, layer, high, low, offset in table:
                    g = (dev if near else 1 - dev) * count + layer
                    if g not in strip_layers(dev, count, room == 4):
                        continue
                    start = LANES - room
                    value = src[field, g]
                    value = jnp.where(
                        (lane >= start) & (lane < start + high),
                        pltpu.roll(highs, (start - offset) % LANES, 1), value,
                    )
                    start = room - low
                    value = jnp.where(
                        (lane >= start) & (lane < start + low),
                        pltpu.roll(lows, (start - offset) % LANES, 1), value,
                    )
                    dst[field, g] = value

        def put(out, main, k, l, value, cells, room):
            wide = out.shape[3]
            lane = lax.broadcasted_iota(jnp.int32, (cells, LANES), 1)
            first = pltpu.roll(value[:cells], LANES - room, 1)
            last = pltpu.roll(value[:cells], room, 1)
            for start in range(0, wide, LANES):
                part = main[k, l, :, start : start + LANES]
                if start == 0:
                    part = jnp.where(lane < room, first, part)
                if start == wide - LANES:
                    part = jnp.where(lane >= LANES - room, last, part)
                out[k, l, :, start : start + LANES] = part

        two_steps(
            dev, layers, clayers,
            lambda field, g: fs[field, g], lambda field, g: cs[field, g], grids,
            lambda g: base_f & (fx <= n + (g == 2 * layers - 1)) & (fy <= width + (g == 2 * layers - 1)),
            keep_c, state_f, state_c,
            lambda k, l, value: put(out_f, main_f, k, l, value, n, 4),
            lambda k, l, value: put(out_c, main_c, k, l, value, nc, 2),
        )

    for_each_core(body)


def partners(count, parity):
    pairs = [(i, ((i + parity) ^ 1) - parity) for i in range(count)]
    return [(i, j) for i, j in pairs if 0 <= j < count]


def swap(value, axis, parity):
    return lax.ppermute(value, axis, partners(lax.axis_size(axis), parity))


def call(kernel, out_shape, operands, scratch=(), flops=0, space=pltpu.VMEM, limit=24):
    size = sum(o.size for o in out_shape) * 4
    call = pl.pallas_call(
        kernel,
        out_shape=out_shape,
        in_specs=[pl.BlockSpec(memory_space=space)] * len(operands),
        out_specs=[pl.BlockSpec(memory_space=pltpu.VMEM)] * len(out_shape),
        scratch_shapes=list(scratch),
        cost_estimate=pl.CostEstimate(flops=flops, bytes_accessed=size, transcendentals=0),
        compiler_params=pltpu.CompilerParams(vmem_limit_bytes=limit * 1024 * 1024),
    )
    if space == pltpu.HBM:
        operands = [pltpu.with_memory_space_constraint(o, space) for o in operands]
    return call(*operands)


def shape(*dims):
    return jax.ShapeDtypeStruct(dims, jnp.float32)


def per_device(*inputs):
    _, layers, n, width = inputs[0].shape
    _, clayers, nc, cwidth = inputs[3].shape
    _, fine_rows, _, coarse_rows = tables(layers, clayers)
    rows = (width // LANES) * fine_rows + (cwidth // LANES) * coarse_rows
    height, cheight = n + MARGIN, nc + MARGIN

    edge = shape(rows, LANES)
    own_f, own_c, to_even, to_odd = call(
        pack_x_kernel,
        (shape(FINE_FIELDS, layers, n, width), shape(COARSE_FIELDS, clayers, nc, cwidth), edge, edge),
        inputs,
        scratch=(pltpu.SemaphoreType.DMA((6,)),),
        space=pltpu.HBM,
        limit=24,
    )
    got_odd = swap(to_odd, "gx", 1)
    got_even = swap(to_even, "gx", 0)
    far_f, far_c = swap(own_f, "dev", 0), swap(own_c, "dev", 0)

    side = shape(height + cheight, LANES)
    own_fh, own_ch, to_even, to_odd = call(
        pack_y_kernel,
        (
            shape(FINE_FIELDS, layers, MARGIN, width),
            shape(COARSE_FIELDS, clayers, MARGIN, cwidth),
            side,
            side,
        ),
        (own_f, own_c, got_even, got_odd),
    )
    own_yo = swap(to_odd, "gy", 1)
    own_ye = swap(to_even, "gy", 0)
    far_fh, far_ch = swap(own_fh, "dev", 0), swap(own_ch, "dev", 0)

    def states(lanes, clanes):
        return (
            pltpu.VMEM((3, 2 * layers, height, lanes), jnp.float32),
            pltpu.VMEM((3, 2 * clayers, cheight, clanes), jnp.float32),
        )

    results = (shape(*inputs[0].shape), shape(*inputs[3].shape))
    strips = (
        (FINE_FIELDS, 2 * layers, height, LANES),
        (COARSE_FIELDS, 2 * clayers, cheight, LANES),
    )
    main_f, main_c, strip_f, strip_c = call(
        main_kernel,
        results + tuple(shape(*dims) for dims in strips),
        (own_f, own_c, far_f, far_c, own_fh, own_ch, far_fh, far_ch),
        scratch=states(width, cwidth),
        flops=MAIN_FLOPS,
    )
    far_yo, far_ye = swap(own_yo, "dev", 0), swap(own_ye, "dev", 0)
    return call(
        strip_kernel,
        results,
        (strip_f, strip_c, main_f, main_c, own_ye, own_yo, far_ye, far_yo),
        scratch=tuple(pltpu.VMEM(dims, jnp.float32) for dims in strips) + states(LANES, LANES),
    )


MAIN_FLOPS = 4_000_000


def solution(mesh):
    spec = P(None, "dev", "gx", "gy")

    return jax.shard_map(
        per_device,
        mesh=mesh,
        in_specs=(spec,) * 6,
        out_specs=(spec, spec),
        check_vma=False,
    )
```

time: 40.2 us -> 31 us (0.77)
  Pallas kernels: 15 us -> 9.18 us
  local copies, waits for them, and re-layouts: 5.47 us -> 0 us
  waiting for transfers between devices: 7.4 us -> 9.34 us
    pallas_call x3 -> x4, Pallas kernels: 15 us -> 9.18 us  [call(): return call(*operands)]
    unnamed x12 -> x0, local copies, waits for them, and re-layouts: 5.47 us -> none
    ppermute x8 -> x10, waiting for transfers between devices: 7.4 us -> 9.34 us  [swap(): return lax.ppermute(value, axis, partners(lax.axis_size(axis), parity))]
    ppermute x8 -> x10, starting transfers between devices: 11.4 us -> 11.6 us  [swap(): return lax.ppermute(value, axis, partners(lax.axis_size(axis), parity))]
  transfers between devices with their start and end apart: 8 -> 10, of which waited for: 4 -> 4; matrix products, arithmetic and copies ran while one was open for 0% -> 0% of each run, Pallas kernels for 0% -> 13%
where the time goes in v2:
time: 31 us; the launch traced here: 30.8 us
  starting transfers between devices  11.6 us (37%)
  waiting for transfers between devices  9.34 us (30%)
  Pallas kernels  9.18 us (30%)
  between operations  0.71 us (2%)
    ppermute x10, starting transfers between devices, swap(): return lax.ppermute(value, axis, partners(lax.axis_size(axis), parity))  11.6 us
    ppermute x10, waiting for transfers between devices, swap(): return lax.ppermute(value, axis, partners(lax.axis_size(axis), parity))  9.34 us
    pallas_call x4, Pallas kernels, call(): return call(*operands)  9.18 us
  transfers between devices with their start and end apart: 10, of which 4 were waited for; matrix products, arithmetic and copies ran while one was open for 0% of the time, Pallas kernels for 13%

profile of v2, /device:TPU:21, one launch (start us, length us, event | category | flops | bytes accessed | tf_op | source)
XLA Modules:
  0.0 30.8 jit_solution(17722611275617766081)
XLA Ops:
  0.6 1.4 %shard_map.77 = (f32[10,4,16,256]{3,2,1,0:T(8,128)S(1)}, f32[9,8,8,128]{3,2,1,0:T(8,128)S(1)}, f32[272,128]{1,0:T(8,128)S(1)}, f32[272,128]{1,0:T(8,128)S(1)}) custom-call(f32[3,4,16,256]{3,2,1,0:T(8,128)} %fu.1, f32[3,4,16,256]{3,2,1,0:T(8,128)} %fp.1, f32[4,4,16,256]{3,2,1,0:T(8,128)} %fm.1, f32[3,8,8,128]{3,2,1,0:T(8,128)} %cu.1, f32[3,8,8,128]{3,2,1,0:T(8,128)} %cp.1, ...), custom_call_target="tpu_custom_call" | custom-call | bytes 1228800 | tf_op jit(solution)/shard_map/pallas_call | solution.py:522
  2.0 0.7 %collective-permute-start = (f32[10,4,16,256]{3,2,1,0:T(8,128)S(1)}, f32[10,4,16,256]{3,2,1,0:T(8,128)S(1)}, u32[]{:S(2)}, u32[]{:S(2)}) collective-permute-start(f32[10,4,16,256]{3,2,1,0:T(8,128)S(1)} %get-tuple-element.14.fine.own_f), channel_id=1, source_target_pairs={{0,1},{1,0},{2,3},{3,2},{4,5},{5,4},{6,7},{7,6},{8,9},{9,8},{10,11... | collective-permute-start | bytes 1966088 | tf_op jit(solution)/shard_map/ppermute | solution.py:506
  2.8 1.2 %collective-permute-start.2 = (f32[272,128]{1,0:T(8,128)S(1)}, f32[272,128]{1,0:T(8,128)S(1)}, u32[]{:S(2)}, u32[]{:S(2)}) collective-permute-start(f32[272,128]{1,0:T(8,128)S(1)} %get-tuple-element.16), channel_id=1, source_target_pairs={{0,8},{8,0},{16,24},{24,16},{1,9},{9,1},{17,25},{25,17},{2,10},{10... | collective-permute-start | bytes 417800 | tf_op jit(solution)/shard_map/ppermute | solution.py:506
  4.0 2.1 %collective-permute-start.3 = (f32[272,128]{1,0:T(8,128)S(1)}, f32[272,128]{1,0:T(8,128)S(1)}, u32[]{:S(2)}, u32[]{:S(2)}) collective-permute-start(f32[272,128]{1,0:T(8,128)S(1)} %get-tuple-element.17), channel_id=1, source_target_pairs={{8,16},{16,8},{9,17},{17,9},{10,18},{18,10},{11,19},{19,11},{12,20... | collective-permute-start | bytes 417800 | tf_op jit(solution)/shard_map/ppermute | solution.py:506
  6.1 1.8 %collective-permute-done.2.got_even = f32[272,128]{1,0:T(8,128)S(1)} collective-permute-done((f32[272,128]{1,0:T(8,128)S(1)}, f32[272,128]{1,0:T(8,128)S(1)}, u32[]{:S(2)}, u32[]{:S(2)}) %collective-permute-start.2) | collective-permute-done | bytes 139296 | tf_op jit(solution)/shard_map/ppermute | solution.py:506
  7.9 3.7 %collective-permute-done.3.got_odd = f32[272,128]{1,0:T(8,128)S(1)} collective-permute-done((f32[272,128]{1,0:T(8,128)S(1)}, f32[272,128]{1,0:T(8,128)S(1)}, u32[]{:S(2)}, u32[]{:S(2)}) %collective-permute-start.3) | collective-permute-done | bytes 139296 | tf_op jit(solution)/shard_map/ppermute | solution.py:506
  11.6 0.8 %shard_map.78 = (f32[10,4,8,256]{3,2,1,0:T(8,128)S(1)}, f32[9,8,8,128]{3,2,1,0:T(8,128)S(1)}, f32[40,128]{1,0:T(8,128)S(1)}, f32[40,128]{1,0:T(8,128)S(1)}) custom-call(f32[10,4,16,256]{3,2,1,0:T(8,128)S(1)} %get-tuple-element.14.fine.own_f, f32[9,8,8,128]{3,2,1,0:T(8,128)S(1)} %get-tuple-element.15.coarse.own_c, ...), custom_call_target="tpu_custom_call" | custom-call | bytes 663552 | tf_op jit(solution)/shard_map/pallas_call | solution.py:522
  12.4 1.3 %collective-permute-start.4 = (f32[10,4,8,256]{3,2,1,0:T(8,128)S(1)}, f32[10,4,8,256]{3,2,1,0:T(8,128)S(1)}, u32[]{:S(2)}, u32[]{:S(2)}) collective-permute-start(f32[10,4,8,256]{3,2,1,0:T(8,128)S(1)} %get-tuple-element.18.own_fh), channel_id=1, source_target_pairs={{0,1},{1,0},{2,3},{3,2},{4,5},{5,4},{6,7},{7,6},{8,9},{9,8},{10,11... | collective-permute-start | bytes 983048 | tf_op jit(solution)/shard_map/ppermute | solution.py:506
  13.7 0.1 collective-permute-start.1
  13.8 0.4 %collective-permute-start.5 = (f32[9,8,8,128]{3,2,1,0:T(8,128)S(1)}, f32[9,8,8,128]{3,2,1,0:T(8,128)S(1)}, u32[]{:S(2)}, u32[]{:S(2)}) collective-permute-start(f32[9,8,8,128]{3,2,1,0:T(8,128)S(1)} %get-tuple-element.19.own_ch), channel_id=1, source_target_pairs={{0,1},{1,0},{2,3},{3,2},{4,5},{5,4},{6,7},{7,6},{8,9},{9,8},{10,11... | collective-permute-start | bytes 884744 | tf_op jit(solution)/shard_map/ppermute | solution.py:506
  14.2 1.3 %collective-permute-start.6 = (f32[40,128]{1,0:T(8,128)S(1)}, f32[40,128]{1,0:T(8,128)S(1)}, u32[]{:S(2)}, u32[]{:S(2)}) collective-permute-start(f32[40,128]{1,0:T(8,128)S(1)} %get-tuple-element.24), channel_id=1, source_target_pairs={{0,2},{2,0},{4,6},{6,4},{1,3},{3,1},{5,7},{7,5},{8,10},{10,8},{12,... | collective-permute-start | bytes 61448 | tf_op jit(solution)/shard_map/ppermute | solution.py:506
  15.5 1.3 %collective-permute-done.6.own_ye = f32[40,128]{1,0:T(8,128)S(1)} collective-permute-done((f32[40,128]{1,0:T(8,128)S(1)}, f32[40,128]{1,0:T(8,128)S(1)}, u32[]{:S(2)}, u32[]{:S(2)}) %collective-permute-start.6) | collective-permute-done | bytes 20512 | tf_op jit(solution)/shard_map/ppermute | solution.py:506
  16.9 2.1 %collective-permute-start.7 = (f32[40,128]{1,0:T(8,128)S(1)}, f32[40,128]{1,0:T(8,128)S(1)}, u32[]{:S(2)}, u32[]{:S(2)}) collective-permute-start(f32[40,128]{1,0:T(8,128)S(1)} %get-tuple-element.25), channel_id=1, source_target_pairs={{2,4},{4,2},{3,5},{5,3},{10,12},{12,10},{11,13},{13,11},{18,20},{2... | collective-permute-start | bytes 61448 | tf_op jit(solution)/shard_map/ppermute | solution.py:506
  18.9 2.4 %collective-permute-done.7.own_yo = f32[40,128]{1,0:T(8,128)S(1)} collective-permute-done((f32[40,128]{1,0:T(8,128)S(1)}, f32[40,128]{1,0:T(8,128)S(1)}, u32[]{:S(2)}, u32[]{:S(2)}) %collective-permute-start.7) | collective-permute-done | bytes 20512 | tf_op jit(solution)/shard_map/ppermute | solution.py:506
  21.4 2.4 %collective-permute-start.8 = (f32[40,128]{1,0:T(8,128)S(1)}, f32[40,128]{1,0:T(8,128)S(1)}, u32[]{:S(2)}, u32[]{:S(2)}) collective-permute-start(f32[40,128]{1,0:T(8,128)S(1)} %collective-permute-done.6.own_ye), channel_id=1, source_target_pairs={{0,1},{1,0},{2,3},{3,2},{4,5},{5,4},{6,7},{7,6},{8,9},{9,8},{10,11... | collective-permute-start | bytes 61448 | tf_op jit(solution)/shard_map/ppermute | solution.py:506
  23.8 0.0 collective-permute-done.1.far_c
  23.8 0.0 collective-permute-start.9
  23.8 0.0 collective-permute-done.5.far_ch
  23.8 0.0 collective-permute-done.4.far_fh
  23.8 0.0 collective-permute-done.far_f
  23.8 3.3 %shard_map.79 = (f32[3,4,16,256]{3,2,1,0:T(8,128)S(1)}, f32[3,8,8,128]{3,2,1,0:T(8,128)S(1)}, f32[10,8,24,128]{3,2,1,0:T(8,128)S(1)}, f32[9,16,16,128]{3,2,1,0:T(8,128)S(1)}) custom-call(f32[10,4,16,256]{3,2,1,0:T(8,128)S(1)} %get-tuple-element.14.fine.own_f, f32[9,8,8,128]{3,2,1,0:T(8,128)S(1)} %get-tuple-element.15.coarse.own_c, ...), custom_call_target="tpu_custom_call" | custom-call | flops 4000000 | bytes 2457600 | tf_op jit(solution)/shard_map/pallas_call | solution.py:522
  27.0 0.0 collective-permute-done.8.far_ye
  27.1 0.0 collective-permute-done.9.far_yo
  27.1 3.7 %shard_map.80 = (f32[3,4,16,256]{3,2,1,0:T(8,128)}, f32[3,8,8,128]{3,2,1,0:T(8,128)}) custom-call(f32[10,8,24,128]{3,2,1,0:T(8,128)S(1)} %get-tuple-element.20.strip_f, f32[9,16,16,128]{3,2,1,0:T(8,128)S(1)} %get-tuple-element.21.strip_c, f32[3,4,16,256]{3,2,1,0:T(8,128)S(1)} %get-tuple-element.22.main_f, f32[3,8,8,128]{3,2,1,0:T(8,128)S(1)} %get-tuple-element.23.main_c, ...), custom_call_target="tpu_custom_call" | custom-call | bytes 294912 | tf_op jit(solution)/shard_map/pallas_call | solution.py:522
Async XLA Ops:
  2.0 21.8 %collective-permute-start = (f32[10,4,16,256]{3,2,1,0:T(8,128)S(1)}, f32[10,4,16,256]{3,2,1,0:T(8,128)S(1)}, u32[]{:S(2)}, u32[]{:S(2)}) collective-permute-start(f32[10,4,16,256]{3,2,1,0:T(8,128)S(1)} %get-tuple-element.14.fine.own_f), channel_id=1, source_target_pairs={{0,1},{1,0},{2,3},{3,2},{4,5},{5,4},{6,7},{7,6},{8,9},{9,8},{10,11... | collective-permute-start | bytes 1966088 | tf_op jit(solution)/shard_map/ppermute | solution.py:506
  2.8 5.2 %collective-permute-start.2 = (f32[272,128]{1,0:T(8,128)S(1)}, f32[272,128]{1,0:T(8,128)S(1)}, u32[]{:S(2)}, u32[]{:S(2)}) collective-permute-start(f32[272,128]{1,0:T(8,128)S(1)} %get-tuple-element.16), channel_id=1, source_target_pairs={{0,8},{8,0},{16,24},{24,16},{1,9},{9,1},{17,25},{25,17},{2,10},{10... | collective-permute-start | bytes 417800 | tf_op jit(solution)/shard_map/ppermute | solution.py:506
  4.0 7.7 %collective-permute-start.3 = (f32[272,128]{1,0:T(8,128)S(1)}, f32[272,128]{1,0:T(8,128)S(1)}, u32[]{:S(2)}, u32[]{:S(2)}) collective-permute-start(f32[272,128]{1,0:T(8,128)S(1)} %get-tuple-element.17), channel_id=1, source_target_pairs={{8,16},{16,8},{9,17},{17,9},{10,18},{18,10},{11,19},{19,11},{12,20... | collective-permute-start | bytes 417800 | tf_op jit(solution)/shard_map/ppermute | solution.py:506
  12.4 11.3 %collective-permute-start.4 = (f32[10,4,8,256]{3,2,1,0:T(8,128)S(1)}, f32[10,4,8,256]{3,2,1,0:T(8,128)S(1)}, u32[]{:S(2)}, u32[]{:S(2)}) collective-permute-start(f32[10,4,8,256]{3,2,1,0:T(8,128)S(1)} %get-tuple-element.18.own_fh), channel_id=1, source_target_pairs={{0,1},{1,0},{2,3},{3,2},{4,5},{5,4},{6,7},{7,6},{8,9},{9,8},{10,11... | collective-permute-start | bytes 983048 | tf_op jit(solution)/shard_map/ppermute | solution.py:506
  13.7 10.0 %collective-permute-start.1 = (f32[9,8,8,128]{3,2,1,0:T(8,128)S(1)}, f32[9,8,8,128]{3,2,1,0:T(8,128)S(1)}, u32[]{:S(2)}, u32[]{:S(2)}) collective-permute-start(f32[9,8,8,128]{3,2,1,0:T(8,128)S(1)} %get-tuple-element.15.coarse.own_c), channel_id=1, source_target_pairs={{0,1},{1,0},{2,3},{3,2},{4,5},{5,4},{6,7},{7,6},{8,9},{9,8},{10,11... | collective-permute-start | bytes 884744 | tf_op jit(solution)/shard_map/ppermute | solution.py:506
  13.8 10.0 %collective-permute-start.5 = (f32[9,8,8,128]{3,2,1,0:T(8,128)S(1)}, f32[9,8,8,128]{3,2,1,0:T(8,128)S(1)}, u32[]{:S(2)}, u32[]{:S(2)}) collective-permute-start(f32[9,8,8,128]{3,2,1,0:T(8,128)S(1)} %get-tuple-element.19.own_ch), channel_id=1, source_target_pairs={{0,1},{1,0},{2,3},{3,2},{4,5},{5,4},{6,7},{7,6},{8,9},{9,8},{10,11... | collective-permute-start | bytes 884744 | tf_op jit(solution)/shard_map/ppermute | solution.py:506
  14.2 2.6 %collective-permute-start.6 = (f32[40,128]{1,0:T(8,128)S(1)}, f32[40,128]{1,0:T(8,128)S(1)}, u32[]{:S(2)}, u32[]{:S(2)}) collective-permute-start(f32[40,128]{1,0:T(8,128)S(1)} %get-tuple-element.24), channel_id=1, source_target_pairs={{0,2},{2,0},{4,6},{6,4},{1,3},{3,1},{5,7},{7,5},{8,10},{10,8},{12,... | collective-permute-start | bytes 61448 | tf_op jit(solution)/shard_map/ppermute | solution.py:506
  16.9 4.5 %collective-permute-start.7 = (f32[40,128]{1,0:T(8,128)S(1)}, f32[40,128]{1,0:T(8,128)S(1)}, u32[]{:S(2)}, u32[]{:S(2)}) collective-permute-start(f32[40,128]{1,0:T(8,128)S(1)} %get-tuple-element.25), channel_id=1, source_target_pairs={{2,4},{4,2},{3,5},{5,3},{10,12},{12,10},{11,13},{13,11},{18,20},{2... | collective-permute-start | bytes 61448 | tf_op jit(solution)/shard_map/ppermute | solution.py:506
  21.4 5.7 %collective-permute-start.8 = (f32[40,128]{1,0:T(8,128)S(1)}, f32[40,128]{1,0:T(8,128)S(1)}, u32[]{:S(2)}, u32[]{:S(2)}) collective-permute-start(f32[40,128]{1,0:T(8,128)S(1)} %collective-permute-done.6.own_ye), channel_id=1, source_target_pairs={{0,1},{1,0},{2,3},{3,2},{4,5},{5,4},{6,7},{7,6},{8,9},{9,8},{10,11... | collective-permute-start | bytes 61448 | tf_op jit(solution)/shard_map/ppermute | solution.py:506
  23.8 3.3 %collective-permute-start.9 = (f32[40,128]{1,0:T(8,128)S(1)}, f32[40,128]{1,0:T(8,128)S(1)}, u32[]{:S(2)}, u32[]{:S(2)}) collective-permute-start(f32[40,128]{1,0:T(8,128)S(1)} %collective-permute-done.7.own_yo), channel_id=1, source_target_pairs={{0,1},{1,0},{2,3},{3,2},{4,5},{5,4},{6,7},{7,6},{8,9},{9,8},{10,11... | collective-permute-start | bytes 61448 | tf_op jit(solution)/shard_map/ppermute | solution.py:506

commit v3 on v2

--- a/solution.py
+++ b/solution.py
@@ -1,3 +1,5 @@
+import functools
+
 import jax
 import jax.numpy as jnp
 from jax import lax
@@ -45,22 +47,28 @@
 
 
 def tables(fine_layers, coarse_layers):
-    fine, fine_rows = plane_table(
+    fine, fine_lanes = plane_table(
         FINE_FIELDS, fine_layers, lambda f, l: fine_widths(f, l, fine_layers)
     )
-    coarse, coarse_rows = plane_table(COARSE_FIELDS, coarse_layers, lambda f, l: coarse_widths(f))
-    assert fine_rows <= LANES and coarse_rows <= LANES
-    return fine, round_up(fine_rows, 8), coarse, round_up(coarse_rows, 8)
-
-
-def groups_of(fine_layers, coarse_layers, fine_parts, coarse_parts):
-    fine, fine_rows, coarse, coarse_rows = tables(fine_layers, coarse_layers)
-    return (fine, 0, fine_rows, fine_parts), (
-        coarse,
-        fine_parts * fine_rows,
-        coarse_rows,
-        coarse_parts,
-    )
+    coarse, coarse_lanes = plane_table(COARSE_FIELDS, coarse_layers, lambda f, l: coarse_widths(f))
+    assert fine_lanes <= LANES and coarse_lanes <= LANES
+    return fine, coarse
+
+
+def edge_rows(tables_of_grids, parts_of_grids, first):
+    pieces, at = [], 0
+    for grid, (table, parts) in enumerate(zip(tables_of_grids, parts_of_grids)):
+        for field, layer, high, low, _ in table:
+            size = high if first else low
+            for t in range(parts):
+                pieces.append((grid, field, layer, t, size, at))
+                at += size
+    return pieces, round_up(at, 8)
+
+
+def grid_tables(fine_shape, coarse_shape):
+    fine, coarse = tables(fine_shape[1], coarse_shape[1])
+    return (fine, coarse), (fine_shape[3] // LANES, coarse_shape[3] // LANES)
 
 
 def pack_x_kernel(fu, fp, fm, cu, cp, cm, fine, coarse, to_even, to_odd, sems):
@@ -76,20 +84,15 @@
         copy.start()
     for copy in copies:
         copy.wait()
-    groups = groups_of(
-        fine.shape[1], coarse.shape[1], fine.shape[3] // LANES, coarse.shape[3] // LANES
-    )
+    grids = grid_tables(fine.shape, coarse.shape)
 
     def fill(out, first):
-        for (table, base, rows, parts), ref in zip(groups, (fine, coarse)):
-            for field, layer, high, low, offset in table:
-                size = high if first else low
-                start = 0 if first else ref.shape[2] - low
-                for t in range(parts):
-                    at = base + t * rows + offset
-                    out[at : at + size, :] = ref[
-                        field, layer, start : start + size, t * LANES : (t + 1) * LANES
-                    ]
+        for grid, field, layer, t, size, at in edge_rows(*grids, first)[0]:
+            ref = (fine, coarse)[grid]
+            start = 0 if first else ref.shape[2] - size
+            out[at : at + size, :] = ref[
+                field, layer, start : start + size, t * LANES : (t + 1) * LANES
+            ]
 
     even = lax.rem(lax.axis_index("gx"), 2) == 0
 
@@ -104,22 +107,46 @@
         fill(to_odd, False)
 
 
-def pack_y_kernel(fine, coarse, got_even, got_odd, fine_halo, coarse_halo, to_even, to_odd):
-    groups = groups_of(
-        fine.shape[1], coarse.shape[1], fine.shape[3] // LANES, coarse.shape[3] // LANES
-    )
+def edge_columns(table, read, height, width):
+    lane = lax.broadcasted_iota(jnp.int32, (height, LANES), 1)
+    firsts = jnp.zeros((height, LANES), jnp.float32)
+    lasts = jnp.zeros((height, LANES), jnp.float32)
+    for field, layer, high, low, offset in table:
+        first = read(field, layer, slice(0, LANES))
+        last = read(field, layer, slice(width - LANES, width))
+        first = pltpu.roll(first, offset, 1) if offset else first
+        last = pltpu.roll(last, (offset + low) % LANES, 1)
+        firsts = jnp.where((lane >= offset) & (lane < offset + high), first, firsts)
+        lasts = jnp.where((lane >= offset) & (lane < offset + low), last, lasts)
+    return firsts, lasts
+
+
+def pack_inner_kernel(fine, coarse, firsts_ref, lasts_ref):
+    at = 0
+    for table, ref in zip(grid_tables(fine.shape, coarse.shape)[0], (fine, coarse)):
+        rows = ref.shape[2]
+        firsts, lasts = edge_columns(
+            table, lambda field, layer, lanes: ref[field, layer, :, lanes], rows, ref.shape[3]
+        )
+        firsts_ref[at : at + rows, :] = firsts
+        lasts_ref[at : at + rows, :] = lasts
+        at += rows
+
+
+def pack_y_kernel(fine_rows, firsts_ref, lasts_ref, got_even, got_odd, fine_halo, coarse_halo, to_even, to_odd):
+    halos = (fine_halo, coarse_halo)
+    grids = grid_tables(fine_halo.shape, coarse_halo.shape)
 
     def halo(high_ref, low_ref):
-        for (table, base, rows, parts), out in zip(groups, (fine_halo, coarse_halo)):
-            for field, layer, high, low, offset in table:
-                for t in range(parts):
-                    at = base + t * rows + offset
-                    lanes = slice(t * LANES, (t + 1) * LANES)
-                    out[field, layer, :high, lanes] = high_ref[at : at + high, :]
-                    out[field, layer, MARGIN - low :, lanes] = low_ref[at : at + low, :]
-
-    for (table, *_), out in zip(groups, (fine_halo, coarse_halo)):
-        for field, layer, high, low, offset in table:
+        for first, ref in ((True, high_ref), (False, low_ref)):
+            for grid, field, layer, t, size, at in edge_rows(*grids, first)[0]:
+                start = 0 if first else MARGIN - size
+                halos[grid][field, layer, start : start + size, t * LANES : (t + 1) * LANES] = ref[
+                    at : at + size, :
+                ]
+
+    for table, out in zip(grids[0], halos):
+        for field, layer, *_ in table:
             out[field, layer] = jnp.zeros((MARGIN, out.shape[3]), jnp.float32)
 
     even = lax.rem(lax.axis_index("gx"), 2) == 0
@@ -132,37 +159,34 @@
     def _():
         halo(got_odd, got_even)
 
-    packed = []
-    for (table, *_), ref, edge in zip(groups, (fine, coarse), (fine_halo, coarse_halo)):
-        shape = (ref.shape[2] + MARGIN, LANES)
-        lane = lax.broadcasted_iota(jnp.int32, shape, 1)
-        firsts = jnp.zeros(shape, jnp.float32)
-        lasts = jnp.zeros(shape, jnp.float32)
-        for field, layer, high, low, offset in table:
-            left, right = slice(0, LANES), slice(ref.shape[3] - LANES, ref.shape[3])
-            first, last = (
-                jnp.concatenate([ref[field, layer, :, s], edge[field, layer, :, s]], axis=0)
-                for s in (left, right)
-            )
-            first = pltpu.roll(first, offset, 1) if offset else first
-            last = pltpu.roll(last, (offset + low) % LANES, 1)
-            firsts = jnp.where((lane >= offset) & (lane < offset + high), first, firsts)
-            lasts = jnp.where((lane >= offset) & (lane < offset + low), last, lasts)
-        packed.append((firsts, lasts))
-    height = fine.shape[2] + MARGIN
+    columns = [
+        edge_columns(
+            table, lambda field, layer, lanes: out[field, layer, :, lanes], MARGIN, out.shape[3]
+        )
+        for table, out in zip(grids[0], halos)
+    ]
     even_y = lax.rem(lax.axis_index("gy"), 2) == 0
 
+    def place(first_out, last_out):
+        for side, (inner, out) in enumerate(((firsts_ref, first_out), (lasts_ref, last_out))):
+            pieces = [
+                inner[:fine_rows, :],
+                columns[0][side],
+                inner[fine_rows:, :],
+                columns[1][side],
+            ]
+            at = 0
+            for piece in pieces:
+                out[at : at + piece.shape[0], :] = piece
+                at += piece.shape[0]
+
     @pl.when(even_y)
     def _():
-        for at, (firsts, lasts) in zip((slice(0, height), slice(height, None)), packed):
-            to_even[at, :] = lasts
-            to_odd[at, :] = firsts
+        place(to_odd, to_even)
 
     @pl.when(jnp.logical_not(even_y))
     def _():
-        for at, (firsts, lasts) in zip((slice(0, height), slice(height, None)), packed):
-            to_even[at, :] = firsts
-            to_odd[at, :] = lasts
+        place(to_even, to_odd)
 
 
 def ahead(value, axis):
@@ -357,8 +381,40 @@
     return (at >= 0) & (at < lax.axis_size(axis) * size)
 
 
+def reader(dev, own, far, own_halo, far_halo):
+    count = own.shape[1]
+
+    def read(field, g, lanes=slice(None)):
+        ref, edge = (own, own_halo) if g // count == dev else (far, far_halo)
+        return jnp.concatenate(
+            [ref[field, g % count, :, lanes], edge[field, g % count, :, lanes]], axis=0
+        )
+
+    return read
+
+
+def ends_kernel(own_f, own_c, far_f, far_c, own_fh, own_ch, far_fh, far_ch, strip_f, strip_c):
+    def body(dev):
+        for own, far, own_halo, far_halo, strip, fields, room in (
+            (own_f, far_f, own_fh, far_fh, strip_f, FINE_FIELDS, 4),
+            (own_c, far_c, own_ch, far_ch, strip_c, COARSE_FIELDS, 2),
+        ):
+            read = reader(dev, own, far, own_halo, far_halo)
+            wide = own.shape[3]
+            lane = lax.broadcasted_iota(jnp.int32, strip.shape[2:], 1)
+            for field in range(fields):
+                for g in strip_layers(dev, own.shape[1], room == 4):
+                    left = pltpu.roll(read(field, g, slice(0, LANES)), room, 1)
+                    right = pltpu.roll(
+                        read(field, g, slice(wide - LANES, wide)), LANES - room, 1
+                    )
+                    strip[field, g] = jnp.where(lane < LANES // 2, left, right)
+
+    for_each_core(body)
+
+
 def main_kernel(
-    own_f, own_c, far_f, far_c, own_fh, own_ch, far_fh, far_ch, out_f, out_c, strip_f, strip_c, state_f, state_c
+    own_f, own_c, far_f, far_c, own_fh, own_ch, far_fh, far_ch, out_f, out_c, state_f, state_c
 ):
     layers, n, width = own_f.shape[1:]
     clayers, nc, cwidth = own_c.shape[1:]
@@ -370,18 +426,8 @@
     grids = Grids(height, cheight, width, cwidth, lambda f: jnp.right_shift(f, 1))
 
     def body(dev):
-        def reader(own, far, own_halo, far_halo, count):
-            def read(field, g, lanes=slice(None)):
-                mine = g // count == dev
-                ref, edge = (own, own_halo) if mine else (far, far_halo)
-                return jnp.concatenate(
-                    [ref[field, g % count, :, lanes], edge[field, g % count, :, lanes]], axis=0
-                )
-
-            return read
-
-        fine = reader(own_f, far_f, own_fh, far_fh, layers)
-        coarse = reader(own_c, far_c, own_ch, far_ch, clayers)
+        fine = reader(dev, own_f, far_f, own_fh, far_fh)
+        coarse = reader(dev, own_c, far_c, own_ch, far_ch)
 
         def store_f(k, l, value):
             out_f[k, l] = value[:n]
@@ -394,19 +440,6 @@
             lambda g: rows_f & (fx <= n + (g == 2 * layers - 1)), keep_c,
             state_f, state_c, store_f, store_c,
         )
-        for read, strip, fields, count, room in (
-            (fine, strip_f, FINE_FIELDS, layers, 4),
-            (coarse, strip_c, COARSE_FIELDS, clayers, 2),
-        ):
-            lane = lax.broadcasted_iota(jnp.int32, strip.shape[2:], 1)
-            wide = own_f.shape[3] if room == 4 else own_c.shape[3]
-            for field in range(fields):
-                for g in strip_layers(dev, count, room == 4):
-                    left = pltpu.roll(read(field, g, slice(0, LANES)), room, 1)
-                    right = pltpu.roll(
-                        read(field, g, slice(wide - LANES, wide)), LANES - room, 1
-                    )
-                    strip[field, g] = jnp.where(lane < LANES // 2, left, right)
 
     for_each_core(body)
 
@@ -426,7 +459,7 @@
     layers, n, width = main_f.shape[1:]
     clayers, nc, cwidth = main_c.shape[1:]
     height, cheight = n + MARGIN, nc + MARGIN
-    fine_table, _, coarse_table, _ = tables(layers, clayers)
+    fine_table, coarse_table = tables(layers, clayers)
     middle = LANES // 2
     fx = row_index(height, (height, LANES))
     cx = row_index(cheight, (cheight, LANES))
@@ -529,8 +562,8 @@
 def per_device(*inputs):
     _, layers, n, width = inputs[0].shape
     _, clayers, nc, cwidth = inputs[3].shape
-    _, fine_rows, _, coarse_rows = tables(layers, clayers)
-    rows = (width // LANES) * fine_rows + (cwidth // LANES) * coarse_rows
+    grids = grid_tables(inputs[0].shape, inputs[3].shape)
+    rows = max(edge_rows(*grids, first)[1] for first in (True, False))
     height, cheight = n + MARGIN, nc + MARGIN
 
     edge = shape(rows, LANES)
@@ -546,16 +579,19 @@
     got_even = swap(to_even, "gx", 0)
     far_f, far_c = swap(own_f, "dev", 0), swap(own_c, "dev", 0)
 
+    inner = shape(n + nc, LANES)
+    firsts, lasts = call(pack_inner_kernel, (inner, inner), (own_f, own_c))
+
     side = shape(height + cheight, LANES)
     own_fh, own_ch, to_even, to_odd = call(
-        pack_y_kernel,
+        functools.partial(pack_y_kernel, n),
         (
             shape(FINE_FIELDS, layers, MARGIN, width),
             shape(COARSE_FIELDS, clayers, MARGIN, cwidth),
             side,
             side,
         ),
-        (own_f, own_c, got_even, got_odd),
+        (firsts, lasts, got_even, got_odd),
     )
     own_yo = swap(to_odd, "gy", 1)
     own_ye = swap(to_even, "gy", 0)
@@ -572,13 +608,11 @@
         (FINE_FIELDS, 2 * layers, height, LANES),
         (COARSE_FIELDS, 2 * clayers, cheight, LANES),
     )
-    main_f, main_c, strip_f, strip_c = call(
-        main_kernel,
-        results + tuple(shape(*dims) for dims in strips),
-        (own_f, own_c, far_f, far_c, own_fh, own_ch, far_fh, far_ch),
-        scratch=states(width, cwidth),
-        flops=MAIN_FLOPS,
-    )
+    tiles = (own_f, own_c, far_f, far_c, own_fh, own_ch, far_fh, far_ch)
+    main_f, main_c = call(
+        main_kernel, results, tiles, scratch=states(width, cwidth), flops=MAIN_FLOPS
+    )
+    strip_f, strip_c = call(ends_kernel, tuple(shape(*dims) for dims in strips), tiles)
     far_yo, far_ye = swap(own_yo, "dev", 0), swap(own_ye, "dev", 0)
     return call(
         strip_kernel,

time: 31 us -> 29.9 us (0.965)
  waiting for transfers between devices: 9.34 us -> 8.59 us
  Pallas kernels: 9.18 us -> 8.8 us
    ppermute x10, waiting for transfers between devices: 9.34 us -> 8.59 us  [swap(): return lax.ppermute(value, axis, partners(lax.axis_size(axis), parity))]
    pallas_call x4 -> x6, Pallas kernels: 9.18 us -> 8.8 us  [call(): return call(*operands)]
  transfers between devices with their start and end apart: 10 -> 10, of which waited for: 4 -> 4; matrix products, arithmetic and copies ran while one was open for 0% -> 0% of each run, Pallas kernels for 13% -> 12%
where the time goes in v3:
time: 29.9 us; the launch traced here: 29.7 us
  starting transfers between devices  11.6 us (39%)
  Pallas kernels  8.8 us (29%)
  waiting for transfers between devices  8.59 us (29%)
  between operations  0.72 us (2%)
    ppermute x10, starting transfers between devices, swap(): return lax.ppermute(value, axis, partners(lax.axis_size(axis), parity))  11.6 us
    pallas_call x6, Pallas kernels, call(): return call(*operands)  8.8 us
    ppermute x10, waiting for transfers between devices, swap(): return lax.ppermute(value, axis, partners(lax.axis_size(axis), parity))  8.59 us
  transfers between devices with their start and end apart: 10, of which 4 were waited for; matrix products, arithmetic and copies ran while one was open for 0% of the time, Pallas kernels for 12%

profile of v3, /device:TPU:21, one launch (start us, length us, event | category | flops | bytes accessed | tf_op | source)
XLA Modules:
  0.0 29.7 jit_solution(6077807064296638381)
XLA Ops:
  0.6 1.4 %shard_map.77 = (f32[10,4,16,256]{3,2,1,0:T(8,128)S(1)}, f32[9,8,8,128]{3,2,1,0:T(8,128)S(1)}, f32[240,128]{1,0:T(8,128)S(1)}, f32[240,128]{1,0:T(8,128)S(1)}) custom-call(f32[3,4,16,256]{3,2,1,0:T(8,128)} %fu.1, f32[3,4,16,256]{3,2,1,0:T(8,128)} %fp.1, f32[4,4,16,256]{3,2,1,0:T(8,128)} %fm.1, f32[3,8,8,128]{3,2,1,0:T(8,128)} %cu.1, f32[3,8,8,128]{3,2,1,0:T(8,128)} %cp.1, ...), custom_call_target="tpu_custom_call" | custom-call | bytes 1196032 | tf_op jit(solution)/shard_map/pallas_call | solution.py:555
  2.0 0.7 %collective-permute-start = (f32[10,4,16,256]{3,2,1,0:T(8,128)S(1)}, f32[10,4,16,256]{3,2,1,0:T(8,128)S(1)}, u32[]{:S(2)}, u32[]{:S(2)}) collective-permute-start(f32[10,4,16,256]{3,2,1,0:T(8,128)S(1)} %get-tuple-element.16.fine.own_f), channel_id=1, source_target_pairs={{0,1},{1,0},{2,3},{3,2},{4,5},{5,4},{6,7},{7,6},{8,9},{9,8},{10,11... | collective-permute-start | bytes 1966088 | tf_op jit(solution)/shard_map/ppermute | solution.py:539
  2.8 1.2 %collective-permute-start.2 = (f32[240,128]{1,0:T(8,128)S(1)}, f32[240,128]{1,0:T(8,128)S(1)}, u32[]{:S(2)}, u32[]{:S(2)}) collective-permute-start(f32[240,128]{1,0:T(8,128)S(1)} %get-tuple-element.20), channel_id=1, source_target_pairs={{0,8},{8,0},{16,24},{24,16},{1,9},{9,1},{17,25},{25,17},{2,10},{10... | collective-permute-start | bytes 368648 | tf_op jit(solution)/shard_map/ppermute | solution.py:539
  4.0 2.1 %collective-permute-start.3 = (f32[240,128]{1,0:T(8,128)S(1)}, f32[240,128]{1,0:T(8,128)S(1)}, u32[]{:S(2)}, u32[]{:S(2)}) collective-permute-start(f32[240,128]{1,0:T(8,128)S(1)} %get-tuple-element.21), channel_id=1, source_target_pairs={{8,16},{16,8},{9,17},{17,9},{10,18},{18,10},{11,19},{19,11},{12,20... | collective-permute-start | bytes 368648 | tf_op jit(solution)/shard_map/ppermute | solution.py:539
  6.1 0.4 %shard_map.78 = (f32[24,128]{1,0:T(8,128)S(1)}, f32[24,128]{1,0:T(8,128)S(1)}) custom-call(f32[10,4,16,256]{3,2,1,0:T(8,128)S(1)} %get-tuple-element.16.fine.own_f, f32[9,8,8,128]{3,2,1,0:T(8,128)S(1)} %get-tuple-element.17.coarse.own_c), custom_call_target="tpu_custom_call" | custom-call | bytes 24576 | tf_op jit(solution)/shard_map/pallas_call | solution.py:555
  6.5 1.1 %collective-permute-done.2.got_even = f32[240,128]{1,0:T(8,128)S(1)} collective-permute-done((f32[240,128]{1,0:T(8,128)S(1)}, f32[240,128]{1,0:T(8,128)S(1)}, u32[]{:S(2)}, u32[]{:S(2)}) %collective-permute-start.2) | collective-permute-done | bytes 122912 | tf_op jit(solution)/shard_map/ppermute | solution.py:539
  7.6 3.7 %collective-permute-done.3.got_odd = f32[240,128]{1,0:T(8,128)S(1)} collective-permute-done((f32[240,128]{1,0:T(8,128)S(1)}, f32[240,128]{1,0:T(8,128)S(1)}, u32[]{:S(2)}, u32[]{:S(2)}) %collective-permute-start.3) | collective-permute-done | bytes 122912 | tf_op jit(solution)/shard_map/ppermute | solution.py:539
  11.3 0.5 %shard_map.79 = (f32[10,4,8,256]{3,2,1,0:T(8,128)S(1)}, f32[9,8,8,128]{3,2,1,0:T(8,128)S(1)}, f32[40,128]{1,0:T(8,128)S(1)}, f32[40,128]{1,0:T(8,128)S(1)}) custom-call(f32[24,128]{1,0:T(8,128)S(1)} %get-tuple-element.18.firsts_ref, f32[24,128]{1,0:T(8,128)S(1)} %get-tuple-element.19.lasts_ref, f32[240,128]{1,0:T(8,128)S(1)} %collective-permute-done.2.got_even, ...), custom_call_target="tpu_custom_call" | custom-call | bytes 663552 | tf_op jit(solution)/shard_map/pallas_call | solution.py:555
  11.7 1.3 %collective-permute-start.4 = (f32[10,4,8,256]{3,2,1,0:T(8,128)S(1)}, f32[10,4,8,256]{3,2,1,0:T(8,128)S(1)}, u32[]{:S(2)}, u32[]{:S(2)}) collective-permute-start(f32[10,4,8,256]{3,2,1,0:T(8,128)S(1)} %get-tuple-element.22.own_fh), channel_id=1, source_target_pairs={{0,1},{1,0},{2,3},{3,2},{4,5},{5,4},{6,7},{7,6},{8,9},{9,8},{10,11... | collective-permute-start | bytes 983048 | tf_op jit(solution)/shard_map/ppermute | solution.py:539
  13.0 0.1 collective-permute-start.1
  13.1 0.4 %collective-permute-start.5 = (f32[9,8,8,128]{3,2,1,0:T(8,128)S(1)}, f32[9,8,8,128]{3,2,1,0:T(8,128)S(1)}, u32[]{:S(2)}, u32[]{:S(2)}) collective-permute-start(f32[9,8,8,128]{3,2,1,0:T(8,128)S(1)} %get-tuple-element.23.own_ch), channel_id=1, source_target_pairs={{0,1},{1,0},{2,3},{3,2},{4,5},{5,4},{6,7},{7,6},{8,9},{9,8},{10,11... | collective-permute-start | bytes 884744 | tf_op jit(solution)/shard_map/ppermute | solution.py:539
  13.5 1.3 %collective-permute-start.6 = (f32[40,128]{1,0:T(8,128)S(1)}, f32[40,128]{1,0:T(8,128)S(1)}, u32[]{:S(2)}, u32[]{:S(2)}) collective-permute-start(f32[40,128]{1,0:T(8,128)S(1)} %get-tuple-element.28), channel_id=1, source_target_pairs={{0,2},{2,0},{4,6},{6,4},{1,3},{3,1},{5,7},{7,5},{8,10},{10,8},{12,... | collective-permute-start | bytes 61448 | tf_op jit(solution)/shard_map/ppermute | solution.py:539
  14.8 1.3 %collective-permute-done.6.own_ye = f32[40,128]{1,0:T(8,128)S(1)} collective-permute-done((f32[40,128]{1,0:T(8,128)S(1)}, f32[40,128]{1,0:T(8,128)S(1)}, u32[]{:S(2)}, u32[]{:S(2)}) %collective-permute-start.6) | collective-permute-done | bytes 20512 | tf_op jit(solution)/shard_map/ppermute | solution.py:539
  16.2 2.1 %collective-permute-start.7 = (f32[40,128]{1,0:T(8,128)S(1)}, f32[40,128]{1,0:T(8,128)S(1)}, u32[]{:S(2)}, u32[]{:S(2)}) collective-permute-start(f32[40,128]{1,0:T(8,128)S(1)} %get-tuple-element.29), channel_id=1, source_target_pairs={{2,4},{4,2},{3,5},{5,3},{10,12},{12,10},{11,13},{13,11},{18,20},{2... | collective-permute-start | bytes 61448 | tf_op jit(solution)/shard_map/ppermute | solution.py:539
  18.2 2.4 %collective-permute-done.7.own_yo = f32[40,128]{1,0:T(8,128)S(1)} collective-permute-done((f32[40,128]{1,0:T(8,128)S(1)}, f32[40,128]{1,0:T(8,128)S(1)}, u32[]{:S(2)}, u32[]{:S(2)}) %collective-permute-start.7) | collective-permute-done | bytes 20512 | tf_op jit(solution)/shard_map/ppermute | solution.py:539
  20.7 2.4 %collective-permute-start.8 = (f32[40,128]{1,0:T(8,128)S(1)}, f32[40,128]{1,0:T(8,128)S(1)}, u32[]{:S(2)}, u32[]{:S(2)}) collective-permute-start(f32[40,128]{1,0:T(8,128)S(1)} %collective-permute-done.6.own_ye), channel_id=1, source_target_pairs={{0,1},{1,0},{2,3},{3,2},{4,5},{5,4},{6,7},{7,6},{8,9},{9,8},{10,11... | collective-permute-start | bytes 61448 | tf_op jit(solution)/shard_map/ppermute | solution.py:539
  23.1 0.0 collective-permute-done.1.far_c
  23.1 0.0 collective-permute-start.9
  23.1 0.0 collective-permute-done.5.far_ch
  23.1 0.0 collective-permute-done.4.far_fh
  23.1 0.0 collective-permute-done.far_f
  23.1 0.9 %shard_map.80 = (f32[10,8,24,128]{3,2,1,0:T(8,128)S(1)}, f32[9,16,16,128]{3,2,1,0:T(8,128)S(1)}) custom-call(f32[10,4,16,256]{3,2,1,0:T(8,128)S(1)} %get-tuple-element.16.fine.own_f, f32[9,8,8,128]{3,2,1,0:T(8,128)S(1)} %get-tuple-element.17.coarse.own_c, f32[10,4,16,256]{3,2,1,0:T(8,128)S(1)} %collective-permute-done.far_f, ...), custom_call_target="tpu_custom_call" | custom-call | bytes 2162688 | tf_op jit(solution)/shard_map/pallas_call | solution.py:555
  24.0 1.9 %shard_map.81 = (f32[3,4,16,256]{3,2,1,0:T(8,128)S(1)}, f32[3,8,8,128]{3,2,1,0:T(8,128)S(1)}) custom-call(f32[10,4,16,256]{3,2,1,0:T(8,128)S(1)} %get-tuple-element.16.fine.own_f, f32[9,8,8,128]{3,2,1,0:T(8,128)S(1)} %get-tuple-element.17.coarse.own_c, f32[10,4,16,256]{3,2,1,0:T(8,128)S(1)} %collective-permute-done.far_f, ...), custom_call_target="tpu_custom_call" | custom-call | flops 4000000 | bytes 294912 | tf_op jit(solution)/shard_map/pallas_call | solution.py:555
  25.9 0.0 collective-permute-done.8.far_ye
  25.9 0.0 collective-permute-done.9.far_yo
  25.9 3.7 %shard_map.82 = (f32[3,4,16,256]{3,2,1,0:T(8,128)}, f32[3,8,8,128]{3,2,1,0:T(8,128)}) custom-call(f32[10,8,24,128]{3,2,1,0:T(8,128)S(1)} %get-tuple-element.24.strip_f, f32[9,16,16,128]{3,2,1,0:T(8,128)S(1)} %get-tuple-element.25.strip_c, f32[3,4,16,256]{3,2,1,0:T(8,128)S(1)} %get-tuple-element.26.main_f, f32[3,8,8,128]{3,2,1,0:T(8,128)S(1)} %get-tuple-element.27.main_c, ...), custom_call_target="tpu_custom_call" | custom-call | bytes 294912 | tf_op jit(solution)/shard_map/pallas_call | solution.py:555
Async XLA Ops:
  2.0 21.1 %collective-permute-start = (f32[10,4,16,256]{3,2,1,0:T(8,128)S(1)}, f32[10,4,16,256]{3,2,1,0:T(8,128)S(1)}, u32[]{:S(2)}, u32[]{:S(2)}) collective-permute-start(f32[10,4,16,256]{3,2,1,0:T(8,128)S(1)} %get-tuple-element.16.fine.own_f), channel_id=1, source_target_pairs={{0,1},{1,0},{2,3},{3,2},{4,5},{5,4},{6,7},{7,6},{8,9},{9,8},{10,11... | collective-permute-start | bytes 1966088 | tf_op jit(solution)/shard_map/ppermute | solution.py:539
  2.8 4.8 %collective-permute-start.2 = (f32[240,128]{1,0:T(8,128)S(1)}, f32[240,128]{1,0:T(8,128)S(1)}, u32[]{:S(2)}, u32[]{:S(2)}) collective-permute-start(f32[240,128]{1,0:T(8,128)S(1)} %get-tuple-element.20), channel_id=1, source_target_pairs={{0,8},{8,0},{16,24},{24,16},{1,9},{9,1},{17,25},{25,17},{2,10},{10... | collective-permute-start | bytes 368648 | tf_op jit(solution)/shard_map/ppermute | solution.py:539
  4.0 7.3 %collective-permute-start.3 = (f32[240,128]{1,0:T(8,128)S(1)}, f32[240,128]{1,0:T(8,128)S(1)}, u32[]{:S(2)}, u32[]{:S(2)}) collective-permute-start(f32[240,128]{1,0:T(8,128)S(1)} %get-tuple-element.21), channel_id=1, source_target_pairs={{8,16},{16,8},{9,17},{17,9},{10,18},{18,10},{11,19},{19,11},{12,20... | collective-permute-start | bytes 368648 | tf_op jit(solution)/shard_map/ppermute | solution.py:539
  11.7 11.3 %collective-permute-start.4 = (f32[10,4,8,256]{3,2,1,0:T(8,128)S(1)}, f32[10,4,8,256]{3,2,1,0:T(8,128)S(1)}, u32[]{:S(2)}, u32[]{:S(2)}) collective-permute-start(f32[10,4,8,256]{3,2,1,0:T(8,128)S(1)} %get-tuple-element.22.own_fh), channel_id=1, source_target_pairs={{0,1},{1,0},{2,3},{3,2},{4,5},{5,4},{6,7},{7,6},{8,9},{9,8},{10,11... | collective-permute-start | bytes 983048 | tf_op jit(solution)/shard_map/ppermute | solution.py:539
  13.0 10.0 %collective-permute-start.1 = (f32[9,8,8,128]{3,2,1,0:T(8,128)S(1)}, f32[9,8,8,128]{3,2,1,0:T(8,128)S(1)}, u32[]{:S(2)}, u32[]{:S(2)}) collective-permute-start(f32[9,8,8,128]{3,2,1,0:T(8,128)S(1)} %get-tuple-element.17.coarse.own_c), channel_id=1, source_target_pairs={{0,1},{1,0},{2,3},{3,2},{4,5},{5,4},{6,7},{7,6},{8,9},{9,8},{10,11... | collective-permute-start | bytes 884744 | tf_op jit(solution)/shard_map/ppermute | solution.py:539
  13.1 10.0 %collective-permute-start.5 = (f32[9,8,8,128]{3,2,1,0:T(8,128)S(1)}, f32[9,8,8,128]{3,2,1,0:T(8,128)S(1)}, u32[]{:S(2)}, u32[]{:S(2)}) collective-permute-start(f32[9,8,8,128]{3,2,1,0:T(8,128)S(1)} %get-tuple-element.23.own_ch), channel_id=1, source_target_pairs={{0,1},{1,0},{2,3},{3,2},{4,5},{5,4},{6,7},{7,6},{8,9},{9,8},{10,11... | collective-permute-start | bytes 884744 | tf_op jit(solution)/shard_map/ppermute | solution.py:539
  13.5 2.6 %collective-permute-start.6 = (f32[40,128]{1,0:T(8,128)S(1)}, f32[40,128]{1,0:T(8,128)S(1)}, u32[]{:S(2)}, u32[]{:S(2)}) collective-permute-start(f32[40,128]{1,0:T(8,128)S(1)} %get-tuple-element.28), channel_id=1, source_target_pairs={{0,2},{2,0},{4,6},{6,4},{1,3},{3,1},{5,7},{7,5},{8,10},{10,8},{12,... | collective-permute-start | bytes 61448 | tf_op jit(solution)/shard_map/ppermute | solution.py:539
  16.2 4.5 %collective-permute-start.7 = (f32[40,128]{1,0:T(8,128)S(1)}, f32[40,128]{1,0:T(8,128)S(1)}, u32[]{:S(2)}, u32[]{:S(2)}) collective-permute-start(f32[40,128]{1,0:T(8,128)S(1)} %get-tuple-element.29), channel_id=1, source_target_pairs={{2,4},{4,2},{3,5},{5,3},{10,12},{12,10},{11,13},{13,11},{18,20},{2... | collective-permute-start | bytes 61448 | tf_op jit(solution)/shard_map/ppermute | solution.py:539
  20.7 5.2 %collective-permute-start.8 = (f32[40,128]{1,0:T(8,128)S(1)}, f32[40,128]{1,0:T(8,128)S(1)}, u32[]{:S(2)}, u32[]{:S(2)}) collective-permute-start(f32[40,128]{1,0:T(8,128)S(1)} %collective-permute-done.6.own_ye), channel_id=1, source_target_pairs={{0,1},{1,0},{2,3},{3,2},{4,5},{5,4},{6,7},{7,6},{8,9},{9,8},{10,11... | collective-permute-start | bytes 61448 | tf_op jit(solution)/shard_map/ppermute | solution.py:539
  23.1 2.9 %collective-permute-start.9 = (f32[40,128]{1,0:T(8,128)S(1)}, f32[40,128]{1,0:T(8,128)S(1)}, u32[]{:S(2)}, u32[]{:S(2)}) collective-permute-start(f32[40,128]{1,0:T(8,128)S(1)} %collective-permute-done.7.own_yo), channel_id=1, source_target_pairs={{0,1},{1,0},{2,3},{3,2},{4,5},{5,4},{6,7},{7,6},{8,9},{9,8},{10,11... | collective-permute-start | bytes 61448 | tf_op jit(solution)/shard_map/ppermute | solution.py:539

commit v4 on v3

v4 whole, which is shorter than its diff:
```python
import functools

import jax
import jax.numpy as jnp
from jax import lax
from jax.experimental import pallas as pl
from jax.experimental.pallas import tpu as pltpu
from jax.sharding import PartitionSpec as P


time_step = 0.15
LANES = 128
MARGIN = 8
U, Q, RHO, MU, LAM, W = 0, 3, 6, 7, 8, 9
FINE_FIELDS, COARSE_FIELDS = 10, 9


def fine_widths(field, layer, layers):
    bottom, above = layer == layers - 1, layer == layers - 2
    if field < Q:
        return (4 if bottom else 3 if above else 2), 2
    if field <= RHO:
        return (2 if bottom else 1), 1
    return (2 if bottom or above else 1), 2


def coarse_widths(field):
    if field < Q:
        return 2, 2
    if field <= RHO:
        return 1, 1
    return 1, 2


def plane_table(fields, layers, widths, slot, span):
    assert 2 * layers * span == LANES
    table = []
    for layer in range(layers):
        for field in range(fields):
            high, low = widths(field, layer)
            table.append((field, layer, high, low, slot(field) + layer * span))
    return table


def fine_slot(field):
    if field < Q:
        return 4 * field
    if field in (MU, LAM):
        return 12 + 2 * (field - MU)
    return LANES // 2 + {W: 0, Q: 2, Q + 1: 4, Q + 2: 6, RHO: 8}[field]


def coarse_slot(field):
    if field < Q:
        return 2 * field
    return 6 if field == MU else LANES // 2 + {LAM: 0, Q: 2, Q + 1: 3, Q + 2: 4, RHO: 5}[field]


def round_up(value, multiple):
    return -(-value // multiple) * multiple


FINE_SPAN, COARSE_SPAN = 16, 8


def tables(fine_layers, coarse_layers):
    fine = plane_table(
        FINE_FIELDS, fine_layers, lambda f, l: fine_widths(f, l, fine_layers), fine_slot, FINE_SPAN
    )
    coarse = plane_table(
        COARSE_FIELDS, coarse_layers, lambda f, l: coarse_widths(f), coarse_slot, COARSE_SPAN
    )
    return fine, coarse


def edge_rows(tables_of_grids, parts_of_grids, first):
    pieces, at = [], 0
    for grid, (table, parts) in enumerate(zip(tables_of_grids, parts_of_grids)):
        for field, layer, high, low, _ in table:
            size = high if first else low
            for t in range(parts):
                pieces.append((grid, field, layer, t, size, at))
                at += size
    return pieces, round_up(at, 8)


def grid_tables(fine_shape, coarse_shape):
    fine, coarse = tables(fine_shape[1], coarse_shape[1])
    return (fine, coarse), (fine_shape[3] // LANES, coarse_shape[3] // LANES)


def pack_x_kernel(fu, fp, fm, cu, cp, cm, fine, coarse, to_even, to_odd, sems):
    copies = []
    for out, sources in ((fine, (fu, fp, fm)), (coarse, (cu, cp, cm))):
        for first, source in zip((U, Q, RHO), sources):
            copies.append(
                pltpu.make_async_copy(
                    source, out.at[first : first + source.shape[0]], sems.at[len(copies)]
                )
            )
    for copy in copies:
        copy.start()
    for copy in copies:
        copy.wait()
    grids = grid_tables(fine.shape, coarse.shape)

    def fill(out, first):
        for grid, field, layer, t, size, at in edge_rows(*grids, first)[0]:
            ref = (fine, coarse)[grid]
            start = 0 if first else ref.shape[2] - size
            out[at : at + size, :] = ref[
                field, layer, start : start + size, t * LANES : (t + 1) * LANES
            ]

    even = lax.rem(lax.axis_index("gx"), 2) == 0

    @pl.when(even)
    def _():
        fill(to_even, False)
        fill(to_odd, True)

    @pl.when(jnp.logical_not(even))
    def _():
        fill(to_even, True)
        fill(to_odd, False)


class Bundle:
    def __init__(self, fine_shape, coarse_shape):
        self.layers = fine_shape[1], coarse_shape[1]
        self.parts = fine_shape[3] // LANES, coarse_shape[3] // LANES
        self.rows = fine_shape[2] // 8 + 1, coarse_shape[2] // 8 + 1
        self.halo_base, self.ends_base, at = [], [], 0
        for grid, fields in enumerate((FINE_FIELDS, COARSE_FIELDS)):
            self.halo_base.append(at)
            at += fields * self.layers[grid] * self.parts[grid]
            self.ends_base.append(at)
            at += fields * self.rows[grid]
        self.size = at

    def halo(self, grid, field, layer, part):
        return self.halo_base[grid] + (field * self.layers[grid] + layer) * self.parts[grid] + part

    def ends(self, ref, grid, field):
        base = self.ends_base[grid] + field * self.rows[grid]
        return jnp.concatenate([ref[base + r] for r in range(self.rows[grid])], axis=0)


def end_columns(read, layers, span):
    for layer in range(layers):
        first, last = read(layer)
        lane = lax.broadcasted_iota(jnp.int32, first.shape, 1)
        value = jnp.where(lane < LANES // 2, first, last)
        value = pltpu.roll(value, layer * span + span // 2, 1)
        total = value if layer == 0 else jnp.where(lane >= layer * span, value, total)
    return total


def pack_inner_kernel(fine, coarse, fine_ends, coarse_ends):
    for ref, out, span in ((fine, fine_ends, FINE_SPAN), (coarse, coarse_ends, COARSE_SPAN)):
        for field in range(ref.shape[0]):

            def read(layer):
                return ref[field, layer, :, :LANES], ref[field, layer, :, ref.shape[3] - LANES :]

            out[field] = end_columns(read, ref.shape[1], span)


def pack_y_kernel(bundle, fine_ends, coarse_ends, got_even, got_odd, out, to_even, to_odd):
    grids = tables(*bundle.layers), bundle.parts

    def halo(high_ref, low_ref):
        for first, ref in ((True, high_ref), (False, low_ref)):
            for grid, field, layer, t, size, at in edge_rows(*grids, first)[0]:
                start = 0 if first else MARGIN - size
                out[bundle.halo(grid, field, layer, t), start : start + size, :] = ref[
                    at : at + size, :
                ]

    for grid, table in enumerate(grids[0]):
        for field, layer, *_ in table:
            for t in range(bundle.parts[grid]):
                out[bundle.halo(grid, field, layer, t)] = jnp.zeros((MARGIN, LANES), jnp.float32)

    even = lax.rem(lax.axis_index("gx"), 2) == 0

    @pl.when(even)
    def _():
        halo(got_even, got_odd)

    @pl.when(jnp.logical_not(even))
    def _():
        halo(got_odd, got_even)

    packed = []
    for grid, (table, inner, span) in enumerate(
        zip(grids[0], (fine_ends, coarse_ends), (FINE_SPAN, COARSE_SPAN))
    ):
        rows = inner.shape[1] + MARGIN
        lane = lax.broadcasted_iota(jnp.int32, (rows, LANES), 1)
        within = jnp.bitwise_and(lane, span - 1)
        sides = [[None, None], [None, None]]
        for field, layer, high, low, slot in sorted(table, key=lambda entry: entry[4]):
            if layer:
                continue

            def read(layer):
                parts = (0, bundle.parts[grid] - 1)
                return [out[bundle.halo(grid, field, layer, t)] for t in parts]

            ends = jnp.concatenate(
                [inner[field], end_columns(read, bundle.layers[grid], span)], axis=0
            )
            base = bundle.ends_base[grid] + field * bundle.rows[grid]
            for r in range(bundle.rows[grid]):
                out[base + r] = ends[r * 8 : (r + 1) * 8]
            half, start = divmod(slot, LANES // 2)
            for side, first in enumerate((span // 2, span // 2 - low)):
                shift = (slot - first) % LANES
                value = pltpu.roll(ends, shift, 1) if shift else ends
                before = sides[side][half]
                sides[side][half] = (
                    value if before is None else jnp.where(within >= start, value, before)
                )
        packed.append([jnp.where(lane < LANES // 2, lower, upper) for lower, upper in sides])
    even_y = lax.rem(lax.axis_index("gy"), 2) == 0

    def place(first_out, last_out):
        at = 0
        for firsts, lasts in packed:
            rows = slice(at, at + firsts.shape[0])
            first_out[rows, :] = firsts
            last_out[rows, :] = lasts
            at += firsts.shape[0]

    @pl.when(even_y)
    def _():
        place(to_odd, to_even)

    @pl.when(jnp.logical_not(even_y))
    def _():
        place(to_even, to_odd)


def ahead(value, axis):
    return pltpu.roll(value, value.shape[axis] - 1, axis)


def behind(value, axis):
    return value - pltpu.roll(value, 1, axis)


def stress_of(here, below, medium, stretched):
    rigidity, lame = medium[0], medium[1]
    dx = [ahead(f, 0) - f for f in here]
    dy = [ahead(f, 1) - f for f in here]
    dz = [b - f for b, f in zip(below, here)]
    if stretched:
        dz = [f * medium[2] for f in dz]
    trace = lame * (dx[0] + dy[1] + dz[2])
    double = rigidity + rigidity
    return (
        trace + double * dx[0],
        trace + double * dy[1],
        trace + double * dz[2],
        rigidity * (dy[0] + dx[1]),
        rigidity * (dz[0] + dx[2]),
        rigidity * (dz[1] + dy[2]),
    )


def force_of(stress, above, outward):
    nx, ny, nz, xy, xz, yz = stress
    up = [xz, yz, nz]
    if above is not None:
        up = [f - a for f, a in zip(up, (above[4], above[5], above[2]))]
    if outward is not None:
        up = [f * outward for f in up]
    return (
        behind(nx, 0) + behind(xy, 1) + up[0],
        behind(xy, 0) + behind(ny, 1) + up[1],
        behind(xz, 0) + behind(yz, 1) + up[2],
    )


def bf16_parts(value):
    parts = []
    for _ in range(3):
        part = value.astype(jnp.bfloat16)
        parts.append(part)
        value = value - part.astype(jnp.float32)
    return parts


def select_lanes(planes, matrix):
    rows = planes[0].shape[0]
    parts = bf16_parts(jnp.concatenate(planes, axis=0))
    product = jnp.dot(
        jnp.concatenate(parts, axis=0), matrix, preferred_element_type=jnp.float32
    )
    size = rows * len(planes)
    total = product[:size] + product[size : 2 * size] + product[2 * size :]
    return [total[k * rows : (k + 1) * rows] for k in range(len(planes))]


def select_rows(matrix, planes):
    lanes = planes[0].shape[1]
    parts = bf16_parts(jnp.concatenate(planes, axis=1))
    product = jnp.dot(
        jnp.concatenate([matrix] * 3, axis=1),
        jnp.concatenate(parts, axis=0),
        preferred_element_type=jnp.float32,
    )
    return [product[:, k * lanes : (k + 1) * lanes] for k in range(len(planes))]


def bf16_mask(condition):
    return jnp.where(condition, 1.0, 0.0).astype(jnp.bfloat16)


class Grids:
    def __init__(self, height, cheight, lanes, clanes, lane_of):
        def pairs(shape, fine_axis, size_of):
            f = lax.broadcasted_iota(jnp.int32, shape, fine_axis)
            c = lax.broadcasted_iota(jnp.int32, shape, 1 - fine_axis)
            return bf16_mask(size_of(f) == c)

        def row_of(f):
            turn = height - MARGIN // 2
            return jnp.right_shift(jnp.where(f < turn, f, f - height + 2 * cheight), 1)

        self.up_rows = pairs((height, cheight), 0, row_of)
        self.down_rows = pairs((cheight, height), 1, row_of)
        self.up_lanes = pairs((clanes, lanes), 1, lane_of)
        self.down_lanes = pairs((lanes, clanes), 0, lane_of)

    def prolong(self, planes):
        return select_rows(self.up_rows, select_lanes(planes, self.up_lanes))

    def restrict(self, planes):
        planes = select_lanes(select_rows(self.down_rows, planes), self.down_lanes)
        return [0.25 * plane for plane in planes]


def row_index(height, shape):
    index = lax.broadcasted_iota(jnp.int32, shape, 0)
    return jnp.where(index < height - MARGIN // 2, index, index - height)


def solver(plane, medium, ghost_above, ghost_below, last, stretched):
    known = {}

    def here(g):
        if g < 0:
            return ghost_above
        if g == last + 1:
            return ghost_below
        return [plane(k, g) for k in range(3)]

    def stress(g):
        if g < 0 and ghost_above is None:
            return None
        if g not in known:
            fields = (MU, LAM, W) if stretched else (MU, LAM)
            known[g] = stress_of(
                here(g), here(g + 1), [medium(k, max(g, 0)) for k in fields], stretched
            )
        return known[g]

    return stress


def advance(plane, before, medium, stress, g, scale, stretched):
    force = force_of(stress(g), stress(g - 1), medium(W, g) if stretched else None)
    rate = scale / medium(RHO, g)
    return [
        plane(k, g) + plane(k, g) - before(k, g) + force[k] * rate for k in range(3)
    ]


def step_scales():
    scale = jnp.float32(time_step * time_step)
    return scale, 0.25 * scale


def first_step(dev, layers, clayers, fine, coarse, grids, keep_f, keep_c, state_f, state_c):
    depth, cdepth = 2 * layers, 2 * clayers
    scale, cscale = step_scales()
    three = range(3)
    ghost_f = grids.prolong([coarse(k, 0) for k in three])
    ghost_c = grids.restrict([fine(k, depth - 1) for k in three])
    zero_c = [jnp.zeros_like(ghost_c[0])] * 3
    stress_f = solver(fine, fine, None, ghost_f, depth - 1, True)
    stress_c = solver(coarse, coarse, ghost_c, zero_c, cdepth - 1, False)
    near = {*range(max(dev * layers - 1, 0), min((dev + 1) * layers + 1, depth)), depth - 1}
    cnear = {0, *range(max(dev * clayers - 1, 0), min((dev + 1) * clayers + 1, cdepth))}
    for g in sorted(near):
        values = advance(fine, lambda k, g: fine(Q + k, g), fine, stress_f, g, scale, True)
        for k in three:
            state_f[k, g] = jnp.where(keep_f(g), values[k], 0.0)
    for g in sorted(cnear):
        values = advance(coarse, lambda k, g: coarse(Q + k, g), coarse, stress_c, g, cscale, False)
        for k in three:
            state_c[k, g] = jnp.where(keep_c, values[k], 0.0)


def second_step(dev, layers, clayers, fine, coarse, grids, state_f, state_c, out_f, out_c):
    depth, cdepth = 2 * layers, 2 * clayers
    scale, cscale = step_scales()
    ghost_f = ghost_c = None
    if dev == 1:
        ghost_f = grids.prolong([state_c[k, 0] for k in range(3)])
    else:
        ghost_c = grids.restrict([state_f[k, depth - 1] for k in range(3)])
    zero_c = [jnp.zeros(state_c.shape[2:], jnp.float32)] * 3
    now_f, now_c = lambda k, g: state_f[k, g], lambda k, g: state_c[k, g]
    stress_f = solver(now_f, fine, None, ghost_f, depth - 1, True)
    stress_c = solver(now_c, coarse, ghost_c, zero_c, cdepth - 1, False)
    for l in range(layers):
        values = advance(now_f, fine, fine, stress_f, dev * layers + l, scale, True)
        for k in range(3):
            out_f[k, l] = values[k][: out_f.shape[2]]
    for l in range(clayers):
        values = advance(now_c, coarse, coarse, stress_c, dev * clayers + l, cscale, False)
        for k in range(3):
            out_c[k, l] = values[k][: out_c.shape[2]]


def for_each_core(body):
    dev = lax.axis_index("dev")

    @pl.when(dev == 0)
    def _():
        body(0)

    @pl.when(dev != 0)
    def _():
        body(1)


def inside(index, axis, size):
    at = index + lax.axis_index(axis) * size
    return (at >= 0) & (at < lax.axis_size(axis) * size)


def readers(dev, bundle, own_f, own_c, far_f, far_c, own_b, far_b):
    def reader(grid, own, far):
        def read(field, g):
            layer = g % bundle.layers[grid]
            mine = g // bundle.layers[grid] == dev
            ref, tiles = (own, own_b) if mine else (far, far_b)
            halo = [
                tiles[bundle.halo(grid, field, layer, t)] for t in range(bundle.parts[grid])
            ]
            return jnp.concatenate([ref[field, layer], jnp.concatenate(halo, axis=1)], axis=0)

        return read

    return reader(0, own_f, far_f), reader(1, own_c, far_c)


def tile_grids(own_f, own_c):
    return Grids(
        own_f.shape[2] + MARGIN, own_c.shape[2] + MARGIN, own_f.shape[3], own_c.shape[3],
        lambda f: jnp.right_shift(f, 1),
    )


def first_kernel(bundle, own_f, own_c, far_f, far_c, own_b, far_b, state_f, state_c):
    _, layers, n, width = own_f.shape
    _, clayers, nc, cwidth = own_c.shape
    fx = row_index(n + MARGIN, (n + MARGIN, width))
    cx = row_index(nc + MARGIN, (nc + MARGIN, cwidth))
    rows_f = inside(fx, "gx", n) & (fx >= -1)
    keep_c = inside(cx, "gx", nc) & (cx >= -1) & (cx <= nc)
    grids = tile_grids(own_f, own_c)

    def body(dev):
        fine, coarse = readers(dev, bundle, own_f, own_c, far_f, far_c, own_b, far_b)
        first_step(
            dev, layers, clayers, fine, coarse, grids,
            lambda g: rows_f & (fx <= n + (g == 2 * layers - 1)), keep_c, state_f, state_c,
        )

    for_each_core(body)


def second_kernel(
    bundle, own_f, own_c, far_f, far_c, own_b, far_b, state_f, state_c, out_f, out_c, strip_f, strip_c
):
    grids = tile_grids(own_f, own_c)

    def body(dev):
        fine, coarse = readers(dev, bundle, own_f, own_c, far_f, far_c, own_b, far_b)
        second_step(
            dev, own_f.shape[1], own_c.shape[1], fine, coarse, grids, state_f, state_c, out_f, out_c
        )

    for_each_core(body)
    top = lax.axis_index("dev") == 0
    for grid, (strip, span) in enumerate(((strip_f, FINE_SPAN), (strip_c, COARSE_SPAN))):
        lane = lax.broadcasted_iota(jnp.int32, (strip.shape[1], LANES), 1)
        for field in range(strip.shape[0]):
            own, far = bundle.ends(own_b, grid, field), bundle.ends(far_b, grid, field)
            upper, lower = jnp.where(top, own, far), jnp.where(top, far, own)
            whole = jnp.where(lane < LANES // 2, upper, pltpu.roll(lower, LANES // 2, 1))
            strip[field, :, :LANES] = pltpu.roll(whole, LANES - span // 4, 1)
            strip[field, :, LANES:] = whole


def strip_kernel(
    strip_f, strip_c, main_f, main_c, own_ye, own_yo, far_ye, far_yo, out_f, out_c
):
    layers, n, width = main_f.shape[1:]
    clayers, nc, cwidth = main_c.shape[1:]
    height, cheight = n + MARGIN, nc + MARGIN
    depth, cdepth = 2 * layers, 2 * clayers
    fine_table, coarse_table = tables(layers, clayers)
    three = range(3)
    top = lax.axis_index("dev") == 0
    even = lax.rem(lax.axis_index("gy"), 2) == 0
    wide = 2 * LANES

    def places(rows, span, extent):
        lane = lax.broadcasted_iota(jnp.int32, (rows, wide), 1)
        low = lane < LANES
        inner = jnp.bitwise_and(lane, LANES - 1)
        within = jnp.bitwise_and(lane, span - 1)
        room = span // 4
        at = jnp.where(low, within - room, within + extent - span // 2)
        used = within < span - room
        return jnp.right_shift(inner, span.bit_length() - 1), at, used

    fg, fy, used_f = places(height, FINE_SPAN, width)
    cg, cy, used_c = places(cheight, COARSE_SPAN, cwidth)
    fx, cx = row_index(height, (height, wide)), row_index(cheight, (cheight, wide))
    last = (fg == depth - 1).astype(jnp.int32)
    keep_f = (
        used_f & inside(fx, "gx", n) & inside(fy, "gy", width)
        & (fx >= -1) & (fy >= -1) & (fx <= n + last) & (fy <= width + last)
    )
    keep_c = (
        used_c & inside(cx, "gx", nc) & inside(cy, "gy", cwidth)
        & (cx >= -1) & (cx <= nc) & (cy >= -1) & (cy <= cwidth)
    )

    def filled(table, src, start, span):
        rows = src.shape[1]
        room = span // 4
        lane = lax.broadcasted_iota(jnp.int32, (rows, LANES), 1)
        within = jnp.bitwise_and(lane, span - 1)
        sides = []
        for e, o in ((own_ye, own_yo), (far_ye, far_yo)):
            e, o = e[start : start + rows, :], o[start : start + rows, :]
            sides.append((jnp.where(even, o, e), jnp.where(even, e, o)))
        uppers = [jnp.where(top, a, b) for a, b in zip(*sides)]
        lowers = [jnp.where(top, b, a) for a, b in zip(*sides)]
        fields = []
        for field in range(src.shape[0]):
            entries = [entry for entry in table if entry[0] == field]
            slot = entries[0][4]
            width_of = (max(e[3] for e in entries), max(e[2] for e in entries))
            parts = []
            for side in range(2):
                size = width_of[side]
                first = span // 2 if side else room - size
                shift = (first - slot) % LANES
                halo = jnp.where(
                    lane < LANES // 2,
                    pltpu.roll(uppers[side], shift, 1) if shift else uppers[side],
                    pltpu.roll(lowers[side], (shift + LANES // 2) % LANES, 1),
                )
                parts.append(
                    jnp.where(
                        (within >= first) & (within < first + size),
                        halo,
                        src[field, :, side * LANES : (side + 1) * LANES],
                    )
                )
            fields.append(jnp.concatenate(parts, axis=1))
        return fields

    fine = filled(fine_table, strip_f, 0, FINE_SPAN)
    coarse = filled(coarse_table, strip_c, height, COARSE_SPAN)

    def fine_lane(f):
        tile, inner = jnp.bitwise_and(f, LANES), jnp.bitwise_and(f, LANES - 1)
        bottom = inner - (depth - 1) * FINE_SPAN
        return jnp.where(bottom >= 0, tile + jnp.right_shift(bottom, 1), -1)

    grids = Grids(height, cheight, wide, wide, fine_lane)
    scale = jnp.float32(time_step * time_step)

    def shifted(value, lanes):
        return pltpu.roll(value, lanes % wide, 1)

    def lift(stress, lanes, at_top, above):
        return [jnp.where(at_top, a, shifted(stress[k], lanes)) for k, a in zip((2, 4, 5), above)]

    def step(u, p, v, q):
        ghost_f = grids.prolong(v)
        ghost_c = grids.restrict(u)
        below = [jnp.where(fg == depth - 1, b, shifted(f, -FINE_SPAN)) for f, b in zip(u, ghost_f)]
        stress = stress_of(u, below, [fine[k] for k in (MU, LAM, W)], True)
        up = lift(stress, FINE_SPAN, fg == 0, [0.0] * 3)
        force = force_of(stress, {2: up[0], 4: up[1], 5: up[2]}, fine[W])
        rate = scale / fine[RHO]
        next_u = [a + a - b + f * rate for a, b, f in zip(u, p, force)]
        medium = [coarse[k] for k in (MU, LAM)]
        under = [jnp.where(cg == cdepth - 1, 0.0, shifted(f, -COARSE_SPAN)) for f in v]
        stress = stress_of(v, under, medium, False)
        above = stress_of(ghost_c, v, medium, False)
        up = lift(stress, COARSE_SPAN, cg == 0, [above[k] for k in (2, 4, 5)])
        force = force_of(stress, {2: up[0], 4: up[1], 5: up[2]}, None)
        rate = (0.25 * scale) / coarse[RHO]
        next_v = [a + a - b + f * rate for a, b, f in zip(v, q, force)]
        return next_u, next_v

    u, v = fine[:3], coarse[:3]
    next_u, next_v = step(u, fine[Q:RHO], v, coarse[Q:RHO])
    next_u = [jnp.where(keep_f, f, 0.0) for f in next_u]
    next_v = [jnp.where(keep_c, f, 0.0) for f in next_v]
    last_u, last_v = step(next_u, u, next_v, v)

    for values, out, main, span in (
        (last_u, out_f, main_f, FINE_SPAN),
        (last_v, out_c, main_c, COARSE_SPAN),
    ):
        cells, extent = out.shape[2:]
        room = span // 4
        lane = lax.broadcasted_iota(jnp.int32, (cells, LANES), 1)
        for k in three:
            ends = [values[k][:cells, side * LANES : (side + 1) * LANES] for side in range(2)]
            ends = [jnp.where(top, e, pltpu.roll(e, LANES // 2, 1)) for e in ends]
            for l in range(out.shape[1]):
                first = pltpu.roll(ends[0], LANES - l * span - room, 1)
                final = pltpu.roll(ends[1], LANES - l * span - span // 2, 1)
                for start in range(0, extent, LANES):
                    part = main[k, l, :, start : start + LANES]
                    if start == 0:
                        part = jnp.where(lane < room, first, part)
                    if start == extent - LANES:
                        part = jnp.where(lane >= LANES - room, final, part)
                    out[k, l, :, start : start + LANES] = part


def partners(count, parity):
    pairs = [(i, ((i + parity) ^ 1) - parity) for i in range(count)]
    return [(i, j) for i, j in pairs if 0 <= j < count]


def swap(value, axis, parity):
    return lax.ppermute(value, axis, partners(lax.axis_size(axis), parity))


def call(kernel, out_shape, operands, scratch=(), flops=0, space=pltpu.VMEM, limit=24):
    size = sum(o.size for o in out_shape) * 4
    call = pl.pallas_call(
        kernel,
        out_shape=out_shape,
        in_specs=[pl.BlockSpec(memory_space=space)] * len(operands),
        out_specs=[pl.BlockSpec(memory_space=pltpu.VMEM)] * len(out_shape),
        scratch_shapes=list(scratch),
        cost_estimate=pl.CostEstimate(flops=flops, bytes_accessed=size, transcendentals=0),
        compiler_params=pltpu.CompilerParams(vmem_limit_bytes=limit * 1024 * 1024),
    )
    if space == pltpu.HBM:
        operands = [pltpu.with_memory_space_constraint(o, space) for o in operands]
    return call(*operands)


def shape(*dims):
    return jax.ShapeDtypeStruct(dims, jnp.float32)


def per_device(*inputs):
    _, layers, n, width = inputs[0].shape
    _, clayers, nc, cwidth = inputs[3].shape
    grids = grid_tables(inputs[0].shape, inputs[3].shape)
    rows = max(edge_rows(*grids, first)[1] for first in (True, False))
    height, cheight = n + MARGIN, nc + MARGIN

    edge = shape(rows, LANES)
    own_f, own_c, to_even, to_odd = call(
        pack_x_kernel,
        (shape(FINE_FIELDS, layers, n, width), shape(COARSE_FIELDS, clayers, nc, cwidth), edge, edge),
        inputs,
        scratch=(pltpu.SemaphoreType.DMA((6,)),),
        space=pltpu.HBM,
        limit=24,
    )
    got_odd = swap(to_odd, "gx", 1)
    got_even = swap(to_even, "gx", 0)
    far_f, far_c = swap(own_f, "dev", 0), swap(own_c, "dev", 0)

    fine_ends, coarse_ends = call(
        pack_inner_kernel,
        (shape(FINE_FIELDS, n, LANES), shape(COARSE_FIELDS, nc, LANES)),
        (own_f, own_c),
    )

    bundle = Bundle(inputs[0].shape, inputs[3].shape)
    side = shape(height + cheight, LANES)
    own_b, to_even, to_odd = call(
        functools.partial(pack_y_kernel, bundle),
        (shape(bundle.size, 8, LANES), side, side),
        (fine_ends, coarse_ends, got_even, got_odd),
    )
    own_yo = swap(to_odd, "gy", 1)
    own_ye = swap(to_even, "gy", 0)
    far_b = swap(own_b, "dev", 0)

    tiles = (own_f, own_c, far_f, far_c, own_b, far_b)
    states = call(
        functools.partial(first_kernel, bundle),
        (shape(3, 2 * layers, height, width), shape(3, 2 * clayers, cheight, cwidth)),
        tiles,
        flops=STEP_FLOPS,
    )
    results = (shape(*inputs[0].shape), shape(*inputs[3].shape))
    strips = (
        shape(FINE_FIELDS, height, 2 * LANES),
        shape(COARSE_FIELDS, cheight, 2 * LANES),
    )
    main_f, main_c, strip_f, strip_c = call(
        functools.partial(second_kernel, bundle),
        results + strips,
        tiles + tuple(states),
        flops=STEP_FLOPS,
    )
    far_yo, far_ye = swap(own_yo, "dev", 0), swap(own_ye, "dev", 0)
    return call(
        strip_kernel, results, (strip_f, strip_c, main_f, main_c, own_ye, own_yo, far_ye, far_yo)
    )


STEP_FLOPS = 2_000_000


def solution(mesh):
    spec = P(None, "dev", "gx", "gy")

    return jax.shard_map(
        per_device,
        mesh=mesh,
        in_specs=(spec,) * 6,
        out_specs=(spec, spec),
        check_vma=False,
    )
```

time: 29.9 us -> 24.9 us (0.83)
  waiting for transfers between devices: 8.59 us -> 6.14 us
  Pallas kernels: 8.8 us -> 6.45 us
    ppermute x10 -> x9, waiting for transfers between devices: 8.59 us -> 6.14 us  [swap(): return lax.ppermute(value, axis, partners(lax.axis_size(axis), parity))]
    pallas_call x6, Pallas kernels: 8.8 us -> 6.45 us  [call(): return call(*operands)]
    ppermute x10 -> x9, starting transfers between devices: 11.6 us -> 11.4 us  [swap(): return lax.ppermute(value, axis, partners(lax.axis_size(axis), parity))]
  transfers between devices with their start and end apart: 10 -> 9, of which waited for: 4 -> 3; matrix products, arithmetic and copies ran while one was open for 0% -> 0% of each run, Pallas kernels for 12% -> 8%
where the time goes in v4:
time: 24.9 us; the launch traced here: 24.7 us
  starting transfers between devices  11.4 us (46%)
  Pallas kernels  6.45 us (26%)
  waiting for transfers between devices  6.14 us (25%)
  between operations  0.71 us (3%)
    ppermute x9, starting transfers between devices, swap(): return lax.ppermute(value, axis, partners(lax.axis_size(axis), parity))  11.4 us
    pallas_call x6, Pallas kernels, call(): return call(*operands)  6.45 us
    ppermute x9, waiting for transfers between devices, swap(): return lax.ppermute(value, axis, partners(lax.axis_size(axis), parity))  6.14 us
  transfers between devices with their start and end apart: 9, of which 3 were waited for; matrix products, arithmetic and copies ran while one was open for 0% of the time, Pallas kernels for 8%

profile of v4, /device:TPU:21, one launch (start us, length us, event | category | flops | bytes accessed | tf_op | source)
XLA Modules:
  0.0 24.7 jit_solution(17598397372585845298)
XLA Ops:
  0.6 1.4 %shard_map.77 = (f32[10,4,16,256]{3,2,1,0:T(8,128)S(1)}, f32[9,8,8,128]{3,2,1,0:T(8,128)S(1)}, f32[240,128]{1,0:T(8,128)S(1)}, f32[240,128]{1,0:T(8,128)S(1)}) custom-call(f32[3,4,16,256]{3,2,1,0:T(8,128)} %fu.1, f32[3,4,16,256]{3,2,1,0:T(8,128)} %fp.1, f32[4,4,16,256]{3,2,1,0:T(8,128)} %fm.1, f32[3,8,8,128]{3,2,1,0:T(8,128)} %cu.1, f32[3,8,8,128]{3,2,1,0:T(8,128)} %cp.1, ...), custom_call_target="tpu_custom_call" | custom-call | bytes 1196032 | tf_op jit(solution)/shard_map/pallas_call | solution.py:669
  2.0 1.3 %collective-permute-start.2 = (f32[240,128]{1,0:T(8,128)S(1)}, f32[240,128]{1,0:T(8,128)S(1)}, u32[]{:S(2)}, u32[]{:S(2)}) collective-permute-start(f32[240,128]{1,0:T(8,128)S(1)} %get-tuple-element.21), channel_id=1, source_target_pairs={{0,8},{8,0},{16,24},{24,16},{1,9},{9,1},{17,25},{25,17},{2,10},{10... | collective-permute-start | bytes 368648 | tf_op jit(solution)/shard_map/ppermute | solution.py:653
  3.3 2.1 %collective-permute-start.3 = (f32[240,128]{1,0:T(8,128)S(1)}, f32[240,128]{1,0:T(8,128)S(1)}, u32[]{:S(2)}, u32[]{:S(2)}) collective-permute-start(f32[240,128]{1,0:T(8,128)S(1)} %get-tuple-element.22), channel_id=1, source_target_pairs={{8,16},{16,8},{9,17},{17,9},{10,18},{18,10},{11,19},{19,11},{12,20... | collective-permute-start | bytes 368648 | tf_op jit(solution)/shard_map/ppermute | solution.py:653
  5.4 0.2 shard_map.78
  5.6 0.7 %collective-permute-done.2.got_even = f32[240,128]{1,0:T(8,128)S(1)} collective-permute-done((f32[240,128]{1,0:T(8,128)S(1)}, f32[240,128]{1,0:T(8,128)S(1)}, u32[]{:S(2)}, u32[]{:S(2)}) %collective-permute-start.2) | collective-permute-done | bytes 122912 | tf_op jit(solution)/shard_map/ppermute | solution.py:653
  6.3 3.5 %collective-permute-done.3.got_odd = f32[240,128]{1,0:T(8,128)S(1)} collective-permute-done((f32[240,128]{1,0:T(8,128)S(1)}, f32[240,128]{1,0:T(8,128)S(1)}, u32[]{:S(2)}, u32[]{:S(2)}) %collective-permute-start.3) | collective-permute-done | bytes 122912 | tf_op jit(solution)/shard_map/ppermute | solution.py:653
  9.8 0.9 %shard_map.79 = (f32[200,8,128]{2,1,0:T(8,128)S(1)}, f32[40,128]{1,0:T(8,128)S(1)}, f32[40,128]{1,0:T(8,128)S(1)}) custom-call(f32[10,16,128]{2,1,0:T(8,128)S(1)} %get-tuple-element.19.fine_ends, f32[9,8,128]{2,1,0:T(8,128)S(1)} %get-tuple-element.20.coarse_ends, f32[240,128]{1,0:T(8,128)S(1)} %collective-permute-done.2.got_even, ...), custom_call_target="tpu_custom_call" | custom-call | bytes 860160 | tf_op jit(solution)/shard_map/pallas_call | solution.py:669
  10.7 2.2 %collective-permute-start.4 = (f32[200,8,128]{2,1,0:T(8,128)S(1)}, f32[200,8,128]{2,1,0:T(8,128)S(1)}, u32[]{:S(2)}, u32[]{:S(2)}) collective-permute-start(f32[200,8,128]{2,1,0:T(8,128)S(1)} %get-tuple-element.23.own_b), channel_id=1, source_target_pairs={{0,1},{1,0},{2,3},{3,2},{4,5},{5,4},{6,7},{7,6},{8,9},{9,8},{10,11... | collective-permute-start | bytes 2457608 | tf_op jit(solution)/shard_map/ppermute | solution.py:653
  12.9 0.1 collective-permute-start
  13.0 0.4 %collective-permute-start.1 = (f32[9,8,8,128]{3,2,1,0:T(8,128)S(1)}, f32[9,8,8,128]{3,2,1,0:T(8,128)S(1)}, u32[]{:S(2)}, u32[]{:S(2)}) collective-permute-start(f32[9,8,8,128]{3,2,1,0:T(8,128)S(1)} %get-tuple-element.18.coarse.own_c), channel_id=1, source_target_pairs={{0,1},{1,0},{2,3},{3,2},{4,5},{5,4},{6,7},{7,6},{8,9},{9,8},{10,11... | collective-permute-start | bytes 884744 | tf_op jit(solution)/shard_map/ppermute | solution.py:653
  13.4 1.3 %collective-permute-start.5 = (f32[40,128]{1,0:T(8,128)S(1)}, f32[40,128]{1,0:T(8,128)S(1)}, u32[]{:S(2)}, u32[]{:S(2)}) collective-permute-start(f32[40,128]{1,0:T(8,128)S(1)} %get-tuple-element.30), channel_id=1, source_target_pairs={{0,2},{2,0},{4,6},{6,4},{1,3},{3,1},{5,7},{7,5},{8,10},{10,8},{12,... | collective-permute-start | bytes 61448 | tf_op jit(solution)/shard_map/ppermute | solution.py:653
  14.7 1.9 %collective-permute-start.6 = (f32[40,128]{1,0:T(8,128)S(1)}, f32[40,128]{1,0:T(8,128)S(1)}, u32[]{:S(2)}, u32[]{:S(2)}) collective-permute-start(f32[40,128]{1,0:T(8,128)S(1)} %get-tuple-element.31), channel_id=1, source_target_pairs={{2,4},{4,2},{3,5},{5,3},{10,12},{12,10},{11,13},{13,11},{18,20},{2... | collective-permute-start | bytes 61448 | tf_op jit(solution)/shard_map/ppermute | solution.py:653
  16.6 0.0 collective-permute-done.5.own_ye
  16.6 0.6 %collective-permute-start.7 = (f32[40,128]{1,0:T(8,128)S(1)}, f32[40,128]{1,0:T(8,128)S(1)}, u32[]{:S(2)}, u32[]{:S(2)}) collective-permute-start(f32[40,128]{1,0:T(8,128)S(1)} %collective-permute-done.5.own_ye), channel_id=1, source_target_pairs={{0,1},{1,0},{2,3},{3,2},{4,5},{5,4},{6,7},{7,6},{8,9},{9,8},{10,11... | collective-permute-start | bytes 61448 | tf_op jit(solution)/shard_map/ppermute | solution.py:653
  17.3 1.9 %collective-permute-done.6.own_yo = f32[40,128]{1,0:T(8,128)S(1)} collective-permute-done((f32[40,128]{1,0:T(8,128)S(1)}, f32[40,128]{1,0:T(8,128)S(1)}, u32[]{:S(2)}, u32[]{:S(2)}) %collective-permute-start.6) | collective-permute-done | bytes 20512 | tf_op jit(solution)/shard_map/ppermute | solution.py:653
  19.2 1.5 %collective-permute-start.8 = (f32[40,128]{1,0:T(8,128)S(1)}, f32[40,128]{1,0:T(8,128)S(1)}, u32[]{:S(2)}, u32[]{:S(2)}) collective-permute-start(f32[40,128]{1,0:T(8,128)S(1)} %collective-permute-done.6.own_yo), channel_id=1, source_target_pairs={{0,1},{1,0},{2,3},{3,2},{4,5},{5,4},{6,7},{7,6},{8,9},{9,8},{10,11... | collective-permute-start | bytes 61448 | tf_op jit(solution)/shard_map/ppermute | solution.py:653
  20.7 0.0 collective-permute-done.1.far_c
  20.7 0.0 collective-permute-done.far_f
  20.8 0.0 collective-permute-done.4.far_b
  20.8 1.1 %shard_map.80 = (f32[3,8,24,256]{3,2,1,0:T(8,128)S(1)}, f32[3,16,16,128]{3,2,1,0:T(8,128)S(1)}) custom-call(f32[10,4,16,256]{3,2,1,0:T(8,128)S(1)} %get-tuple-element.17.fine.own_f, f32[9,8,8,128]{3,2,1,0:T(8,128)S(1)} %get-tuple-element.18.coarse.own_c, f32[10,4,16,256]{3,2,1,0:T(8,128)S(1)} %collective-permute-done.far_f, ...), custom_call_target="tpu_custom_call" | custom-call | flops 2000000 | bytes 983040 | tf_op jit(solution)/shard_map/pallas_call | solution.py:669
  21.8 0.7 %shard_map.81 = (f32[3,4,16,256]{3,2,1,0:T(8,128)S(1)}, f32[3,8,8,128]{3,2,1,0:T(8,128)S(1)}, f32[10,24,256]{2,1,0:T(8,128)S(1)}, f32[9,16,256]{2,1,0:T(8,128)S(1)}) custom-call(f32[10,4,16,256]{3,2,1,0:T(8,128)S(1)} %get-tuple-element.17.fine.own_f, f32[9,8,8,128]{3,2,1,0:T(8,128)S(1)} %get-tuple-element.18.coarse.own_c, ...), custom_call_target="tpu_custom_call" | custom-call | flops 2000000 | bytes 688128 | tf_op jit(solution)/shard_map/pallas_call | solution.py:669
  22.6 0.0 collective-permute-done.7.far_ye
  22.6 0.0 collective-permute-done.8.far_yo
  22.6 2.1 %shard_map.82 = (f32[3,4,16,256]{3,2,1,0:T(8,128)}, f32[3,8,8,128]{3,2,1,0:T(8,128)}) custom-call(f32[10,24,256]{2,1,0:T(8,128)S(1)} %get-tuple-element.26.strip_f, f32[9,16,256]{2,1,0:T(8,128)S(1)} %get-tuple-element.27.strip_c, f32[3,4,16,256]{3,2,1,0:T(8,128)S(1)} %get-tuple-element.28.main_f, f32[3,8,8,128]{3,2,1,0:T(8,128)S(1)} %get-tuple-element.29.main_c, ...), custom_call_target="tpu_custom_call" | custom-call | bytes 294912 | tf_op jit(solution)/shard_map/pallas_call | solution.py:669
Async XLA Ops:
  2.0 4.3 %collective-permute-start.2 = (f32[240,128]{1,0:T(8,128)S(1)}, f32[240,128]{1,0:T(8,128)S(1)}, u32[]{:S(2)}, u32[]{:S(2)}) collective-permute-start(f32[240,128]{1,0:T(8,128)S(1)} %get-tuple-element.21), channel_id=1, source_target_pairs={{0,8},{8,0},{16,24},{24,16},{1,9},{9,1},{17,25},{25,17},{2,10},{10... | collective-permute-start | bytes 368648 | tf_op jit(solution)/shard_map/ppermute | solution.py:653
  3.3 6.5 %collective-permute-start.3 = (f32[240,128]{1,0:T(8,128)S(1)}, f32[240,128]{1,0:T(8,128)S(1)}, u32[]{:S(2)}, u32[]{:S(2)}) collective-permute-start(f32[240,128]{1,0:T(8,128)S(1)} %get-tuple-element.22), channel_id=1, source_target_pairs={{8,16},{16,8},{9,17},{17,9},{10,18},{18,10},{11,19},{19,11},{12,20... | collective-permute-start | bytes 368648 | tf_op jit(solution)/shard_map/ppermute | solution.py:653
  10.7 10.0 %collective-permute-start.4 = (f32[200,8,128]{2,1,0:T(8,128)S(1)}, f32[200,8,128]{2,1,0:T(8,128)S(1)}, u32[]{:S(2)}, u32[]{:S(2)}) collective-permute-start(f32[200,8,128]{2,1,0:T(8,128)S(1)} %get-tuple-element.23.own_b), channel_id=1, source_target_pairs={{0,1},{1,0},{2,3},{3,2},{4,5},{5,4},{6,7},{7,6},{8,9},{9,8},{10,11... | collective-permute-start | bytes 2457608 | tf_op jit(solution)/shard_map/ppermute | solution.py:653
  12.9 7.8 %collective-permute-start = (f32[10,4,16,256]{3,2,1,0:T(8,128)S(1)}, f32[10,4,16,256]{3,2,1,0:T(8,128)S(1)}, u32[]{:S(2)}, u32[]{:S(2)}) collective-permute-start(f32[10,4,16,256]{3,2,1,0:T(8,128)S(1)} %get-tuple-element.17.fine.own_f), channel_id=1, source_target_pairs={{0,1},{1,0},{2,3},{3,2},{4,5},{5,4},{6,7},{7,6},{8,9},{9,8},{10,11... | collective-permute-start | bytes 1966088 | tf_op jit(solution)/shard_map/ppermute | solution.py:653
  13.0 7.8 %collective-permute-start.1 = (f32[9,8,8,128]{3,2,1,0:T(8,128)S(1)}, f32[9,8,8,128]{3,2,1,0:T(8,128)S(1)}, u32[]{:S(2)}, u32[]{:S(2)}) collective-permute-start(f32[9,8,8,128]{3,2,1,0:T(8,128)S(1)} %get-tuple-element.18.coarse.own_c), channel_id=1, source_target_pairs={{0,1},{1,0},{2,3},{3,2},{4,5},{5,4},{6,7},{7,6},{8,9},{9,8},{10,11... | collective-permute-start | bytes 884744 | tf_op jit(solution)/shard_map/ppermute | solution.py:653
  13.4 3.2 %collective-permute-start.5 = (f32[40,128]{1,0:T(8,128)S(1)}, f32[40,128]{1,0:T(8,128)S(1)}, u32[]{:S(2)}, u32[]{:S(2)}) collective-permute-start(f32[40,128]{1,0:T(8,128)S(1)} %get-tuple-element.30), channel_id=1, source_target_pairs={{0,2},{2,0},{4,6},{6,4},{1,3},{3,1},{5,7},{7,5},{8,10},{10,8},{12,... | collective-permute-start | bytes 61448 | tf_op jit(solution)/shard_map/ppermute | solution.py:653
  14.7 4.5 %collective-permute-start.6 = (f32[40,128]{1,0:T(8,128)S(1)}, f32[40,128]{1,0:T(8,128)S(1)}, u32[]{:S(2)}, u32[]{:S(2)}) collective-permute-start(f32[40,128]{1,0:T(8,128)S(1)} %get-tuple-element.31), channel_id=1, source_target_pairs={{2,4},{4,2},{3,5},{5,3},{10,12},{12,10},{11,13},{13,11},{18,20},{2... | collective-permute-start | bytes 61448 | tf_op jit(solution)/shard_map/ppermute | solution.py:653
  16.6 5.9 %collective-permute-start.7 = (f32[40,128]{1,0:T(8,128)S(1)}, f32[40,128]{1,0:T(8,128)S(1)}, u32[]{:S(2)}, u32[]{:S(2)}) collective-permute-start(f32[40,128]{1,0:T(8,128)S(1)} %collective-permute-done.5.own_ye), channel_id=1, source_target_pairs={{0,1},{1,0},{2,3},{3,2},{4,5},{5,4},{6,7},{7,6},{8,9},{9,8},{10,11... | collective-permute-start | bytes 61448 | tf_op jit(solution)/shard_map/ppermute | solution.py:653
  19.2 3.4 %collective-permute-start.8 = (f32[40,128]{1,0:T(8,128)S(1)}, f32[40,128]{1,0:T(8,128)S(1)}, u32[]{:S(2)}, u32[]{:S(2)}) collective-permute-start(f32[40,128]{1,0:T(8,128)S(1)} %collective-permute-done.6.own_yo), channel_id=1, source_target_pairs={{0,1},{1,0},{2,3},{3,2},{4,5},{5,4},{6,7},{7,6},{8,9},{9,8},{10,11... | collective-permute-start | bytes 61448 | tf_op jit(solution)/shard_map/ppermute | solution.py:653

commit v5 on v4

--- a/solution.py
+++ b/solution.py
@@ -129,21 +129,27 @@
     def __init__(self, fine_shape, coarse_shape):
         self.layers = fine_shape[1], coarse_shape[1]
         self.parts = fine_shape[3] // LANES, coarse_shape[3] // LANES
-        self.rows = fine_shape[2] // 8 + 1, coarse_shape[2] // 8 + 1
-        self.halo_base, self.ends_base, at = [], [], 0
+        self.rows = fine_shape[2] // 8, coarse_shape[2] // 8
+        self.halo_base, self.ends_base, self.inner_base, at, inner = [], [], [], 0, 0
         for grid, fields in enumerate((FINE_FIELDS, COARSE_FIELDS)):
             self.halo_base.append(at)
             at += fields * self.layers[grid] * self.parts[grid]
             self.ends_base.append(at)
-            at += fields * self.rows[grid]
-        self.size = at
+            at += fields
+            self.inner_base.append(inner)
+            inner += fields * self.rows[grid]
+        self.size, self.inner_size = at, inner
+        self.halo_fields = FINE_FIELDS, COARSE_FIELDS
 
     def halo(self, grid, field, layer, part):
         return self.halo_base[grid] + (field * self.layers[grid] + layer) * self.parts[grid] + part
 
-    def ends(self, ref, grid, field):
-        base = self.ends_base[grid] + field * self.rows[grid]
-        return jnp.concatenate([ref[base + r] for r in range(self.rows[grid])], axis=0)
+    def inner(self, grid, field, row):
+        return self.inner_base[grid] + field * self.rows[grid] + row
+
+    def ends(self, inner, tiles, grid, field):
+        own = [inner[self.inner(grid, field, r)] for r in range(self.rows[grid])]
+        return jnp.concatenate(own + [tiles[self.ends_base[grid] + field]], axis=0)
 
 
 def end_columns(read, layers, span):
@@ -156,17 +162,49 @@
     return total
 
 
-def pack_inner_kernel(fine, coarse, fine_ends, coarse_ends):
-    for ref, out, span in ((fine, fine_ends, FINE_SPAN), (coarse, coarse_ends, COARSE_SPAN)):
+def packed_columns(table, ends_of, span):
+    sides = [[None, None], [None, None]]
+    for field, layer, high, low, slot in sorted(table, key=lambda entry: entry[4]):
+        if layer:
+            continue
+        ends = ends_of(field)
+        lane = lax.broadcasted_iota(jnp.int32, ends.shape, 1)
+        within = jnp.bitwise_and(lane, span - 1)
+        half, start = divmod(slot, LANES // 2)
+        for side, first in enumerate((span // 2, span // 2 - low)):
+            shift = (slot - first) % LANES
+            value = pltpu.roll(ends, shift, 1) if shift else ends
+            before = sides[side][half]
+            sides[side][half] = (
+                value if before is None else jnp.where(within >= start, value, before)
+            )
+    return [jnp.where(lane < LANES // 2, lower, upper) for lower, upper in sides]
+
+
+SPANS = FINE_SPAN, COARSE_SPAN
+
+
+def pack_inner_kernel(bundle, fine, coarse, inner, firsts_ref, lasts_ref):
+    at = 0
+    for grid, (table, ref) in enumerate(zip(tables(*bundle.layers), (fine, coarse))):
+        fields = []
         for field in range(ref.shape[0]):
 
             def read(layer):
                 return ref[field, layer, :, :LANES], ref[field, layer, :, ref.shape[3] - LANES :]
 
-            out[field] = end_columns(read, ref.shape[1], span)
-
-
-def pack_y_kernel(bundle, fine_ends, coarse_ends, got_even, got_odd, out, to_even, to_odd):
+            ends = end_columns(read, ref.shape[1], SPANS[grid])
+            fields.append(ends)
+            for r in range(bundle.rows[grid]):
+                inner[bundle.inner(grid, field, r)] = ends[r * 8 : (r + 1) * 8]
+        rows = slice(at, at + ref.shape[2])
+        firsts_ref[rows, :], lasts_ref[rows, :] = packed_columns(
+            table, lambda field: fields[field], SPANS[grid]
+        )
+        at += ref.shape[2]
+
+
+def pack_y_kernel(bundle, firsts_ref, lasts_ref, got_even, got_odd, out, to_even, to_odd):
     grids = tables(*bundle.layers), bundle.parts
 
     def halo(high_ref, low_ref):
@@ -179,7 +217,7 @@
 
     for grid, table in enumerate(grids[0]):
         for field, layer, *_ in table:
-            for t in range(bundle.parts[grid]):
+            for t in range(bundle.parts[grid] if field < Q else 0):
                 out[bundle.halo(grid, field, layer, t)] = jnp.zeros((MARGIN, LANES), jnp.float32)
 
     even = lax.rem(lax.axis_index("gx"), 2) == 0
@@ -192,46 +230,33 @@
     def _():
         halo(got_odd, got_even)
 
-    packed = []
-    for grid, (table, inner, span) in enumerate(
-        zip(grids[0], (fine_ends, coarse_ends), (FINE_SPAN, COARSE_SPAN))
-    ):
-        rows = inner.shape[1] + MARGIN
-        lane = lax.broadcasted_iota(jnp.int32, (rows, LANES), 1)
-        within = jnp.bitwise_and(lane, span - 1)
-        sides = [[None, None], [None, None]]
-        for field, layer, high, low, slot in sorted(table, key=lambda entry: entry[4]):
-            if layer:
-                continue
+    packed, at = [], 0
+    for grid, table in enumerate(grids[0]):
+        fields = []
+        for field in range(bundle.halo_fields[grid]):
 
             def read(layer):
                 parts = (0, bundle.parts[grid] - 1)
                 return [out[bundle.halo(grid, field, layer, t)] for t in parts]
 
-            ends = jnp.concatenate(
-                [inner[field], end_columns(read, bundle.layers[grid], span)], axis=0
-            )
-            base = bundle.ends_base[grid] + field * bundle.rows[grid]
-            for r in range(bundle.rows[grid]):
-                out[base + r] = ends[r * 8 : (r + 1) * 8]
-            half, start = divmod(slot, LANES // 2)
-            for side, first in enumerate((span // 2, span // 2 - low)):
-                shift = (slot - first) % LANES
-                value = pltpu.roll(ends, shift, 1) if shift else ends
-                before = sides[side][half]
-                sides[side][half] = (
-                    value if before is None else jnp.where(within >= start, value, before)
-                )
-        packed.append([jnp.where(lane < LANES // 2, lower, upper) for lower, upper in sides])
+            ends = end_columns(read, bundle.layers[grid], SPANS[grid])
+            fields.append(ends)
+            out[bundle.ends_base[grid] + field] = ends
+        columns = packed_columns(table, lambda field: fields[field], SPANS[grid])
+        rows = slice(at, at + 8 * bundle.rows[grid])
+        packed.append((rows, columns))
+        at = rows.stop
     even_y = lax.rem(lax.axis_index("gy"), 2) == 0
 
     def place(first_out, last_out):
         at = 0
-        for firsts, lasts in packed:
-            rows = slice(at, at + firsts.shape[0])
-            first_out[rows, :] = firsts
-            last_out[rows, :] = lasts
-            at += firsts.shape[0]
+        for rows, (firsts, lasts) in packed:
+            size = rows.stop - rows.start
+            first_out[at : at + size, :] = firsts_ref[rows, :]
+            last_out[at : at + size, :] = lasts_ref[rows, :]
+            first_out[at + size : at + size + MARGIN, :] = firsts
+            last_out[at + size : at + size + MARGIN, :] = lasts
+            at += size + MARGIN
 
     @pl.when(even_y)
     def _():
@@ -486,7 +511,8 @@
 
 
 def second_kernel(
-    bundle, own_f, own_c, far_f, far_c, own_b, far_b, state_f, state_c, out_f, out_c, strip_f, strip_c
+    bundle, own_f, own_c, far_f, far_c, own_b, far_b, own_i, far_i, state_f, state_c,
+    out_f, out_c, strip_f, strip_c,
 ):
     grids = tile_grids(own_f, own_c)
 
@@ -501,7 +527,8 @@
     for grid, (strip, span) in enumerate(((strip_f, FINE_SPAN), (strip_c, COARSE_SPAN))):
         lane = lax.broadcasted_iota(jnp.int32, (strip.shape[1], LANES), 1)
         for field in range(strip.shape[0]):
-            own, far = bundle.ends(own_b, grid, field), bundle.ends(far_b, grid, field)
+            own = bundle.ends(own_i, own_b, grid, field)
+            far = bundle.ends(far_i, far_b, grid, field)
             upper, lower = jnp.where(top, own, far), jnp.where(top, far, own)
             whole = jnp.where(lane < LANES // 2, upper, pltpu.roll(lower, LANES // 2, 1))
             strip[field, :, :LANES] = pltpu.roll(whole, LANES - span // 4, 1)
@@ -509,7 +536,8 @@
 
 
 def strip_kernel(
-    strip_f, strip_c, main_f, main_c, own_ye, own_yo, far_ye, far_yo, out_f, out_c
+    strip_f, strip_c, main_f, main_c, own_ye, own_yo, far_ye, far_yo, out_f, out_c,
+    stage_f, stage_c, sems,
 ):
     layers, n, width = main_f.shape[1:]
     clayers, nc, cwidth = main_c.shape[1:]
@@ -583,12 +611,52 @@
     fine = filled(fine_table, strip_f, 0, FINE_SPAN)
     coarse = filled(coarse_table, strip_c, height, COARSE_SPAN)
 
-    def fine_lane(f):
-        tile, inner = jnp.bitwise_and(f, LANES), jnp.bitwise_and(f, LANES - 1)
-        bottom = inner - (depth - 1) * FINE_SPAN
-        return jnp.where(bottom >= 0, tile + jnp.right_shift(bottom, 1), -1)
-
-    grids = Grids(height, cheight, wide, wide, fine_lane)
+    def gather(value, index, axis):
+        return jnp.take_along_axis(value, index, axis=axis)
+
+    row = lax.broadcasted_iota(jnp.int32, (8, LANES), 0)
+    lane = lax.broadcasted_iota(jnp.int32, (8, LANES), 1)
+    bottom = (depth - 1) * FINE_SPAN
+    up_lane = jnp.right_shift(jnp.maximum(lane - bottom, 0), 1)
+    down_lane = jnp.minimum(lane * 2 + bottom, LANES - 2)
+
+    def blocks(plane):
+        return [
+            [plane[r : r + 8, t : t + LANES] for r in range(0, plane.shape[0], 8)]
+            for t in range(0, wide, LANES)
+        ]
+
+    def joined(tiles):
+        return jnp.concatenate([jnp.concatenate(column, axis=0) for column in tiles], axis=1)
+
+    def prolong(plane):
+        tiles = []
+        for column in blocks(plane):
+            column = [gather(block, up_lane, 1) for block in column]
+            out = [
+                gather(column[b // 2], jnp.right_shift(row, 1) + 4 * (b % 2), 0)
+                for b in range(n // 8)
+            ]
+            edge = jnp.right_shift(row, 1) + jnp.where(row < 4, 0, 4)
+            tiles.append(out + [gather(column[-1], edge, 0)])
+        return joined(tiles)
+
+    def restrict(plane):
+        def pair_rows(block, index):
+            return gather(block, index, 0) + gather(block, index + 1, 0)
+
+        tiles = []
+        for column in blocks(plane):
+            column = [gather(f, down_lane, 1) + gather(f, down_lane + 1, 1) for f in column]
+            low, high = jnp.minimum(row * 2, 6), jnp.maximum(row * 2 - 8, 0)
+            out = [
+                jnp.where(row < 4, pair_rows(column[2 * b], low), pair_rows(column[2 * b + 1], high))
+                for b in range(nc // 8)
+            ]
+            edge = jnp.where(row < 2, row * 2, jnp.maximum(row * 2 - 8, 0))
+            tiles.append(out + [pair_rows(column[-1], edge)])
+        return 0.25 * joined(tiles)
+
     scale = jnp.float32(time_step * time_step)
 
     def shifted(value, lanes):
@@ -598,8 +666,8 @@
         return [jnp.where(at_top, a, shifted(stress[k], lanes)) for k, a in zip((2, 4, 5), above)]
 
     def step(u, p, v, q):
-        ghost_f = grids.prolong(v)
-        ghost_c = grids.restrict(u)
+        ghost_f = [prolong(f) for f in v]
+        ghost_c = [restrict(f) for f in u]
         below = [jnp.where(fg == depth - 1, b, shifted(f, -FINE_SPAN)) for f, b in zip(u, ghost_f)]
         stress = stress_of(u, below, [fine[k] for k in (MU, LAM, W)], True)
         up = lift(stress, FINE_SPAN, fg == 0, [0.0] * 3)
@@ -622,9 +690,10 @@
     next_v = [jnp.where(keep_c, f, 0.0) for f in next_v]
     last_u, last_v = step(next_u, u, next_v, v)
 
-    for values, out, main, span in (
-        (last_u, out_f, main_f, FINE_SPAN),
-        (last_v, out_c, main_c, COARSE_SPAN),
+    copies = []
+    for values, result, out, main, span in (
+        (last_u, out_f, stage_f, main_f, FINE_SPAN),
+        (last_v, out_c, stage_c, main_c, COARSE_SPAN),
     ):
         cells, extent = out.shape[2:]
         room = span // 4
@@ -642,6 +711,10 @@
                     if start == extent - LANES:
                         part = jnp.where(lane >= LANES - room, final, part)
                     out[k, l, :, start : start + LANES] = part
+            copies.append(pltpu.make_async_copy(out.at[k], result.at[k], sems.at[len(copies)]))
+            copies[-1].start()
+    for copy in copies:
+        copy.wait()
 
 
 def partners(count, parity):
@@ -653,13 +726,15 @@
     return lax.ppermute(value, axis, partners(lax.axis_size(axis), parity))
 
 
-def call(kernel, out_shape, operands, scratch=(), flops=0, space=pltpu.VMEM, limit=24):
+def call(
+    kernel, out_shape, operands, scratch=(), flops=0, space=pltpu.VMEM, to=pltpu.VMEM, limit=24
+):
     size = sum(o.size for o in out_shape) * 4
     call = pl.pallas_call(
         kernel,
         out_shape=out_shape,
         in_specs=[pl.BlockSpec(memory_space=space)] * len(operands),
-        out_specs=[pl.BlockSpec(memory_space=pltpu.VMEM)] * len(out_shape),
+        out_specs=[pl.BlockSpec(memory_space=to)] * len(out_shape),
         scratch_shapes=list(scratch),
         cost_estimate=pl.CostEstimate(flops=flops, bytes_accessed=size, transcendentals=0),
         compiler_params=pltpu.CompilerParams(vmem_limit_bytes=limit * 1024 * 1024),
@@ -693,18 +768,20 @@
     got_even = swap(to_even, "gx", 0)
     far_f, far_c = swap(own_f, "dev", 0), swap(own_c, "dev", 0)
 
-    fine_ends, coarse_ends = call(
-        pack_inner_kernel,
-        (shape(FINE_FIELDS, n, LANES), shape(COARSE_FIELDS, nc, LANES)),
+    bundle = Bundle(inputs[0].shape, inputs[3].shape)
+    inner = shape(n + nc, LANES)
+    own_i, firsts, lasts = call(
+        functools.partial(pack_inner_kernel, bundle),
+        (shape(bundle.inner_size, 8, LANES), inner, inner),
         (own_f, own_c),
     )
-
-    bundle = Bundle(inputs[0].shape, inputs[3].shape)
+    far_i = swap(own_i, "dev", 0)
+
     side = shape(height + cheight, LANES)
     own_b, to_even, to_odd = call(
         functools.partial(pack_y_kernel, bundle),
         (shape(bundle.size, 8, LANES), side, side),
-        (fine_ends, coarse_ends, got_even, got_odd),
+        (firsts, lasts, got_even, got_odd),
     )
     own_yo = swap(to_odd, "gy", 1)
     own_ye = swap(to_even, "gy", 0)
@@ -725,12 +802,17 @@
     main_f, main_c, strip_f, strip_c = call(
         functools.partial(second_kernel, bundle),
         results + strips,
-        tiles + tuple(states),
+        tiles + (own_i, far_i) + tuple(states),
         flops=STEP_FLOPS,
     )
     far_yo, far_ye = swap(own_yo, "dev", 0), swap(own_ye, "dev", 0)
     return call(
-        strip_kernel, results, (strip_f, strip_c, main_f, main_c, own_ye, own_yo, far_ye, far_yo)
+        strip_kernel,
+        results,
+        (strip_f, strip_c, main_f, main_c, own_ye, own_yo, far_ye, far_yo),
+        scratch=tuple(pltpu.VMEM(r.shape, jnp.float32) for r in results)
+        + (pltpu.SemaphoreType.DMA((6,)),),
+        to=pltpu.HBM,
     )
 
 

time: 24.9 us -> 27.1 us (1.088)
  waiting for transfers between devices: 6.14 us -> 7.82 us
  starting transfers between devices: 11.4 us -> 12.2 us
  Pallas kernels: 6.45 us -> 6.15 us
    ppermute x9 -> x10, waiting for transfers between devices: 6.14 us -> 7.82 us  [swap(): return lax.ppermute(value, axis, partners(lax.axis_size(axis), parity))]
    ppermute x9 -> x10, starting transfers between devices: 11.4 us -> 12.2 us  [swap(): return lax.ppermute(value, axis, partners(lax.axis_size(axis), parity))]
    pallas_call x6, Pallas kernels: 6.45 us -> 6.15 us  [call(): return call(*operands)]
  transfers between devices with their start and end apart: 9 -> 10, of which waited for: 3 -> 4; matrix products, arithmetic and copies ran while one was open for 0% -> 0% of each run, Pallas kernels for 8% -> 8%
where the time goes in v5:
time: 27.1 us; the launch traced here: 26.9 us
  starting transfers between devices  12.2 us (45%)
  waiting for transfers between devices  7.82 us (29%)
  Pallas kernels  6.15 us (23%)
  between operations  0.71 us (3%)
    ppermute x10, starting transfers between devices, swap(): return lax.ppermute(value, axis, partners(lax.axis_size(axis), parity))  12.2 us
    ppermute x10, waiting for transfers between devices, swap(): return lax.ppermute(value, axis, partners(lax.axis_size(axis), parity))  7.82 us
    pallas_call x6, Pallas kernels, call(): return call(*operands)  6.15 us
  transfers between devices with their start and end apart: 10, of which 4 were waited for; matrix products, arithmetic and copies ran while one was open for 0% of the time, Pallas kernels for 8%

profile of v5, /device:TPU:21, one launch (start us, length us, event | category | flops | bytes accessed | tf_op | source)
XLA Modules:
  0.0 26.9 jit_solution(15483372955044296868)
XLA Ops:
  0.6 1.4 %shard_map.77 = (f32[10,4,16,256]{3,2,1,0:T(8,128)S(1)}, f32[9,8,8,128]{3,2,1,0:T(8,128)S(1)}, f32[240,128]{1,0:T(8,128)S(1)}, f32[240,128]{1,0:T(8,128)S(1)}) custom-call(f32[3,4,16,256]{3,2,1,0:T(8,128)} %fu.1, f32[3,4,16,256]{3,2,1,0:T(8,128)} %fp.1, f32[4,4,16,256]{3,2,1,0:T(8,128)} %fm.1, f32[3,8,8,128]{3,2,1,0:T(8,128)} %cu.1, f32[3,8,8,128]{3,2,1,0:T(8,128)} %cp.1, ...), custom_call_target="tpu_custom_call" | custom-call | bytes 1196032 | tf_op jit(solution)/shard_map/pallas_call | solution.py:744
  2.0 1.3 %collective-permute-start.2 = (f32[240,128]{1,0:T(8,128)S(1)}, f32[240,128]{1,0:T(8,128)S(1)}, u32[]{:S(2)}, u32[]{:S(2)}) collective-permute-start(f32[240,128]{1,0:T(8,128)S(1)} %get-tuple-element.22), channel_id=1, source_target_pairs={{0,8},{8,0},{16,24},{24,16},{1,9},{9,1},{17,25},{25,17},{2,10},{10... | collective-permute-start | bytes 368648 | tf_op jit(solution)/shard_map/ppermute | solution.py:726
  3.3 2.1 %collective-permute-start.3 = (f32[240,128]{1,0:T(8,128)S(1)}, f32[240,128]{1,0:T(8,128)S(1)}, u32[]{:S(2)}, u32[]{:S(2)}) collective-permute-start(f32[240,128]{1,0:T(8,128)S(1)} %get-tuple-element.23), channel_id=1, source_target_pairs={{8,16},{16,8},{9,17},{17,9},{10,18},{18,10},{11,19},{19,11},{12,20... | collective-permute-start | bytes 368648 | tf_op jit(solution)/shard_map/ppermute | solution.py:726
  5.4 0.4 %shard_map.78 = (f32[29,8,128]{2,1,0:T(8,128)S(1)}, f32[24,128]{1,0:T(8,128)S(1)}, f32[24,128]{1,0:T(8,128)S(1)}) custom-call(f32[10,4,16,256]{3,2,1,0:T(8,128)S(1)} %get-tuple-element.18.fine.own_f, f32[9,8,8,128]{3,2,1,0:T(8,128)S(1)} %get-tuple-element.19.coarse.own_c), custom_call_target="tpu_custom_call" | custom-call | bytes 143360 | tf_op jit(solution)/shard_map/pallas_call | solution.py:744
  5.8 0.5 %collective-permute-done.2.got_even = f32[240,128]{1,0:T(8,128)S(1)} collective-permute-done((f32[240,128]{1,0:T(8,128)S(1)}, f32[240,128]{1,0:T(8,128)S(1)}, u32[]{:S(2)}, u32[]{:S(2)}) %collective-permute-start.2) | collective-permute-done | bytes 122912 | tf_op jit(solution)/shard_map/ppermute | solution.py:726
  6.3 3.5 %collective-permute-done.3.got_odd = f32[240,128]{1,0:T(8,128)S(1)} collective-permute-done((f32[240,128]{1,0:T(8,128)S(1)}, f32[240,128]{1,0:T(8,128)S(1)}, u32[]{:S(2)}, u32[]{:S(2)}) %collective-permute-start.3) | collective-permute-done | bytes 122912 | tf_op jit(solution)/shard_map/ppermute | solution.py:726
  9.8 0.5 %shard_map.79 = (f32[171,8,128]{2,1,0:T(8,128)S(1)}, f32[40,128]{1,0:T(8,128)S(1)}, f32[40,128]{1,0:T(8,128)S(1)}) custom-call(f32[24,128]{1,0:T(8,128)S(1)} %get-tuple-element.20.firsts_ref, f32[24,128]{1,0:T(8,128)S(1)} %get-tuple-element.21.lasts_ref, f32[240,128]{1,0:T(8,128)S(1)} %collective-permute-done.2.got_even, ...), custom_call_target="tpu_custom_call" | custom-call | bytes 741376 | tf_op jit(solution)/shard_map/pallas_call | solution.py:744
  10.3 2.2 %collective-permute-start.4 = (f32[171,8,128]{2,1,0:T(8,128)S(1)}, f32[171,8,128]{2,1,0:T(8,128)S(1)}, u32[]{:S(2)}, u32[]{:S(2)}) collective-permute-start(f32[171,8,128]{2,1,0:T(8,128)S(1)} %get-tuple-element.24.own_b), channel_id=1, source_target_pairs={{0,1},{1,0},{2,3},{3,2},{4,5},{5,4},{6,7},{7,6},{8,9},{9,8},{10,11... | collective-permute-start | bytes 2101256 | tf_op jit(solution)/shard_map/ppermute | solution.py:726
  12.4 0.1 collective-permute-start
  12.5 0.4 %collective-permute-start.1 = (f32[9,8,8,128]{3,2,1,0:T(8,128)S(1)}, f32[9,8,8,128]{3,2,1,0:T(8,128)S(1)}, u32[]{:S(2)}, u32[]{:S(2)}) collective-permute-start(f32[9,8,8,128]{3,2,1,0:T(8,128)S(1)} %get-tuple-element.19.coarse.own_c), channel_id=1, source_target_pairs={{0,1},{1,0},{2,3},{3,2},{4,5},{5,4},{6,7},{7,6},{8,9},{9,8},{10,11... | collective-permute-start | bytes 884744 | tf_op jit(solution)/shard_map/ppermute | solution.py:726
  13.0 0.1 collective-permute-start.5
  13.0 1.3 %collective-permute-start.6 = (f32[40,128]{1,0:T(8,128)S(1)}, f32[40,128]{1,0:T(8,128)S(1)}, u32[]{:S(2)}, u32[]{:S(2)}) collective-permute-start(f32[40,128]{1,0:T(8,128)S(1)} %get-tuple-element.32), channel_id=1, source_target_pairs={{0,2},{2,0},{4,6},{6,4},{1,3},{3,1},{5,7},{7,5},{8,10},{10,8},{12,... | collective-permute-start | bytes 61448 | tf_op jit(solution)/shard_map/ppermute | solution.py:726
  14.3 1.3 %collective-permute-done.6.own_ye = f32[40,128]{1,0:T(8,128)S(1)} collective-permute-done((f32[40,128]{1,0:T(8,128)S(1)}, f32[40,128]{1,0:T(8,128)S(1)}, u32[]{:S(2)}, u32[]{:S(2)}) %collective-permute-start.6) | collective-permute-done | bytes 20512 | tf_op jit(solution)/shard_map/ppermute | solution.py:726
  15.7 2.1 %collective-permute-start.7 = (f32[40,128]{1,0:T(8,128)S(1)}, f32[40,128]{1,0:T(8,128)S(1)}, u32[]{:S(2)}, u32[]{:S(2)}) collective-permute-start(f32[40,128]{1,0:T(8,128)S(1)} %get-tuple-element.33), channel_id=1, source_target_pairs={{2,4},{4,2},{3,5},{5,3},{10,12},{12,10},{11,13},{13,11},{18,20},{2... | collective-permute-start | bytes 61448 | tf_op jit(solution)/shard_map/ppermute | solution.py:726
  17.7 2.4 %collective-permute-done.7.own_yo = f32[40,128]{1,0:T(8,128)S(1)} collective-permute-done((f32[40,128]{1,0:T(8,128)S(1)}, f32[40,128]{1,0:T(8,128)S(1)}, u32[]{:S(2)}, u32[]{:S(2)}) %collective-permute-start.7) | collective-permute-done | bytes 20512 | tf_op jit(solution)/shard_map/ppermute | solution.py:726
  20.2 2.7 %collective-permute-start.8 = (f32[40,128]{1,0:T(8,128)S(1)}, f32[40,128]{1,0:T(8,128)S(1)}, u32[]{:S(2)}, u32[]{:S(2)}) collective-permute-start(f32[40,128]{1,0:T(8,128)S(1)} %collective-permute-done.6.own_ye), channel_id=1, source_target_pairs={{0,1},{1,0},{2,3},{3,2},{4,5},{5,4},{6,7},{7,6},{8,9},{9,8},{10,11... | collective-permute-start | bytes 61448 | tf_op jit(solution)/shard_map/ppermute | solution.py:726
  22.9 0.0 collective-permute-done.1.far_c
  22.9 0.0 collective-permute-start.9
  22.9 0.0 collective-permute-done.far_f
  22.9 0.0 collective-permute-done.4.far_b
  22.9 1.1 %shard_map.80 = (f32[3,8,24,256]{3,2,1,0:T(8,128)S(1)}, f32[3,16,16,128]{3,2,1,0:T(8,128)S(1)}) custom-call(f32[10,4,16,256]{3,2,1,0:T(8,128)S(1)} %get-tuple-element.18.fine.own_f, f32[9,8,8,128]{3,2,1,0:T(8,128)S(1)} %get-tuple-element.19.coarse.own_c, f32[10,4,16,256]{3,2,1,0:T(8,128)S(1)} %collective-permute-done.far_f, ...), custom_call_target="tpu_custom_call" | custom-call | flops 2000000 | bytes 983040 | tf_op jit(solution)/shard_map/pallas_call | solution.py:744
  24.0 0.0 collective-permute-done.5.far_i
  24.1 0.8 %shard_map.81 = (f32[3,4,16,256]{3,2,1,0:T(8,128)S(1)}, f32[3,8,8,128]{3,2,1,0:T(8,128)S(1)}, f32[10,24,256]{2,1,0:T(8,128)S(1)}, f32[9,16,256]{2,1,0:T(8,128)S(1)}) custom-call(f32[10,4,16,256]{3,2,1,0:T(8,128)S(1)} %get-tuple-element.18.fine.own_f, f32[9,8,8,128]{3,2,1,0:T(8,128)S(1)} %get-tuple-element.19.coarse.own_c, ...), custom_call_target="tpu_custom_call" | custom-call | flops 2000000 | bytes 688128 | tf_op jit(solution)/shard_map/pallas_call | solution.py:744
  24.8 0.0 collective-permute-done.8.far_ye
  24.8 0.0 collective-permute-done.9.far_yo
  24.9 2.0 %shard_map.82 = (f32[3,4,16,256]{3,2,1,0:T(8,128)}, f32[3,8,8,128]{3,2,1,0:T(8,128)}) custom-call(f32[10,24,256]{2,1,0:T(8,128)S(1)} %get-tuple-element.28.strip_f, f32[9,16,256]{2,1,0:T(8,128)S(1)} %get-tuple-element.29.strip_c, f32[3,4,16,256]{3,2,1,0:T(8,128)S(1)} %get-tuple-element.30.main_f, f32[3,8,8,128]{3,2,1,0:T(8,128)S(1)} %get-tuple-element.31.main_c, ...), custom_call_target="tpu_custom_call" | custom-call | bytes 294912 | tf_op jit(solution)/shard_map/pallas_call | solution.py:744
Async XLA Ops:
  2.0 4.3 %collective-permute-start.2 = (f32[240,128]{1,0:T(8,128)S(1)}, f32[240,128]{1,0:T(8,128)S(1)}, u32[]{:S(2)}, u32[]{:S(2)}) collective-permute-start(f32[240,128]{1,0:T(8,128)S(1)} %get-tuple-element.22), channel_id=1, source_target_pairs={{0,8},{8,0},{16,24},{24,16},{1,9},{9,1},{17,25},{25,17},{2,10},{10... | collective-permute-start | bytes 368648 | tf_op jit(solution)/shard_map/ppermute | solution.py:726
  3.3 6.5 %collective-permute-start.3 = (f32[240,128]{1,0:T(8,128)S(1)}, f32[240,128]{1,0:T(8,128)S(1)}, u32[]{:S(2)}, u32[]{:S(2)}) collective-permute-start(f32[240,128]{1,0:T(8,128)S(1)} %get-tuple-element.23), channel_id=1, source_target_pairs={{8,16},{16,8},{9,17},{17,9},{10,18},{18,10},{11,19},{19,11},{12,20... | collective-permute-start | bytes 368648 | tf_op jit(solution)/shard_map/ppermute | solution.py:726
  10.3 12.7 %collective-permute-start.4 = (f32[171,8,128]{2,1,0:T(8,128)S(1)}, f32[171,8,128]{2,1,0:T(8,128)S(1)}, u32[]{:S(2)}, u32[]{:S(2)}) collective-permute-start(f32[171,8,128]{2,1,0:T(8,128)S(1)} %get-tuple-element.24.own_b), channel_id=1, source_target_pairs={{0,1},{1,0},{2,3},{3,2},{4,5},{5,4},{6,7},{7,6},{8,9},{9,8},{10,11... | collective-permute-start | bytes 2101256 | tf_op jit(solution)/shard_map/ppermute | solution.py:726
  12.4 10.5 %collective-permute-start = (f32[10,4,16,256]{3,2,1,0:T(8,128)S(1)}, f32[10,4,16,256]{3,2,1,0:T(8,128)S(1)}, u32[]{:S(2)}, u32[]{:S(2)}) collective-permute-start(f32[10,4,16,256]{3,2,1,0:T(8,128)S(1)} %get-tuple-element.18.fine.own_f), channel_id=1, source_target_pairs={{0,1},{1,0},{2,3},{3,2},{4,5},{5,4},{6,7},{7,6},{8,9},{9,8},{10,11... | collective-permute-start | bytes 1966088 | tf_op jit(solution)/shard_map/ppermute | solution.py:726
  12.5 10.4 %collective-permute-start.1 = (f32[9,8,8,128]{3,2,1,0:T(8,128)S(1)}, f32[9,8,8,128]{3,2,1,0:T(8,128)S(1)}, u32[]{:S(2)}, u32[]{:S(2)}) collective-permute-start(f32[9,8,8,128]{3,2,1,0:T(8,128)S(1)} %get-tuple-element.19.coarse.own_c), channel_id=1, source_target_pairs={{0,1},{1,0},{2,3},{3,2},{4,5},{5,4},{6,7},{7,6},{8,9},{9,8},{10,11... | collective-permute-start | bytes 884744 | tf_op jit(solution)/shard_map/ppermute | solution.py:726
  13.0 11.1 %collective-permute-start.5 = (f32[29,8,128]{2,1,0:T(8,128)S(1)}, f32[29,8,128]{2,1,0:T(8,128)S(1)}, u32[]{:S(2)}, u32[]{:S(2)}) collective-permute-start(f32[29,8,128]{2,1,0:T(8,128)S(1)} %get-tuple-element.25.own_i), channel_id=1, source_target_pairs={{0,1},{1,0},{2,3},{3,2},{4,5},{5,4},{6,7},{7,6},{8,9},{9,8},{10,11... | collective-permute-start | bytes 356360 | tf_op jit(solution)/shard_map/ppermute | solution.py:726
  13.0 2.6 %collective-permute-start.6 = (f32[40,128]{1,0:T(8,128)S(1)}, f32[40,128]{1,0:T(8,128)S(1)}, u32[]{:S(2)}, u32[]{:S(2)}) collective-permute-start(f32[40,128]{1,0:T(8,128)S(1)} %get-tuple-element.32), channel_id=1, source_target_pairs={{0,2},{2,0},{4,6},{6,4},{1,3},{3,1},{5,7},{7,5},{8,10},{10,8},{12,... | collective-permute-start | bytes 61448 | tf_op jit(solution)/shard_map/ppermute | solution.py:726
  15.7 4.5 %collective-permute-start.7 = (f32[40,128]{1,0:T(8,128)S(1)}, f32[40,128]{1,0:T(8,128)S(1)}, u32[]{:S(2)}, u32[]{:S(2)}) collective-permute-start(f32[40,128]{1,0:T(8,128)S(1)} %get-tuple-element.33), channel_id=1, source_target_pairs={{2,4},{4,2},{3,5},{5,3},{10,12},{12,10},{11,13},{13,11},{18,20},{2... | collective-permute-start | bytes 61448 | tf_op jit(solution)/shard_map/ppermute | solution.py:726
  20.2 4.7 %collective-permute-start.8 = (f32[40,128]{1,0:T(8,128)S(1)}, f32[40,128]{1,0:T(8,128)S(1)}, u32[]{:S(2)}, u32[]{:S(2)}) collective-permute-start(f32[40,128]{1,0:T(8,128)S(1)} %collective-permute-done.6.own_ye), channel_id=1, source_target_pairs={{0,1},{1,0},{2,3},{3,2},{4,5},{5,4},{6,7},{7,6},{8,9},{9,8},{10,11... | collective-permute-start | bytes 61448 | tf_op jit(solution)/shard_map/ppermute | solution.py:726
  22.9 1.9 %collective-permute-start.9 = (f32[40,128]{1,0:T(8,128)S(1)}, f32[40,128]{1,0:T(8,128)S(1)}, u32[]{:S(2)}, u32[]{:S(2)}) collective-permute-start(f32[40,128]{1,0:T(8,128)S(1)} %collective-permute-done.7.own_yo), channel_id=1, source_target_pairs={{0,1},{1,0},{2,3},{3,2},{4,5},{5,4},{6,7},{7,6},{8,9},{9,8},{10,11... | collective-permute-start | bytes 61448 | tf_op jit(solution)/shard_map/ppermute | solution.py:726
